TPU v7x, 32 devices: a whole 2x2x4 slice. The times are simulated.
32 devices in a mesh: dp: 4 (over z), seq: 8 (over y, x, core).
Axes of the slice: x: 2, y: 2, z: 4, core: 2. Of those that a mesh axis runs over, the one named last changes fastest.
Arguments:
- queries: bfloat16 [4, 1024, 2048], P('dp', 'seq'), may hold values from -6 to 6
- keys: bfloat16 [4, 1024, 2048], P('dp', 'seq'), may hold values from -6 to 6
- values: bfloat16 [4, 1024, 2048], P('dp', 'seq'), may hold values from -6 to 6
- residual_in: bfloat16 [4, 1024, 2048], P('dp', 'seq'), may hold values from -6 to 6
- cotangent: bfloat16 [4, 1024, 2048], P('dp', 'seq'), may hold values from -0.09375 to 0.09375
- expert_ids: int32 [4, 1024, 2], P('dp', 'seq'), may hold values from 0 to 7, all different within a row; in each aligned block of 128 rows (0 to 127, 128 to 255, ..., all dimensions but the last counted through in order) at most 48 rows name the same one
- router: bfloat16 [2048, 8], replicated, may hold values from -0.125 to 0.125
- attn_gain: float32 [2048], replicated, may hold values from 0.25 to 1.75
- moe_gain: float32 [2048], replicated, may hold values from 0.25 to 1.75
- w_gate: bfloat16 [8, 2048, 256], P('seq', 'dp'), may hold values from -0.125 to 0.125
- w_up: bfloat16 [8, 2048, 256], P('seq', 'dp'), may hold values from -0.125 to 0.125
- w_down: bfloat16 [8, 2048, 256], P('seq', 'dp'), may hold values from -0.375 to 0.375
- trainable: int32 [8], P('seq'), may hold values 0 or 1
Outputs:
- mixed: bfloat16 [4, 1024, 2048], P('dp', 'seq')
- grad_gate: float32 [8, 2048, 256], P('seq', 'dp')
- grad_up: float32 [8, 2048, 256], P('seq', 'dp')
- grad_down: float32 [8, 2048, 256], P('seq', 'dp')
Inputs may be any that keep to these rules, and one draw needn't show every extreme that they name: `expert_ids`: each position names two different experts; among the 128 positions of one index of seq no expert is named by more than 48 choices, a bound that some block reaches.
All inputs are finite; a program needn't handle non-finite values. No bound on the sum of `trainable` on one device may be relied on, other than what follows from the above.
Results may differ from a plain program's by a relative error of at most 0.025.
Values may be sent and summed in bfloat16 or wider, within the bound.
No kernel may reach another device: no remote copies, remote signals or barrier semaphores. Data moves between devices by JAX's collectives and lax.ppermute only.
A program may use at most 128 MiB of HBM per device.

v0:
```python
import jax
import jax.numpy as jnp
from jax import lax
from jax.sharding import PartitionSpec as P

HD = 128


def prefix_2(x, axis, combine, identity):
    peers, index = (lax.axis_size(axis), lax.axis_index(axis))
    everything = lax.all_gather(x.astype(jnp.bfloat16), axis)
    start = jnp.broadcast_to(jnp.asarray(identity, x.dtype), x.shape)

    def step(k, before):
        reached = k < index
        new = combine(before, everything[k].astype(x.dtype))
        return jnp.where(reached, new, before)

    return lax.fori_loop(0, peers, step, start)


def add_states(earlier, later):
    return earlier + later


def body(
    queries,
    keys,
    values,
    residual_in,
    cotangent,
    expert_ids,
    router,
    attn_gain,
    moe_gain,
    w_gate,
    w_up,
    w_down,
    trainable,
):
    tokens = queries.shape[1]
    width = queries.shape[2]
    heads = width // HD
    experts = router.shape[1]
    peers = lax.axis_size("seq")
    slots = max(2, 3 * tokens // peers)
    q_heads = queries[0].reshape(tokens, heads, HD)
    k_heads = keys[0].reshape(tokens, heads, HD)
    v_heads = values[0].reshape(tokens, heads, HD)
    local = jnp.einsum("thd,the->hde", k_heads, v_heads, preferred_element_type=jnp.float32)
    prefix = prefix_2(local, "seq", add_states, jnp.zeros_like(local))
    scores = jnp.einsum("thd,shd->hts", q_heads, k_heads, preferred_element_type=jnp.float32)
    causal = jnp.tril(jnp.ones((tokens, tokens), dtype=bool))
    weights = jnp.where(causal, scores, 0.0).astype(jnp.bfloat16)
    intra = jnp.einsum("hts,shd->thd", weights, v_heads, preferred_element_type=jnp.float32)
    carried = jnp.einsum(
        "thd,hde->the", q_heads.astype(jnp.float32), prefix, precision=lax.Precision.HIGHEST
    )
    attended = intra + carried
    attended = attended * lax.rsqrt(jnp.mean(attended * attended, axis=-1, keepdims=True) + 1e-06)
    stream = residual_in[0].astype(jnp.float32) + attended.reshape(tokens, width) * attn_gain
    normed = (
        stream * lax.rsqrt(jnp.mean(stream * stream, axis=-1, keepdims=True) + 1e-06) * moe_gain
    ).astype(jnp.bfloat16)
    choices_ids = expert_ids[0]
    logits = jnp.dot(normed, router, preferred_element_type=jnp.float32)
    onehot = (choices_ids[..., None] == jnp.arange(experts, dtype=jnp.int32)).astype(jnp.int32)
    chosen = jnp.sum(onehot.astype(jnp.float32) * logits[:, None, :], axis=-1)
    sig = jax.nn.sigmoid(chosen)
    gates = sig / jnp.sum(sig, axis=-1, keepdims=True)
    flat = onehot.reshape(2 * tokens, experts)
    before = jnp.cumsum(flat, axis=0) - flat
    rank = jnp.sum(before * flat, axis=-1)
    target = choices_ids.reshape(2 * tokens) * slots + rank
    placing = (target[:, None] == jnp.arange(experts * slots, dtype=jnp.int32)[None, :]).astype(
        jnp.bfloat16
    )
    contract = (((0,), (0,)), ((), ()))
    both_places = jnp.sum(placing.reshape(tokens, 2, experts * slots), axis=1)
    send_rows = (
        lax.dot_general(both_places, normed, contract, preferred_element_type=jnp.float32)
        .astype(jnp.bfloat16)
        .reshape(experts, slots, width)
    )
    expert_cot = (
        (cotangent[0].astype(jnp.float32)[:, None, :] * gates[:, :, None])
        .reshape(2 * tokens, width)
        .astype(jnp.bfloat16)
    )
    got_rows = lax.all_to_all(send_rows, "seq", split_axis=0, concat_axis=0, tiled=True)
    rows = got_rows.reshape(peers * slots, width)
    gate_full, up_full, down_full = (
        lax.all_gather(w_gate, "dp", axis=1, tiled=True),
        lax.all_gather(w_up, "dp", axis=1, tiled=True),
        lax.all_gather(w_down, "dp", axis=1, tiled=True),
    )
    pre_gate = jnp.dot(rows, gate_full[0], preferred_element_type=jnp.float32)
    pre_up = jnp.dot(rows, up_full[0], preferred_element_type=jnp.float32)
    down_mat = down_full[0]
    sigma = jax.nn.sigmoid(pre_gate)
    act = pre_gate * sigma
    hidden = (act * pre_up).astype(jnp.bfloat16)
    expert_out = lax.dot_general(
        hidden, down_mat, (((1,), (1,)), ((), ())), preferred_element_type=jnp.float32
    ).astype(jnp.bfloat16)
    back = lax.all_to_all(
        expert_out.reshape(peers, slots, width), "seq", split_axis=0, concat_axis=0, tiled=True
    )
    gathered = jnp.dot(
        placing, back.reshape(experts * slots, width), preferred_element_type=jnp.float32
    ).reshape(tokens, 2, width)
    mixed = (stream + jnp.sum(gates[:, :, None] * gathered, axis=1)).astype(jnp.bfloat16)
    cot_rows = lax.all_to_all(
        lax.dot_general(placing, expert_cot, contract, preferred_element_type=jnp.float32)
        .astype(jnp.bfloat16)
        .reshape(experts, slots, width),
        "seq",
        split_axis=0,
        concat_axis=0,
        tiled=True,
    ).reshape(peers * slots, width)
    flag = trainable[0] > 0
    d_hidden = jnp.dot(cot_rows, down_mat, preferred_element_type=jnp.float32)
    d_gate = (d_hidden * pre_up * sigma * (1.0 + pre_gate * (1.0 - sigma))).astype(jnp.bfloat16)
    d_up = (d_hidden * act).astype(jnp.bfloat16)
    term_gate = lax.dot_general(rows, d_gate, contract, preferred_element_type=jnp.float32)
    term_up = lax.dot_general(rows, d_up, contract, preferred_element_type=jnp.float32)
    term_down = lax.dot_general(cot_rows, hidden, contract, preferred_element_type=jnp.float32)
    summed = (
        lax.psum_scatter(
            term_gate[None].astype(jnp.bfloat16), "dp", scatter_dimension=1, tiled=True
        ).astype(jnp.float32),
        lax.psum_scatter(
            term_up[None].astype(jnp.bfloat16), "dp", scatter_dimension=1, tiled=True
        ).astype(jnp.float32),
        lax.psum_scatter(
            term_down[None].astype(jnp.bfloat16), "dp", scatter_dimension=1, tiled=True
        ).astype(jnp.float32),
    )
    scale = flag.astype(jnp.float32)
    return (mixed[None], summed[0] * scale, summed[1] * scale, summed[2] * scale)


def solution(mesh):
    return jax.shard_map(
        body,
        mesh=mesh,
        in_specs=(
            P("dp", "seq", None),
            P("dp", "seq", None),
            P("dp", "seq", None),
            P("dp", "seq", None),
            P("dp", "seq", None),
            P("dp", "seq", None),
            P(),
            P(),
            P(),
            P("seq", "dp", None),
            P("seq", "dp", None),
            P("seq", "dp", None),
            P("seq"),
        ),
        out_specs=(
            P("dp", "seq", None),
            P("seq", "dp", None),
            P("seq", "dp", None),
            P("seq", "dp", None),
        ),
        check_vma=False,
    )
```

profile of v0, /device:TPU:0, one launch (start us, length us, event | category | flops | bytes accessed | tf_op | source)
XLA Modules:
  0.0 231.2 jit_solution(12882464779213107808)
XLA Ops:
  14.2 36.1 %all-gather.12.cloned.1.call-done = bf16[128,128,128]{2,1,0:T(8,128)(2,1)} async-done(((bf16[16,128,128]{2,1,0:T(8,128)(2,1)}), bf16[128,128,128]{2,1,0:T(8,128)(2,1)}) %all-gather.12.cloned.1.call-update) | async-done | bytes 4194320 | tf_op jit(solution)/shard_map/all_gather | solution.py:11
  50.3 13.1 %while.14 = (s32[]{:T(128)}, f32[16,128,128]{2,1,0:T(8,128)S(1)}, s32[]{:T(128)}, bf16[8,16,128,128]{3,2,1,0:T(8,128)(2,1)}, s32[]{:T(128)}, /*index=5*/s32[]{:T(128)}) while((s32[]{:T(128)}, f32[16,128,128]{2,1,0:T(8,128)S(1)}, s32[]{:T(128)}, bf16[8,16,128,128]{3,2,1,0:T(8,128)(2,1)}, s32[]{:T(128)}, /*index=5*/s32[]{:T(128)}) %tuple.55), condition=%wide.region_1.2_spmd.clone, body=%wide.region_0.1_spmd.clone.sunk | while | flops 1048580 | bytes 2621533 | solution.py:19
  51.9 1.6 add_select_fusion.2
  53.6 1.6 add_select_fusion.2
  58.5 1.6 add_select_fusion.2
  63.4 2.0 convolution_bitcast_fusion.1
  65.4 1.9 multiply_reduce_fusion.1
  69.8 1.7 convolution_convert_fusion.2
  71.5 4.4 %all-to-all-start = ((bf16[8,48,2048]{2,1,0:T(8,128)(2,1)}), bf16[8,48,2048]{2,1,0:T(8,128)(2,1)}, u32[]{:S(2)}, u32[]{:S(2)}) async-start(bf16[8,48,2048]{2,1,0:T(8,128)(2,1)} %bitcast.10), calls=%async_computation | async-start | bytes 3145728 | tf_op jit(solution)/shard_map/all_to_all | solution.py:90
  76.1 2.5 %mul.157 = f32[128,2,2048]{2,1,0:T(2,128)} broadcast(f32[128,2048]{1,0:T(8,128)S(1)} %bitcast_convert_fusion), dimensions={0,2} | broadcast | bytes 3145728 | tf_op jit(solution)/shard_map/mul | solution.py:86
  78.7 2.7 %mul.158 = f32[256,2048]{1,0:T(8,128)S(1)} reshape(f32[128,2,2048]{2,1,0:T(2,128)} %mul.157) | data formatting | bytes 4194304 | tf_op jit(solution)/shard_map/mul | solution.py:86
  83.0 1.9 convolution_convert_fusion
  84.9 12.1 %all-to-all-done = bf16[8,48,2048]{2,1,0:T(8,128)(2,1)} async-done(((bf16[8,48,2048]{2,1,0:T(8,128)(2,1)}), bf16[8,48,2048]{2,1,0:T(8,128)(2,1)}, u32[]{:S(2)}, u32[]{:S(2)}) %all-to-all-start) | async-done | bytes 1572896 | tf_op jit(solution)/shard_map/all_to_all | solution.py:90
  97.0 3.6 %all-to-all-start.2 = ((bf16[8,48,2048]{2,1,0:T(8,128)(2,1)}), bf16[8,48,2048]{2,1,0:T(8,128)(2,1)S(1)}, u32[]{:S(2)}, u32[]{:S(2)}) async-start(bf16[8,48,2048]{2,1,0:T(8,128)(2,1)} %bitcast.93), calls=%async_computation.2 | async-start | bytes 3145728 | tf_op jit(solution)/shard_map/all_to_all | solution.py:113
  101.2 2.3 fusion.14
  103.5 5.4 %all-gather.8.cloned.1.call-done = bf16[1,2048,256]{2,1,0:T(8,128)(2,1)} async-done(((bf16[1,512,256]{2,1,0:T(8,128)(2,1)}), bf16[1,2048,256]{2,1,0:T(8,128)(2,1)}) %all-gather.8.cloned.1.call-update) | async-done | bytes 1048592 | tf_op jit(solution)/shard_map/all_gather | solution.py:94
  108.9 3.0 %multiply_convert_fusion.5 = (bf16[384,256]{1,0:T(8,128)(2,1)S(1)}, f32[384,256]{1,0:T(8,128)}) fusion(f32[384,256]{1,0:T(8,128)S(1)} %fusion.14, bf16[384,2048]{1,0:T(8,128)(2,1)} %bitcast.11, bf16[1,2048,256]{2,1,0:T(8,128)(2,1)} %all-gather.8.cloned.1.call-done), kind=kOutput, calls=%fused_computation.49 | convolution fusion | flops 403243008 | bytes 3604480 | tf_op jit(solution)/shard_map/dot_general | solution.py:98
  111.9 9.6 %all-to-all-done.2 = bf16[8,48,2048]{2,1,0:T(8,128)(2,1)S(1)} async-done(((bf16[8,48,2048]{2,1,0:T(8,128)(2,1)}), bf16[8,48,2048]{2,1,0:T(8,128)(2,1)S(1)}, u32[]{:S(2)}, u32[]{:S(2)}) %all-to-all-start.2) | async-done | bytes 1572896 | tf_op jit(solution)/shard_map/all_to_all | solution.py:113
  121.5 1.7 fusion.2
  123.3 14.4 %all-gather.10.cloned.1.call-done = bf16[1,2048,256]{2,1,0:T(8,128)(2,1)} async-done(((bf16[1,512,256]{2,1,0:T(8,128)(2,1)}), bf16[1,2048,256]{2,1,0:T(8,128)(2,1)}) %all-gather.10.cloned.1.call-update) | async-done | bytes 1048592 | tf_op jit(solution)/shard_map/all_gather | solution.py:95
  137.7 1.8 fusion.9
  140.2 3.2 %fusion.1 = bf16[1,2048,256]{2,1,0:T(8,128)(2,1)} fusion(bf16[384,2048]{1,0:T(8,128)(2,1)} %bitcast.11, f32[384,256]{1,0:T(8,128)S(1)} %fusion.9, f32[384,256]{1,0:T(8,128)S(1)} %fusion.14), kind=kOutput, calls=%fused_computation.9 | convolution fusion | flops 403767296 | bytes 3407872 | tf_op jit(solution)/shard_map/dot_general | solution.py:127
  144.7 1.8 convolution_convert_fusion.1
  146.4 4.4 %all-to-all-start.1 = ((bf16[8,48,2048]{2,1,0:T(8,128)(2,1)}), bf16[8,48,2048]{2,1,0:T(8,128)(2,1)}, u32[]{:S(2)}, u32[]{:S(2)}) async-start(bf16[8,48,2048]{2,1,0:T(8,128)(2,1)} %bitcast.15), calls=%async_computation.1 | async-start | bytes 3145728 | tf_op jit(solution)/shard_map/all_to_all | solution.py:106
  151.1 3.3 %fusion = bf16[1,2048,256]{2,1,0:T(8,128)(2,1)} fusion(bf16[384,2048]{1,0:T(8,128)(2,1)} %bitcast.11, f32[384,256]{1,0:T(8,128)S(1)} %fusion.14, f32[384,256]{1,0:T(8,128)S(1)} %copy-done.11, f32[384,256]{1,0:T(8,128)S(1)} %copy-done.12), kind=kOutput, calls=%fused_computation.8 | convolution fusion | flops 404160512 | bytes 3801088 | tf_op jit(solution)/shard_map/dot_general | solution.py:126
  155.4 16.5 %all-to-all-done.1 = bf16[8,48,2048]{2,1,0:T(8,128)(2,1)} async-done(((bf16[8,48,2048]{2,1,0:T(8,128)(2,1)}), bf16[8,48,2048]{2,1,0:T(8,128)(2,1)}, u32[]{:S(2)}, u32[]{:S(2)}) %all-to-all-start.1) | async-done | bytes 1572896 | tf_op jit(solution)/shard_map/all_to_all | solution.py:106
  171.9 2.4 %fusion.3 = f32[128,2048]{1,0:T(8,128)S(1)} fusion(bf16[384,2048,1]{1,0,2:T(8,128)(2,1)} %bitcast.17, f32[128,2]{0,1:T(2,128)S(1)} %multiply_divide_fusion, s32[128,2]{0,1:T(2,128)S(1)} %copy.68), kind=kOutput, calls=%fused_computation.12 | convolution fusion | flops 403537920 | bytes 2623488 | tf_op jit(solution)/shard_map/dot_general | solution.py:109
  175.3 1.8 convert_multiply_fusion
  177.1 17.4 %reduce-scatter.6.cloned.1.call-done = bf16[1,512,256]{2,1,0:T(8,128)(2,1)} async-done(((bf16[1,2048,256]{2,1,0:T(8,128)(2,1)}), bf16[1,512,256]{2,1,0:T(8,128)(2,1)}) %reduce-scatter.6.cloned.1.call-update) | async-done | bytes 262160 | tf_op jit(solution)/shard_map/reduce_scatter | solution.py:133
  194.5 1.8 convert_multiply_fusion.1
  196.3 26.3 %reduce-scatter.4.cloned.1.call-done = bf16[1,512,256]{2,1,0:T(8,128)(2,1)} async-done(((bf16[1,2048,256]{2,1,0:T(8,128)(2,1)}), bf16[1,512,256]{2,1,0:T(8,128)(2,1)}) %reduce-scatter.4.cloned.1.call-update) | async-done | bytes 262160 | tf_op jit(solution)/shard_map/reduce_scatter | solution.py:130
  222.6 1.8 convert_multiply_fusion.2
  (83 shorter events, 23.4 us)
Async XLA Ops:
  7.2 74.2 %copy-start = (bf16[2048,8]{0,1:T(8,128)(2,1)S(1)}, bf16[2048,8]{0,1:T(8,128)(2,1)}, u32[]{:S(2)}) copy-start(bf16[2048,8]{0,1:T(8,128)(2,1)} %param.21) | copy-start | bytes 98308
  7.2 43.1 %all-gather.12.cloned.1.call-start = ((), (), s32[]{:S(2)}) async-start(), calls=%async_computation.12 | async-start | bytes 4718592 | tf_op jit(solution)/shard_map/all_gather | solution.py:11
  9.7 2.7 %copy-start.9 = (s32[1,128,2]{1,2,0:T(2,128)S(1)}, s32[1,128,2]{1,2,0:T(2,128)}, u32[]{:S(2)}) copy-start(s32[1,128,2]{1,2,0:T(2,128)} %param.20) | copy-start | bytes 3076
  9.7 3.1 %copy-start.6 = (bf16[1,128,2048]{2,1,0:T(8,128)(2,1)S(1)}, bf16[1,128,2048]{2,1,0:T(8,128)(2,1)}, u32[]{:S(2)}) copy-start(bf16[1,128,2048]{2,1,0:T(8,128)(2,1)} %param.15) | copy-start | bytes 1572868
  10.8 90.3 %all-gather.6.cloned.1.call-start = ((), (), s32[]{:S(2)}) async-start(), calls=%async_computation.6 | async-start | bytes 1310720 | tf_op jit(solution)/shard_map/all_gather | solution.py:93
  11.6 97.3 %all-gather.8.cloned.1.call-start = ((), (), s32[]{:S(2)}) async-start(), calls=%async_computation.7 | async-start | bytes 1310720 | tf_op jit(solution)/shard_map/all_gather | solution.py:94
  67.4 1.0 copy-start.1
  67.4 1.0 copy-start.7
  67.4 1.3 copy-start.8
  69.0 0.8 copy-start.3
  71.5 4.5 %copy-start.5 = (bf16[1,128,2048]{2,1,0:T(8,128)(2,1)S(1)}, bf16[1,128,2048]{2,1,0:T(8,128)(2,1)}, u32[]{:S(2)}) copy-start(bf16[1,128,2048]{2,1,0:T(8,128)(2,1)} %param.19) | copy-start | bytes 1572868
  71.5 25.5 %all-to-all-start = ((bf16[8,48,2048]{2,1,0:T(8,128)(2,1)}), bf16[8,48,2048]{2,1,0:T(8,128)(2,1)}, u32[]{:S(2)}, u32[]{:S(2)}) async-start(bf16[8,48,2048]{2,1,0:T(8,128)(2,1)} %bitcast.10), calls=%async_computation | async-start | bytes 3145728 | tf_op jit(solution)/shard_map/all_to_all | solution.py:90
  97.0 24.5 %all-to-all-start.2 = ((bf16[8,48,2048]{2,1,0:T(8,128)(2,1)}), bf16[8,48,2048]{2,1,0:T(8,128)(2,1)S(1)}, u32[]{:S(2)}, u32[]{:S(2)}) async-start(bf16[8,48,2048]{2,1,0:T(8,128)(2,1)} %bitcast.93), calls=%async_computation.2 | async-start | bytes 3145728 | tf_op jit(solution)/shard_map/all_to_all | solution.py:113
  100.5 37.1 %all-gather.10.cloned.1.call-start = ((), (), s32[]{:S(2)}) async-start(), calls=%async_computation.8 | async-start | bytes 1310720 | tf_op jit(solution)/shard_map/all_gather | solution.py:95
  101.1 74.2 %reduce-scatter.8.cloned.1.call-start = ((), (), s32[]{:S(2)}) async-start(), calls=%async_computation.11 | async-start | bytes 1310720 | tf_op jit(solution)/shard_map/reduce_scatter | solution.py:136
  123.2 71.2 %reduce-scatter.6.cloned.1.call-start = ((), (), s32[]{:S(2)}) async-start(), calls=%async_computation.10 | async-start | bytes 1310720 | tf_op jit(solution)/shard_map/reduce_scatter | solution.py:133
  139.5 0.7 copy-start.10
  143.4 1.2 copy-start.4
  146.4 4.7 %copy-start.11 = (f32[384,256]{1,0:T(8,128)S(1)}, f32[384,256]{1,0:T(8,128)}, u32[]{:S(2)}) copy-start(f32[384,256]{1,0:T(8,128)} %copy-done.10) | copy-start | bytes 1179652
  146.4 4.7 %copy-start.12 = (f32[384,256]{1,0:T(8,128)S(1)}, f32[384,256]{1,0:T(8,128)}, u32[]{:S(2)}) copy-start(f32[384,256]{1,0:T(8,128)} %get-tuple-element.110) | copy-start | bytes 1179652
  146.4 25.4 %all-to-all-start.1 = ((bf16[8,48,2048]{2,1,0:T(8,128)(2,1)}), bf16[8,48,2048]{2,1,0:T(8,128)(2,1)}, u32[]{:S(2)}, u32[]{:S(2)}) async-start(bf16[8,48,2048]{2,1,0:T(8,128)(2,1)} %bitcast.15), calls=%async_computation.1 | async-start | bytes 3145728 | tf_op jit(solution)/shard_map/all_to_all | solution.py:106
  150.9 71.7 %reduce-scatter.4.cloned.1.call-start = ((), (), s32[]{:S(2)}) async-start(), calls=%async_computation.9 | async-start | bytes 1310720 | tf_op jit(solution)/shard_map/reduce_scatter | solution.py:130
  155.4 18.9 %copy-start.2 = (bf16[1,128,2048]{2,1,0:T(8,128)(2,1)S(1)}, bf16[1,128,2048]{2,1,0:T(8,128)(2,1)}, u32[]{:S(2)}) copy-start(bf16[1,128,2048]{2,1,0:T(8,128)(2,1)} %param.18) | copy-start | bytes 1572868
Sparse Core Ops, SparseCore 0:
  11.0 39.2 all-gather.11
  51.9 27.9 all-gather.5
  81.5 27.3 all-gather.7
  110.3 27.3 all-gather.9
  139.8 26.6 reduce-scatter.7
  168.7 25.7 reduce-scatter.5
  196.8 25.7 reduce-scatter.3
where the time goes:
time: 232 us; the launch traced here: 231 us
  waiting for transfers between devices  140 us (60%)
  matrix products  29.4 us (13%)
  other arithmetic  20.9 us (9%)
  between operations  15.1 us (7%)
  local copies, waits for them, and re-layouts  13.1 us (6%)
  starting transfers between devices  12.9 us (6%)
    all_gather x1, waiting for transfers between devices, prefix_2(): everything = lax.all_gather(x.astype(jnp.bfloat16), axis)  36.1 us
    reduce_scatter x1, waiting for transfers between devices, body(): lax.psum_scatter(term_gate[None].astype(jnp.bfloat16), 'dp', scatter_dime...  26.3 us
    reduce_scatter x1, waiting for transfers between devices, body(): lax.psum_scatter(term_up[None].astype(jnp.bfloat16), 'dp', scatter_dimens...  17.4 us
    all_to_all x1, waiting for transfers between devices, body(): lax.all_to_all(expert_out.reshape(peers, slots, width), 'seq', split_axis...  16.5 us
    all_gather x1, waiting for transfers between devices, body(): lax.all_gather(w_down, 'dp', axis=1, tiled=True)  14.4 us
    select_n x8, other arithmetic, step(): return jnp.where(reached, new, before)  12.9 us
    all_to_all x1, waiting for transfers between devices, body(): lax.all_to_all(send_rows, 'seq', split_axis=0, concat_axis=0, tiled=True)  12.1 us
    all_to_all x1, waiting for transfers between devices, body(): lax.all_to_all(lax.dot_general(placing, expert_cot, contract, preferred_e...  9.6 us
  transfers between devices with their start and end apart: 10, of which 8 were waited for; matrix products, arithmetic and copies ran while one was open for 24% of the time, Pallas kernels for 0%

commit v1 on v0

v1 whole, which is shorter than its diff:
```python
import functools

import jax
import jax.numpy as jnp
from jax import lax
from jax.experimental import pallas as pl
from jax.experimental.pallas import tpu as pltpu
from jax.sharding import PartitionSpec as P


HD = 128
F32 = jnp.float32
BF16 = jnp.bfloat16
MATMUL = (((1,), (0,)), ((), ()))
ROWS = (((0,), (0,)), ((), ()))
LANES = (((1,), (1,)), ((), ()))


def dot(a, b, dims=MATMUL):
    return lax.dot_general(a, b, dims, preferred_element_type=F32)


def kernel_call(body, ins, outs, scratch=(), flops=1_000_000_000, **static):
    place = {"s": pltpu.SMEM, "v": pltpu.VMEM, "h": pltpu.HBM}

    def call(*operands):
        letters = ins + ins[-1] * (len(operands) - len(ins))
        operands = [
            pltpu.with_memory_space_constraint(y, pltpu.HBM) if x == "h" else y
            for x, y in zip(letters, operands)
        ]
        return pl.pallas_call(
            functools.partial(body, **static),
            in_specs=[pl.BlockSpec(memory_space=place[x]) for x in letters],
            out_specs=[pl.BlockSpec(memory_space=place[x]) for x, _, _ in outs],
            out_shape=[
                (pltpu.HBM if x == "h" else jax.ShapeDtypeStruct)(shape, kind)
                for x, shape, kind in outs
            ],
            scratch_shapes=list(scratch),
            cost_estimate=pl.CostEstimate(flops=flops, bytes_accessed=4_000_000, transcendentals=0),
            compiler_params=pltpu.CompilerParams(vmem_limit_bytes=48 * 1024 * 1024),
        )(*operands)

    return call


class Copies:
    def __init__(self, sems):
        self.sems, self.n = sems, 0

    def start(self, source, target):
        copy = pltpu.make_async_copy(source, target, self.sems.at[self.n])
        self.n += 1
        copy.start()
        return copy


def route_kernel(
    i_ref, me_ref, ids_ref, cot_hbm, put_ref, slot_ref, *refs, groups, slots
):
    sends, (cot_ref, buf, sems) = refs[:-3], refs[-3:]
    tokens, rows_n = put_ref.shape
    width = cot_ref.shape[1]
    part = width // groups
    copies = Copies(sems)
    loads = []
    for d in range(groups):
        source = pl.multiple_of((i_ref[0] ^ d) * part, HD)
        loads.append(
            copies.start(
                cot_hbm.at[0, :, pl.ds(source, part)], cot_ref.at[:, pl.ds(d * part, part)]
            )
        )
    id_0, id_1 = ids_ref[0, :, 0:1], ids_ref[0, :, 1:2]
    lanes = lax.broadcasted_iota(jnp.int32, (tokens, HD), 1)
    hit_0, hit_1 = lanes == id_0, lanes == id_1
    count = jnp.where(hit_0, 1.0, jnp.where(hit_1, 1.0, 0.0)).astype(BF16)
    row = lax.broadcasted_iota(jnp.int32, (tokens, tokens), 0)
    col = lax.broadcasted_iota(jnp.int32, (tokens, tokens), 1)
    before = dot(jnp.where(row > col, 1.0, 0.0).astype(BF16), count)
    rank_0 = jnp.sum(jnp.where(hit_0, before, 0.0), axis=1, keepdims=True).astype(jnp.int32)
    rank_1 = jnp.sum(jnp.where(hit_1, before, 0.0), axis=1, keepdims=True).astype(jnp.int32)
    slot_0, slot_1 = id_0 * slots + rank_0, id_1 * slots + rank_1
    slot_ref[:, 0:1] = slot_0
    slot_ref[:, 1:2] = slot_1
    wide = lax.broadcasted_iota(jnp.int32, (tokens, rows_n), 1)
    put = jnp.where(wide == slot_0, 1.0, jnp.where(wide == slot_1, 1.0, 0.0)).astype(BF16)
    put_ref[...] = put
    both = jnp.broadcast_to((id_0 + id_1).astype(F32), (tokens, HD)).astype(BF16)
    buf[:, pl.ds(width, HD)] = dot(put, both, ROWS).astype(BF16)
    for d in range(groups):
        at = pl.ds(d * part, part)
        loads[d].wait()
        buf[:, at] = dot(put, cot_ref[:, at], ROWS).astype(BF16)
    if len(sends) == 1:
        stores = [copies.start(buf, sends[0])]
    else:
        stores = [
            copies.start(buf.at[pl.ds(pl.multiple_of((me_ref[0] ^ k) * slots, 16), slots)], send)
            for k, send in enumerate(sends)
        ]
    for copy in stores:
        copy.wait()


def load_rows(copies, me, pieces, target, slots):
    if len(pieces) == 1:
        return [copies.start(pieces[0], target)]
    return [
        copies.start(piece, target.at[pl.ds(pl.multiple_of((me ^ k) * slots, 16), slots)])
        for k, piece in enumerate(pieces)
    ]


def state_kernel(k_hbm, v_hbm, out_ref, k_ref, v_ref, sems, *, heads, chunks):
    copies = Copies(sems)
    size = heads // chunks
    loads = []
    for c in range(chunks):
        at = pl.ds(c * size * HD, size * HD)
        loads.append(
            [
                copies.start(k_hbm.at[0, :, at], k_ref.at[:, at]),
                copies.start(v_hbm.at[0, :, at], v_ref.at[:, at]),
            ]
        )
    for h in range(heads):
        if h % size == 0:
            for copy in loads[h // size]:
                copy.wait()
        at = pl.ds(h * HD, HD)
        out_ref[h] = dot(k_ref[:, at], v_ref[:, at], ROWS).astype(BF16)


def intra_kernel(q_ref, k_ref, v_ref, out_ref, *, heads):
    tokens = q_ref.shape[1]
    row = lax.broadcasted_iota(jnp.int32, (tokens, tokens), 0)
    col = lax.broadcasted_iota(jnp.int32, (tokens, tokens), 1)
    causal = row >= col
    for h in range(heads):
        at = pl.ds(h * HD, HD)
        scores = dot(q_ref[0, :, at], k_ref[0, :, at], LANES)
        scores = jnp.where(causal, scores, 0.0).astype(BF16)
        out_ref[:, at] = dot(scores, v_ref[0, :, at])


def norm_kernel(
    i_ref, q_ref, prefix_ref, intra_ref, residual_ref, attn_ref, moe_ref, put_ref,
    stream_out, normed_out, send_out, stream_ref, normed_ref, send_ref, sems, *, heads, groups,
):
    tokens, width = stream_ref.shape
    copies, started = Copies(sems), []
    squares = jnp.zeros((tokens, HD), F32)
    for h in range(heads):
        at = pl.ds(h * HD, HD)
        attended = intra_ref[:, at] + dot(q_ref[0, :, at], prefix_ref[h])
        mean = jnp.mean(attended * attended, axis=-1, keepdims=True)
        attended = attended * lax.rsqrt(mean + 1e-06)
        stream = residual_ref[0, :, at].astype(F32) + attended * attn_ref[:, at]
        stream_ref[:, at] = stream
        squares = squares + stream * stream
    scale = lax.rsqrt(jnp.sum(squares, axis=-1, keepdims=True) / width + 1e-06)
    part = width // groups
    for h in range(heads):
        at = pl.ds(h * HD, HD)
        normed_ref[:, at] = (stream_ref[:, at] * scale * moe_ref[:, at]).astype(BF16)
    put = put_ref[...]
    for d in range(groups):
        at = pl.ds(d * part, part)
        source = pl.multiple_of((i_ref[0] ^ d) * part, HD)
        send_ref[:, at] = dot(put, normed_ref[:, pl.ds(source, part)], ROWS).astype(BF16)
        started.append(copies.start(send_ref.at[:, at], send_out.at[:, at]))
    started.append(copies.start(normed_ref, normed_out))
    started.append(copies.start(stream_ref, stream_out))
    for copy in started:
        copy.wait()


def expert_kernel(me_ref, router_ref, rows_hbm, *refs, groups, gathered, pieces, slots):
    own, got, cots = refs[:3], refs[3 : 3 + gathered], refs[3 + gathered : 3 + gathered + pieces]
    hidden_ref, gated_ref, delta_ref, term_ref = refs[3 + gathered + pieces : -4]
    rows_ref, cot_ref, w_ref, sems = refs[-4:]
    rows_n, width = rows_ref.shape
    part = width // groups
    ff = hidden_ref.shape[1]
    copies = Copies(sems)
    loads = []
    for d in range(groups):
        at = pl.ds(d * part, part)
        load = [copies.start(rows_hbm.at[:, at], rows_ref.at[:, at])]
        if d == 0:
            for n in range(3):
                load.append(copies.start(own[n].at[0], w_ref.at[0, :, pl.ds(n * ff, ff)]))
        else:
            load.append(copies.start(got[d - 1], w_ref.at[d]))
            if d == groups - 1 and gathered == groups:
                load.append(copies.start(got[d], w_ref.at[d + 1]))
        loads.append(load)
    cot_loads = load_rows(copies, me_ref[0], cots, cot_ref, slots)
    cuts = [pl.ds(n * ff, ff) for n in range(3)]
    pre_gate, pre_up, d_hidden = (jnp.zeros((rows_n, ff), F32) for _ in range(3))
    logits = jnp.zeros((rows_n, router_ref.shape[0]), F32)
    for d in range(groups):
        at = pl.ds(d * part, part)
        for copy in loads[d]:
            copy.wait()
        if d == groups - 1 and gathered == groups:
            w_ref[d] = w_ref[d] + w_ref[d + 1]
        block = rows_ref[:, at]
        pre_gate = pre_gate + dot(block, w_ref[d, :, cuts[0]])
        pre_up = pre_up + dot(block, w_ref[d, :, cuts[1]])
        logits = logits + dot(block, router_ref[:, at], LANES)
    for copy in cot_loads:
        copy.wait()
    for d in range(groups):
        d_hidden = d_hidden + dot(cot_ref[:, pl.ds(d * part, part)], w_ref[d, :, cuts[2]])
    lanes = lax.broadcasted_iota(jnp.int32, logits.shape, 1)
    me = me_ref[0]
    other = cot_ref[:, pl.ds(width, HD)].astype(F32).astype(jnp.int32)[:, : logits.shape[1]] - me
    sig = 1.0 / (1.0 + jnp.exp(-logits))
    own_sig = jnp.sum(jnp.where(lanes == me, sig, 0.0), axis=1, keepdims=True)
    other_sig = jnp.sum(jnp.where(lanes == other, sig, 0.0), axis=1, keepdims=True)
    gate = own_sig / (own_sig + other_sig)
    d_hidden = d_hidden * gate
    sigma = 1.0 / (1.0 + jnp.exp(-pre_gate))
    act = pre_gate * sigma
    hidden = act * pre_up
    hidden_ref[...] = hidden.astype(BF16)
    gated_ref[...] = (hidden * gate).astype(BF16)
    delta_ref[:, :ff] = (d_hidden * pre_up * sigma * (1.0 + pre_gate * (1.0 - sigma))).astype(BF16)
    delta_ref[:, ff:] = (d_hidden * act).astype(BF16)
    term(rows_ref, cot_ref, delta_ref, gated_ref, term_ref, (groups - 1) * part)


def term(rows_ref, cot_ref, delta_ref, gated_ref, out_ref, start):
    part = out_ref.shape[0]
    ff = gated_ref.shape[1]
    at = pl.ds(start, part)
    out_ref[:, : 2 * ff] = dot(rows_ref[:, at], delta_ref[...], ROWS).astype(BF16)
    out_ref[:, 2 * ff :] = dot(cot_ref[:, at], gated_ref[...], ROWS).astype(BF16)


def output_kernel(
    me_ref, hidden_ref, gated_ref, delta_ref, rows_hbm, *refs, groups, gathered, pieces, slots
):
    own, got, cots = refs[:1], refs[1 : 1 + gathered], refs[1 + gathered : 1 + gathered + pieces]
    out_hbm, near_hbm, *terms = refs[1 + gathered + pieces : -6]
    rows_ref, cot_ref, w_ref, out_ref, near_ref, sems = refs[-6:]
    _, width = rows_ref.shape
    part = width // groups
    ff = hidden_ref.shape[1]
    copies = Copies(sems)
    row_load = copies.start(rows_hbm, rows_ref)
    cot_loads = load_rows(copies, me_ref[0], cots, cot_ref, slots)
    loads = [[copies.start(own[0].at[0], w_ref.at[0])]]
    for d in range(1, groups):
        at = pl.ds(2 * ff, ff)
        load = [copies.start(got[d - 1].at[:, at], w_ref.at[d])]
        if d == groups - 1 and gathered == groups:
            load.append(copies.start(got[d].at[:, at], w_ref.at[d + 1]))
        loads.append(load)
    row_load.wait()
    for copy in cot_loads:
        copy.wait()
    term(rows_ref, cot_ref, delta_ref, gated_ref, near_ref, part)
    stores = [copies.start(near_ref, near_hbm)]
    for n, out in enumerate(terms):
        term(rows_ref, cot_ref, delta_ref, gated_ref, out, (0 if n == 0 else n + 1) * part)
    for d in range(groups):
        for copy in loads[d]:
            copy.wait()
        if d == groups - 1 and gathered == groups:
            w_ref[d] = w_ref[d] + w_ref[d + 1]
        at = pl.ds(d * part, part)
        out_ref[:, at] = dot(hidden_ref[...], w_ref[d], LANES).astype(BF16)
        stores.append(copies.start(out_ref.at[:, at], out_hbm.at[:, at]))
    for copy in stores:
        copy.wait()


def combine_kernel(
    i_ref, stream_ref, normed_ref, router_ref, ids_ref, slot_ref, back_ref, out_ref, *, groups
):
    tokens, width = stream_ref.shape
    rows_n = back_ref.shape[0]
    logits = dot(normed_ref[...], router_ref[...], LANES)
    sig = 1.0 / (1.0 + jnp.exp(-logits))
    lanes = lax.broadcasted_iota(jnp.int32, logits.shape, 1)
    sig_0, sig_1 = (
        jnp.sum(jnp.where(lanes == ids_ref[0, :, j : j + 1], sig, 0.0), axis=1, keepdims=True)
        for j in range(2)
    )
    total = sig_0 + sig_1
    wide = lax.broadcasted_iota(jnp.int32, (tokens, rows_n), 1)
    take = jnp.where(
        wide == slot_ref[:, 0:1],
        sig_0 / total,
        jnp.where(wide == slot_ref[:, 1:2], sig_1 / total, 0.0),
    ).astype(BF16)
    part = width // groups
    for d in range(groups):
        at = pl.ds(pl.multiple_of((i_ref[0] ^ d) * part, HD), part)
        value = stream_ref[:, at] + dot(take, back_ref[:, pl.ds(d * part, part)])
        out_ref[0, :, at] = value.astype(BF16)


def total_kernel(scale_ref, *refs):
    parts, outs = refs[:-3], refs[-3:]
    ff = outs[0].shape[1]
    scale = jnp.where(scale_ref[0] > 0, 1.0, 0.0)
    for n, out in enumerate(outs):
        at = pl.ds(n * ff, ff)
        value = parts[0][:, at].astype(F32)
        for other in parts[1:]:
            value = value + other[:, at].astype(F32)
        out[...] = value * scale


def exclusive_prefix(local, axis):
    n, i = lax.axis_size(axis), lax.axis_index(axis)
    half = local.shape[0] // 2
    core = i % 2
    mine = lax.dynamic_slice_in_dim(local, core * half, half, 0)
    other = lax.dynamic_slice_in_dim(local, (1 - core) * half, half, 0)
    swap = [(j, j ^ 1) for j in range(n)]
    peer = lax.ppermute(other, axis, swap).astype(F32)
    mine = mine.astype(F32)
    total = (mine + peer).astype(BF16)
    before = jnp.zeros_like(mine)
    far = [lax.ppermute(total, axis, [(j, j + d) for j in range(n - d)]) for d in range(2, n, 2)]
    for got in far:
        before = before + got.astype(F32)
    own = before + jnp.where(core == 1, peer, 0.0)
    theirs = before + jnp.where(core == 0, mine, 0.0)
    back = lax.ppermute(theirs.astype(BF16), axis, swap)
    own = own.astype(BF16)
    return jnp.where(core == 0, jnp.concatenate([own, back], 0), jnp.concatenate([back, own], 0))


def send_xor(x, axis, d):
    return lax.ppermute(x, axis, [(j, j ^ d) for j in range(lax.axis_size(axis))])


ENDS = [(0, 1), (3, 2)]
MIDDLE = [(1, 2), (2, 1)]


def gather_xor(x, axis):
    n = lax.axis_size(axis)
    if n != 4:
        return [send_xor(x, axis, d) for d in range(1, n)]
    near, across = send_xor(x, axis, 1), send_xor(x, axis, 2)
    relayed = lax.ppermute(across, axis, [(b, a) for a, b in ENDS])
    middle = lax.ppermute(x, axis, MIDDLE)
    return [near, across, relayed, middle]


def scatter_xor(parts, axis):
    n = lax.axis_size(axis)
    if n != 4:
        return [parts[0]] + [send_xor(parts[d], axis, d) for d in range(1, n)]
    relayed = lax.ppermute(parts[3], axis, ENDS)
    middle = lax.ppermute(parts[3], axis, MIDDLE)
    merged = (parts[2].astype(F32) + relayed.astype(F32)).astype(BF16)
    across = send_xor(merged, axis, 2)
    near = send_xor(parts[1], axis, 1)
    return [parts[0], middle, across, near]


def exchange(x):
    return lax.all_to_all(x, "seq", split_axis=0, concat_axis=0, tiled=True)


def exchange_pieces(blocks):
    return [blocks[0]] + [
        send_xor(blocks[k], "seq", k) for k in range(len(blocks) - 1, 0, -1)
    ][::-1]


def swap_blocks(x, axis, dim):
    n, i = lax.axis_size(axis), lax.axis_index(axis)
    size = x.shape[dim] // n
    return jnp.concatenate(
        [lax.dynamic_slice_in_dim(x, (i ^ d) * size, size, dim) for d in range(n)], axis=dim
    )


def layer(
    queries,
    keys,
    values,
    residual_in,
    cotangent,
    expert_ids,
    router,
    attn_gain,
    moe_gain,
    w_gate,
    w_up,
    w_down,
    trainable,
):
    tokens = queries.shape[1]
    width = queries.shape[2]
    heads = width // HD
    experts = router.shape[1]
    peers = lax.axis_size("seq")
    groups = lax.axis_size("dp")
    slots = max(2, 3 * tokens // peers)
    rows_n = experts * slots
    part = width // groups
    ff = w_gate.shape[2]
    i = lax.axis_index("dp")[None]
    me = lax.axis_index("seq")[None]
    turned = swap_blocks(router.T, "dp", 1)

    split = slots % 16 == 0
    cot_shape = (slots if split else rows_n, width + HD)
    pieces = peers if split else 1
    put, slot, *cot_send = kernel_call(
        route_kernel,
        "ssvh",
        [("v", (tokens, rows_n), BF16), ("v", (tokens, 2), jnp.int32)]
        + [("h", cot_shape, BF16)] * pieces,
        [
            pltpu.VMEM((tokens, width), BF16),
            pltpu.VMEM((rows_n, width + HD), BF16),
            pltpu.SemaphoreType.DMA((groups + pieces,)),
        ],
        groups=groups,
        slots=slots,
    )(i, me, expert_ids, cotangent)
    if split:
        cots = exchange_pieces(cot_send)
    else:
        cots = [exchange(cot_send[0].reshape(experts, slots, -1)).reshape(cot_shape)]

    got = gather_xor(jnp.concatenate([w_gate[0], w_up[0], w_down[0]], axis=1), "dp")
    own = [w_gate, w_up, w_down]

    (local,) = kernel_call(
        state_kernel,
        "h",
        [("v", (heads, HD, HD), BF16)],
        [
            pltpu.VMEM((tokens, width), BF16),
            pltpu.VMEM((tokens, width), BF16),
            pltpu.SemaphoreType.DMA((8,)),
        ],
        heads=heads,
        chunks=4,
    )(keys, values)
    prefix = exclusive_prefix(local, "seq")

    (intra,) = kernel_call(
        intra_kernel, "v", [("v", (tokens, width), F32)], heads=heads
    )(queries, keys, values)
    stream, normed, send_rows = kernel_call(
        norm_kernel,
        "sv",
        [
            ("h", (tokens, width), F32),
            ("h", (tokens, width), BF16),
            ("h", (rows_n, width), BF16),
        ],
        [
            pltpu.VMEM((tokens, width), F32),
            pltpu.VMEM((tokens, width), BF16),
            pltpu.VMEM((rows_n, width), BF16),
            pltpu.SemaphoreType.DMA((groups + 2,)),
        ],
        heads=heads,
        groups=groups,
    )(i, queries, prefix, intra, residual_in, attn_gain[None], moe_gain[None], put)
    rows = exchange(send_rows.reshape(experts, slots, width)).reshape(rows_n, width)

    hidden, gated, delta, far_term = kernel_call(
        expert_kernel,
        "svh",
        [
            ("v", (rows_n, ff), BF16),
            ("v", (rows_n, ff), BF16),
            ("v", (rows_n, 2 * ff), BF16),
            ("v", (part, 3 * ff), BF16),
        ],
        [
            pltpu.VMEM((rows_n, width), BF16),
            pltpu.VMEM((rows_n, width + HD), BF16),
            pltpu.VMEM((len(got) + 1, part, 3 * ff), BF16),
            pltpu.SemaphoreType.DMA((groups + len(got) + 3 + pieces,)),
        ],
        groups=groups,
        gathered=len(got),
        pieces=pieces,
        slots=slots,
    )(me, turned, rows, *own, *got, *cots)
    expert_out, near_term, *terms = kernel_call(
        output_kernel,
        "svvvh",
        [("h", (rows_n, width), BF16), ("h", (part, 3 * ff), BF16)]
        + [("v", (part, 3 * ff), BF16)] * (groups - 2),
        [
            pltpu.VMEM((rows_n, width), BF16),
            pltpu.VMEM((rows_n, width + HD), BF16),
            pltpu.VMEM((len(got) + 1, part, ff), BF16),
            pltpu.VMEM((rows_n, width), BF16),
            pltpu.VMEM((part, 3 * ff), BF16),
            pltpu.SemaphoreType.DMA((groups + len(got) + 3 + pieces,)),
        ],
        groups=groups,
        gathered=len(got),
        pieces=pieces,
        slots=slots,
    )(me, hidden, gated, delta, rows, w_down, *got, *cots)
    terms = [terms[0], near_term, *terms[1:]]
    grads = kernel_call(total_kernel, "sv", [("v", (part, ff), F32)] * 3)(
        trainable, *scatter_xor(terms + [far_term], "dp")
    )

    back = exchange(expert_out.reshape(peers, slots, width)).reshape(rows_n, width)
    (mixed,) = kernel_call(
        combine_kernel, "sv", [("v", (1, tokens, width), BF16)], groups=groups
    )(i, stream, normed, router.T, expert_ids, slot, back)
    return (mixed, grads[0][None], grads[1][None], grads[2][None])


def solution(mesh):
    return jax.shard_map(
        layer,
        mesh=mesh,
        in_specs=(
            P("dp", "seq", None),
            P("dp", "seq", None),
            P("dp", "seq", None),
            P("dp", "seq", None),
            P("dp", "seq", None),
            P("dp", "seq", None),
            P(),
            P(),
            P(),
            P("seq", "dp", None),
            P("seq", "dp", None),
            P("seq", "dp", None),
            P("seq"),
        ),
        out_specs=(
            P("dp", "seq", None),
            P("seq", "dp", None),
            P("seq", "dp", None),
            P("seq", "dp", None),
        ),
        check_vma=False,
    )
```

time: 232 us -> 182 us (0.78)
  waiting for transfers between devices: 140 us -> 89.2 us
  starting transfers between devices: 12.9 us -> 51.9 us
  matrix products: 29.4 us -> 0 us
  Pallas kernels: 0 us -> 27.2 us
  other arithmetic: 20.9 us -> 5.39 us
  between operations: 15.1 us -> 1.59 us
  local copies, waits for them, and re-layouts: 13.1 us -> 5.62 us
    ppermute x0 -> x20, waiting for transfers between devices: none -> 85.3 us  [the longest x11 74.6 us: send_xor(): lax.ppermute(x, axis, [(j, j ^ d) for j in range(lax.axis_size(axis))])]
    all_gather x4 -> x0, waiting for transfers between devices: 55.8 us -> none  [the longest x1 36.1 us: prefix_2(): everything = lax.all_gather(x.astype(jnp.bfloat16), axis)]
    ppermute x0 -> x20, starting transfers between devices: none -> 44.4 us  [the longest x11 22.9 us: send_xor(): lax.ppermute(x, axis, [(j, j ^ d) for j in range(lax.axis_size(axis))])]
    reduce_scatter x3 -> x0, waiting for transfers between devices: 43.7 us -> none  [the longest x1 26.3 us: body(): lax.psum_scatter(term_gate[None].astype(jnp.bfloat16), 'dp', scatter_dime...]
    all_to_all x3 -> x2, waiting for transfers between devices: 38.1 us -> 3.96 us  [exchange(): return lax.all_to_all(x, 'seq', split_axis=0, concat_axis=0, tiled=True)]
    dot_general x14 -> x0, matrix products: 29.4 us -> none  [the longest x1 3.26 us: body(): lax.dot_general(rows, d_gate, contract, preferred_element_type=jnp.float32)]
    pallas_call x0 -> x8, Pallas kernels: none -> 27.2 us  [call(): pl.pallas_call(functools.partial(body, **static), in_specs=[pl.BlockSpec(...]
    select_n x8 -> x1, other arithmetic: 12.9 us -> 0.08 us  [exclusive_prefix(): jnp.where(core == 0, jnp.concatenate([own, back], 0), jnp.concatenate([ba...]
  transfers between devices with their start and end apart: 10 -> 22, of which waited for: 8 -> 13; matrix products, arithmetic and copies ran while one was open for 24% -> 2% of each run, Pallas kernels for 0% -> 9%
where the time goes in v1:
time: 182 us; the launch traced here: 181 us
  waiting for transfers between devices  89.2 us (49%)
  starting transfers between devices  51.9 us (29%)
  Pallas kernels  27.2 us (15%)
  local copies, waits for them, and re-layouts  5.62 us (3%)
  other arithmetic  5.39 us (3%)
    ppermute x11, waiting for transfers between devices, send_xor(): lax.ppermute(x, axis, [(j, j ^ d) for j in range(lax.axis_size(axis))])  74.6 us
    pallas_call x8, Pallas kernels, call(): pl.pallas_call(functools.partial(body, **static), in_specs=[pl.BlockSpec(...  27.2 us
    ppermute x11, starting transfers between devices, send_xor(): lax.ppermute(x, axis, [(j, j ^ d) for j in range(lax.axis_size(axis))])  22.9 us
    ppermute x3, starting transfers between devices, exclusive_prefix(): lax.ppermute(total, axis, [(j, j + d) for j in range(n - d)])  10.9 us
    ppermute x3, waiting for transfers between devices, exclusive_prefix(): lax.ppermute(total, axis, [(j, j + d) for j in range(n - d)])  8.29 us
    all_to_all x2, starting transfers between devices, exchange(): return lax.all_to_all(x, 'seq', split_axis=0, concat_axis=0, tiled=True)  7.46 us
    ppermute x1, starting transfers between devices, scatter_xor(): relayed = lax.ppermute(parts[3], axis, ENDS)  6.47 us
    unnamed x47, local copies, waits for them, and re-layouts  5.59 us
  transfers between devices with their start and end apart: 22, of which 13 were waited for; matrix products, arithmetic and copies ran while one was open for 2% of the time, Pallas kernels for 9%

profile of v1, /device:TPU:0, one launch (start us, length us, event | category | flops | bytes accessed | tf_op | source)
XLA Modules:
  0.0 180.9 jit_solution(11911626345435481896)
XLA Ops:
  0.6 1.9 %shard_map.156 = bf16[16,128,128]{2,1,0:T(8,128)(2,1)S(1)} custom-call(bf16[1,128,2048]{2,1,0:T(8,128)(2,1)} %k_ref.1, bf16[1,128,2048]{2,1,0:T(8,128)(2,1)} %v_ref.1), custom_call_target="tpu_custom_call" | custom-call | flops 1000000000 | bytes 4000000 | tf_op jit(solution)/shard_map/pallas_call | solution.py:32
  4.4 6.4 %collective-permute-start.3 = (bf16[8,128,128]{2,1,0:T(8,128)(2,1)S(1)}, bf16[8,128,128]{2,1,0:T(8,128)(2,1)}, u32[]{:S(2)}, u32[]{:S(2)}) collective-permute-start(bf16[8,128,128]{2,1,0:T(8,128)(2,1)S(1)} %fusion.2), channel_id=1, source_target_pairs={{0,6},{1,7},{8,14},{9,15},{16,22},{17,23},{24,30},{25,31}} | collective-permute-start | bytes 786440 | tf_op jit(solution)/shard_map/ppermute | solution.py:331
  10.9 2.0 %collective-permute-start.2 = (bf16[8,128,128]{2,1,0:T(8,128)(2,1)S(1)}, bf16[8,128,128]{2,1,0:T(8,128)(2,1)}, u32[]{:S(2)}, u32[]{:S(2)}) collective-permute-start(bf16[8,128,128]{2,1,0:T(8,128)(2,1)S(1)} %fusion.2), channel_id=1, source_target_pairs={{0,4},{1,5},{2,6},{3,7},{8,12},{9,13},{10,14},{11,15},{16,20},{17,... | collective-permute-start | bytes 786440 | tf_op jit(solution)/shard_map/ppermute | solution.py:331
  12.8 2.5 %collective-permute-start.1 = (bf16[8,128,128]{2,1,0:T(8,128)(2,1)S(1)}, bf16[8,128,128]{2,1,0:T(8,128)(2,1)}, u32[]{:S(2)}, u32[]{:S(2)}) collective-permute-start(bf16[8,128,128]{2,1,0:T(8,128)(2,1)S(1)} %fusion.2), channel_id=1, source_target_pairs={{0,2},{1,3},{2,4},{3,5},{4,6},{5,7},{8,10},{9,11},{10,12},{11,13},... | collective-permute-start | bytes 786440 | tf_op jit(solution)/shard_map/ppermute | solution.py:331
  16.9 6.7 %collective-permute-done.2 = bf16[8,128,128]{2,1,0:T(8,128)(2,1)} collective-permute-done((bf16[8,128,128]{2,1,0:T(8,128)(2,1)S(1)}, bf16[8,128,128]{2,1,0:T(8,128)(2,1)}, u32[]{:S(2)}, u32[]{:S(2)}) %collective-permute-start.2) | collective-permute-done | bytes 262176 | tf_op jit(solution)/shard_map/ppermute | solution.py:331
  23.6 2.0 %fusion.4 = (bf16[8,128,128]{2,1,0:T(8,128)(2,1)S(1)}, bf16[8,128,128]{2,1,0:T(8,128)(2,1)}) fusion(bf16[8,128,128]{2,1,0:T(8,128)(2,1)S(1)} %collective-permute-done, bf16[8,128,128]{2,1,0:T(8,128)(2,1)} %collective-permute-done.3, bf16[8,128,128]{2,1,0:T(8,128)(2,1)} %collective-permute-done.2, bf16[8,128,128]{2,1,0:T(8,128)(2,1)} %collective-permute-done.1, ...), kind=kLoop, calls=%fused_computation.9 | loop fusion | flops 1703936 | bytes 1835014 | tf_op jit(solution)/shard_map/convert_element_type | solution.py:337
  26.6 2.6 %collective-permute-start.6 = (bf16[512,768]{1,0:T(8,128)(2,1)}, bf16[512,768]{1,0:T(8,128)(2,1)}, u32[]{:S(2)}, u32[]{:S(2)}) collective-permute-start(bf16[512,768]{1,0:T(8,128)(2,1)} %pad_maximum_fusion), channel_id=1, source_target_pairs={{0,16},{8,24},{16,0},{24,8},{1,17},{9,25},{17,1},{25,9},{2,18},{10... | collective-permute-start | bytes 2359304 | tf_op jit(solution)/shard_map/ppermute | solution.py:342
  29.3 2.6 %shard_map.157.intra_ref = f32[128,2048]{1,0:T(8,128)S(1)} custom-call(bf16[1,128,2048]{2,1,0:T(8,128)(2,1)S(1)} %copy-done.9, bf16[1,128,2048]{2,1,0:T(8,128)(2,1)S(1)} %copy-done.7, bf16[1,128,2048]{2,1,0:T(8,128)(2,1)S(1)} %copy-done.8), custom_call_target="tpu_custom_call" | custom-call | flops 1000000000 | bytes 4000000 | tf_op jit(solution)/shard_map/pallas_call | solution.py:32
  31.9 3.5 %shard_map.158 = (bf16[128,384]{1,0:T(8,128)(2,1)S(1)}, s32[128,2]{1,0:T(8,128)S(1)}, bf16[48,2176]{1,0:T(8,128)(2,1)}, bf16[48,2176]{1,0:T(8,128)(2,1)}, bf16[4...) custom-call(s32[1]{0:T(128)} %bitcast.i_ref, ...), custom_call_target="tpu_custom_call" | custom-call | flops 1000000000 | bytes 4000000 | tf_op jit(solution)/shard_map/pallas_call | solution.py:32
  36.2 2.7 %shard_map.159 = (f32[128,2048]{1,0:T(8,128)}, bf16[128,2048]{1,0:T(8,128)(2,1)}, bf16[384,2048]{1,0:T(8,128)(2,1)}) custom-call(s32[1]{0:T(128)} %bitcast.i_ref, bf16[1,128,2048]{2,1,0:T(8,128)(2,1)S(1)} %copy-done.9, bf16[16,128,128]{2,1,0:T(8,128)(2,1)S(1)} %maximum_select_fusion.prefix_ref, f32[128,2048]{1,0:T(8,128)S(1)} %shard_map.157.intra_ref, ...), custom_call_target="tpu_custom_call" | custom-call | flops 1000000000 | bytes 4000000 | tf_op jit(solution)/shard_map/pallas_call | solution.py:32
  39.0 3.9 %all-to-all-start = ((bf16[8,48,2048]{2,1,0:T(8,128)(2,1)}), bf16[8,48,2048]{2,1,0:T(8,128)(2,1)S(1)}, u32[]{:S(2)}, u32[]{:S(2)}) async-start(bf16[8,48,2048]{2,1,0:T(8,128)(2,1)} %bitcast.30), calls=%async_computation | async-start | bytes 3145728 | tf_op jit(solution)/shard_map/all_to_all | solution.py:372
  45.7 19.5 %collective-permute-done.6.refs_4_.refs_2_ = bf16[512,768]{1,0:T(8,128)(2,1)} collective-permute-done((bf16[512,768]{1,0:T(8,128)(2,1)}, bf16[512,768]{1,0:T(8,128)(2,1)}, u32[]{:S(2)}, u32[]{:S(2)}) %collective-permute-start.6) | collective-permute-done | bytes 786464 | tf_op jit(solution)/shard_map/ppermute | solution.py:342
  67.1 7.7 %collective-permute-done.10.refs_9_.refs_7_ = bf16[48,2176]{1,0:T(8,128)(2,1)} collective-permute-done((bf16[48,2176]{1,0:T(8,128)(2,1)}, bf16[48,2176]{1,0:T(8,128)(2,1)}, u32[]{:S(2)}, u32[]{:S(2)}) %collective-permute-start.10) | collective-permute-done | bytes 208928 | tf_op jit(solution)/shard_map/ppermute | solution.py:342
  74.8 2.6 %collective-permute-start.12 = (bf16[48,2176]{1,0:T(8,128)(2,1)}, bf16[48,2176]{1,0:T(8,128)(2,1)}, u32[]{:S(2)}, u32[]{:S(2)}) collective-permute-start(bf16[48,2176]{1,0:T(8,128)(2,1)} %get-tuple-element.37), channel_id=1, source_target_pairs={{0,4},{1,5},{2,6},{3,7},{4,0},{5,1},{6,2},{7,3},{8,12},{9,13},{10,... | collective-permute-start | bytes 626696 | tf_op jit(solution)/shard_map/ppermute | solution.py:342
  77.4 2.3 %collective-permute-start.13 = (bf16[48,2176]{1,0:T(8,128)(2,1)}, bf16[48,2176]{1,0:T(8,128)(2,1)}, u32[]{:S(2)}, u32[]{:S(2)}) collective-permute-start(bf16[48,2176]{1,0:T(8,128)(2,1)} %get-tuple-element.38), channel_id=1, source_target_pairs={{0,5},{1,4},{2,7},{3,6},{4,1},{5,0},{6,3},{7,2},{8,13},{9,12},{10,... | collective-permute-start | bytes 626696 | tf_op jit(solution)/shard_map/ppermute | solution.py:342
  79.7 5.5 %collective-permute-done.12.refs_11_.refs_9_ = bf16[48,2176]{1,0:T(8,128)(2,1)} collective-permute-done((bf16[48,2176]{1,0:T(8,128)(2,1)}, bf16[48,2176]{1,0:T(8,128)(2,1)}, u32[]{:S(2)}, u32[]{:S(2)}) %collective-permute-start.12) | collective-permute-done | bytes 208928 | tf_op jit(solution)/shard_map/ppermute | solution.py:342
  85.2 2.8 %collective-permute-done.13.refs_12_.refs_10_ = bf16[48,2176]{1,0:T(8,128)(2,1)} collective-permute-done((bf16[48,2176]{1,0:T(8,128)(2,1)}, bf16[48,2176]{1,0:T(8,128)(2,1)}, u32[]{:S(2)}, u32[]{:S(2)}) %collective-permute-start.13) | collective-permute-done | bytes 208928 | tf_op jit(solution)/shard_map/ppermute | solution.py:342
  89.4 2.8 %collective-permute-done.14.refs_13_.refs_11_ = bf16[48,2176]{1,0:T(8,128)(2,1)S(1)} collective-permute-done((bf16[48,2176]{1,0:T(8,128)(2,1)}, bf16[48,2176]{1,0:T(8,128)(2,1)S(1)}, u32[]{:S(2)}, u32[]{:S(2)}) %collective-permute-start.14) | collective-permute-done | bytes 208928 | tf_op jit(solution)/shard_map/ppermute | solution.py:342
  92.2 3.9 %collective-permute-done.15.refs_14_.refs_12_ = bf16[48,2176]{1,0:T(8,128)(2,1)S(1)} collective-permute-done((bf16[48,2176]{1,0:T(8,128)(2,1)}, bf16[48,2176]{1,0:T(8,128)(2,1)S(1)}, u32[]{:S(2)}, u32[]{:S(2)}) %collective-permute-start.15) | collective-permute-done | bytes 208928 | tf_op jit(solution)/shard_map/ppermute | solution.py:342
  98.2 6.2 %shard_map.160 = (bf16[384,256]{1,0:T(8,128)(2,1)S(1)}, bf16[384,256]{1,0:T(8,128)(2,1)S(1)}, bf16[384,512]{1,0:T(8,128)(2,1)S(1)}, bf16[512,768]{1,0:T(8,128)(2,1)}) custom-call(s32[1]{0:T(128)} %bitcast.3.me_ref, bf16[8,2048]{1,0:T(8,128)(2,1)S(1)} %pad_maximum_fusion.1.router_ref, bf16[384,2048]{1,0:T(8,128)(2,1)} %bitcast.27, ...), custom_call_target="tpu_custom_call" | custom-call | flops 1000000000 | bytes 4000000 | tf_op jit(solution)/shard_map/pallas_call | solution.py:32
  104.4 6.5 %collective-permute-start.17 = (bf16[512,768]{1,0:T(8,128)(2,1)}, bf16[512,768]{1,0:T(8,128)(2,1)}, u32[]{:S(2)}, u32[]{:S(2)}) collective-permute-start(bf16[512,768]{1,0:T(8,128)(2,1)} %get-tuple-element.46), channel_id=1, source_target_pairs={{0,8},{24,16},{1,9},{25,17},{2,10},{26,18},{3,11},{27,19},{4,12},{... | collective-permute-start | bytes 2359304 | tf_op jit(solution)/shard_map/ppermute | solution.py:363
  110.8 5.6 %shard_map.161 = (bf16[384,2048]{1,0:T(8,128)(2,1)}, bf16[512,768]{1,0:T(8,128)(2,1)}, bf16[512,768]{1,0:T(8,128)(2,1)S(1)}, bf16[512,768]{1,0:T(8,128)(2,1)S(1)}) custom-call(s32[1]{0:T(128)} %bitcast.3.me_ref, bf16[384,256]{1,0:T(8,128)(2,1)S(1)} %get-tuple-element.41.hidden_ref, bf16[384,256]{1,0:T(8,128)(2,1)S(1)} %get-tuple-element.42.gated_ref, ...), custom_call_target="tpu_custom_call" | custom-call | flops 1000000000 | bytes 4000000 | tf_op jit(solution)/shard_map/pallas_call | solution.py:32
  117.4 3.6 %all-to-all-start.1 = ((bf16[8,48,2048]{2,1,0:T(8,128)(2,1)}), bf16[8,48,2048]{2,1,0:T(8,128)(2,1)S(1)}, u32[]{:S(2)}, u32[]{:S(2)}) async-start(bf16[8,48,2048]{2,1,0:T(8,128)(2,1)} %bitcast.31), calls=%async_computation.1 | async-start | bytes 3145728 | tf_op jit(solution)/shard_map/all_to_all | solution.py:372
  121.0 1.7 collective-permute-start.16
  122.7 3.8 %collective-permute-start.19 = (bf16[512,768]{1,0:T(8,128)(2,1)}, bf16[512,768]{1,0:T(8,128)(2,1)}, u32[]{:S(2)}, u32[]{:S(2)}) collective-permute-start(bf16[512,768]{1,0:T(8,128)(2,1)} %get-tuple-element.48), channel_id=1, source_target_pairs={{0,8},{8,0},{16,24},{24,16},{1,9},{9,1},{17,25},{25,17},{2,10},{10... | collective-permute-start | bytes 2359304 | tf_op jit(solution)/shard_map/ppermute | solution.py:342
  127.7 2.3 %add_convert_fusion = bf16[512,768]{1,0:T(8,128)(2,1)} fusion(bf16[512,768]{1,0:T(8,128)(2,1)} %collective-permute-done.17, bf16[512,768]{1,0:T(8,128)(2,1)S(1)} %get-tuple-element.47), kind=kLoop, calls=%fused_computation | loop fusion | flops 1572864 | bytes 2359296 | tf_op jit(solution)/shard_map/convert_element_type | solution.py:365
  129.9 7.3 %collective-permute-start.18 = (bf16[512,768]{1,0:T(8,128)(2,1)}, bf16[512,768]{1,0:T(8,128)(2,1)}, u32[]{:S(2)}, u32[]{:S(2)}) collective-permute-start(bf16[512,768]{1,0:T(8,128)(2,1)} %add_convert_fusion), channel_id=1, source_target_pairs={{0,16},{8,24},{16,0},{24,8},{1,17},{9,25},{17,1},{25,9},{2,18},{10... | collective-permute-start | bytes 2359304 | tf_op jit(solution)/shard_map/ppermute | solution.py:342
  137.9 4.0 %all-to-all-done.1 = bf16[8,48,2048]{2,1,0:T(8,128)(2,1)S(1)} async-done(((bf16[8,48,2048]{2,1,0:T(8,128)(2,1)}), bf16[8,48,2048]{2,1,0:T(8,128)(2,1)S(1)}, u32[]{:S(2)}, u32[]{:S(2)}) %all-to-all-start.1) | async-done | bytes 1572896 | tf_op jit(solution)/shard_map/all_to_all | solution.py:372
  143.8 1.8 shard_map.162
  145.6 4.7 %collective-permute-done.19.refs_3_ = bf16[512,768]{1,0:T(8,128)(2,1)} collective-permute-done((bf16[512,768]{1,0:T(8,128)(2,1)}, bf16[512,768]{1,0:T(8,128)(2,1)}, u32[]{:S(2)}, u32[]{:S(2)}) %collective-permute-start.19) | collective-permute-done | bytes 786464 | tf_op jit(solution)/shard_map/ppermute | solution.py:342
  150.2 27.8 %collective-permute-done.18.refs_2_ = bf16[512,768]{1,0:T(8,128)(2,1)} collective-permute-done((bf16[512,768]{1,0:T(8,128)(2,1)}, bf16[512,768]{1,0:T(8,128)(2,1)}, u32[]{:S(2)}, u32[]{:S(2)}) %collective-permute-start.18) | collective-permute-done | bytes 786464 | tf_op jit(solution)/shard_map/ppermute | solution.py:342
  178.0 2.9 %shard_map.163 = (f32[512,256]{1,0:T(8,128)}, f32[512,256]{1,0:T(8,128)}, f32[512,256]{1,0:T(8,128)}) custom-call(s32[1]{0:T(128)S(6)} %copy.19.scale_ref, bf16[512,768]{1,0:T(8,128)(2,1)S(1)} %copy-done.6, bf16[512,768]{1,0:T(8,128)(2,1)} %collective-permute-done.16.refs_1_, bf16[512,768]{1,0:T(8,128)(2,1)} %collective-permute-done.18.refs_2_, ...), custom_call_target="tpu_custom_call" | custom-call | flops 1000000000 | bytes 4000000 | tf_op jit(solution)/shard_map/pallas_call | solution.py:32
  (75 shorter events, 17.4 us)
Async XLA Ops:
  2.6 23.1 %copy-start.16 = (bf16[1,512,256]{2,1,0:T(8,128)(2,1)S(1)}, bf16[1,512,256]{2,1,0:T(8,128)(2,1)}, u32[]{:S(2)}) copy-start(bf16[1,512,256]{2,1,0:T(8,128)(2,1)} %refs_0_.3) | copy-start | bytes 786436
  2.6 23.1 %copy-start.17 = (bf16[1,512,256]{2,1,0:T(8,128)(2,1)S(1)}, bf16[1,512,256]{2,1,0:T(8,128)(2,1)}, u32[]{:S(2)}) copy-start(bf16[1,512,256]{2,1,0:T(8,128)(2,1)} %refs_0_.2) | copy-start | bytes 786436
  2.6 23.1 %copy-start.18 = (bf16[1,512,256]{2,1,0:T(8,128)(2,1)S(1)}, bf16[1,512,256]{2,1,0:T(8,128)(2,1)}, u32[]{:S(2)}) copy-start(bf16[1,512,256]{2,1,0:T(8,128)(2,1)} %refs_1_.1) | copy-start | bytes 786436
  2.6 1.7 collective-permute-start
  4.4 12.4 %collective-permute-start.3 = (bf16[8,128,128]{2,1,0:T(8,128)(2,1)S(1)}, bf16[8,128,128]{2,1,0:T(8,128)(2,1)}, u32[]{:S(2)}, u32[]{:S(2)}) collective-permute-start(bf16[8,128,128]{2,1,0:T(8,128)(2,1)S(1)} %fusion.2), channel_id=1, source_target_pairs={{0,6},{1,7},{8,14},{9,15},{16,22},{17,23},{24,30},{25,31}} | collective-permute-start | bytes 786440 | tf_op jit(solution)/shard_map/ppermute | solution.py:331
  10.9 12.8 %collective-permute-start.2 = (bf16[8,128,128]{2,1,0:T(8,128)(2,1)S(1)}, bf16[8,128,128]{2,1,0:T(8,128)(2,1)}, u32[]{:S(2)}, u32[]{:S(2)}) collective-permute-start(bf16[8,128,128]{2,1,0:T(8,128)(2,1)S(1)} %fusion.2), channel_id=1, source_target_pairs={{0,4},{1,5},{2,6},{3,7},{8,12},{9,13},{10,14},{11,15},{16,20},{17,... | collective-permute-start | bytes 786440 | tf_op jit(solution)/shard_map/ppermute | solution.py:331
  12.8 10.8 %collective-permute-start.1 = (bf16[8,128,128]{2,1,0:T(8,128)(2,1)S(1)}, bf16[8,128,128]{2,1,0:T(8,128)(2,1)}, u32[]{:S(2)}, u32[]{:S(2)}) collective-permute-start(bf16[8,128,128]{2,1,0:T(8,128)(2,1)S(1)} %fusion.2), channel_id=1, source_target_pairs={{0,2},{1,3},{2,4},{3,5},{4,6},{5,7},{8,10},{9,11},{10,12},{11,13},... | collective-permute-start | bytes 786440 | tf_op jit(solution)/shard_map/ppermute | solution.py:331
  15.3 14.0 %copy-start.7 = (bf16[1,128,2048]{2,1,0:T(8,128)(2,1)S(1)}, bf16[1,128,2048]{2,1,0:T(8,128)(2,1)}, u32[]{:S(2)}) copy-start(bf16[1,128,2048]{2,1,0:T(8,128)(2,1)} %k_ref.1) | copy-start | bytes 1572868
  15.3 14.0 %copy-start.8 = (bf16[1,128,2048]{2,1,0:T(8,128)(2,1)S(1)}, bf16[1,128,2048]{2,1,0:T(8,128)(2,1)}, u32[]{:S(2)}) copy-start(bf16[1,128,2048]{2,1,0:T(8,128)(2,1)} %v_ref.1) | copy-start | bytes 1572868
  15.3 14.0 %copy-start.9 = (bf16[1,128,2048]{2,1,0:T(8,128)(2,1)S(1)}, bf16[1,128,2048]{2,1,0:T(8,128)(2,1)}, u32[]{:S(2)}) copy-start(bf16[1,128,2048]{2,1,0:T(8,128)(2,1)} %q_ref.3) | copy-start | bytes 1572868
  25.7 10.4 %collective-permute-start.4 = (bf16[8,128,128]{2,1,0:T(8,128)(2,1)}, bf16[8,128,128]{2,1,0:T(8,128)(2,1)S(1)}, u32[]{:S(2)}, u32[]{:S(2)}) collective-permute-start(bf16[8,128,128]{2,1,0:T(8,128)(2,1)} %get-tuple-element.53), channel_id=1, source_target_pairs={{0,1},{1,0},{2,3},{3,2},{4,5},{5,4},{6,7},{7,6},{8,9},{9,8},{10,11... | collective-permute-start | bytes 786440 | tf_op jit(solution)/shard_map/ppermute | solution.py:336
  26.6 38.5 %collective-permute-start.6 = (bf16[512,768]{1,0:T(8,128)(2,1)}, bf16[512,768]{1,0:T(8,128)(2,1)}, u32[]{:S(2)}, u32[]{:S(2)}) collective-permute-start(bf16[512,768]{1,0:T(8,128)(2,1)} %pad_maximum_fusion), channel_id=1, source_target_pairs={{0,16},{8,24},{16,0},{24,8},{1,17},{9,25},{17,1},{25,9},{2,18},{10... | collective-permute-start | bytes 2359304 | tf_op jit(solution)/shard_map/ppermute | solution.py:342
  39.0 40.8 %copy-start.2 = (bf16[2048,8]{0,1:T(8,128)(2,1)S(1)}, bf16[2048,8]{0,1:T(8,128)(2,1)}, u32[]{:S(2)}) copy-start(bf16[2048,8]{0,1:T(8,128)(2,1)} %param.19) | copy-start | bytes 98308
  39.0 57.9 %all-to-all-start = ((bf16[8,48,2048]{2,1,0:T(8,128)(2,1)}), bf16[8,48,2048]{2,1,0:T(8,128)(2,1)S(1)}, u32[]{:S(2)}, u32[]{:S(2)}) async-start(bf16[8,48,2048]{2,1,0:T(8,128)(2,1)} %bitcast.30), calls=%async_computation | async-start | bytes 3145728 | tf_op jit(solution)/shard_map/all_to_all | solution.py:372
  42.9 24.3 %collective-permute-start.9 = (bf16[48,2176]{1,0:T(8,128)(2,1)}, bf16[48,2176]{1,0:T(8,128)(2,1)S(1)}, u32[]{:S(2)}, u32[]{:S(2)}) collective-permute-start(bf16[48,2176]{1,0:T(8,128)(2,1)} %get-tuple-element.34), channel_id=1, source_target_pairs={{0,1},{1,0},{2,3},{3,2},{4,5},{5,4},{6,7},{7,6},{8,9},{9,8},{10,11... | collective-permute-start | bytes 626696 | tf_op jit(solution)/shard_map/ppermute | solution.py:342
  43.4 52.8 %collective-permute-start.5 = (bf16[512,768]{1,0:T(8,128)(2,1)}, bf16[512,768]{1,0:T(8,128)(2,1)S(1)}, u32[]{:S(2)}, u32[]{:S(2)}) collective-permute-start(bf16[512,768]{1,0:T(8,128)(2,1)} %pad_maximum_fusion), channel_id=1, source_target_pairs={{0,8},{8,0},{16,24},{24,16},{1,9},{9,1},{17,25},{25,17},{2,10},{10... | collective-permute-start | bytes 2359304 | tf_op jit(solution)/shard_map/ppermute | solution.py:342
  44.9 51.2 %collective-permute-start.8 = (bf16[512,768]{1,0:T(8,128)(2,1)}, bf16[512,768]{1,0:T(8,128)(2,1)S(1)}, u32[]{:S(2)}, u32[]{:S(2)}) collective-permute-start(bf16[512,768]{1,0:T(8,128)(2,1)} %pad_maximum_fusion), channel_id=1, source_target_pairs={{8,16},{16,8},{9,17},{17,9},{10,18},{18,10},{11,19},{19,11},{12,20... | collective-permute-start | bytes 2359304 | tf_op jit(solution)/shard_map/ppermute | solution.py:355
  65.1 31.7 %collective-permute-start.7 = (bf16[512,768]{1,0:T(8,128)(2,1)}, bf16[512,768]{1,0:T(8,128)(2,1)}, u32[]{:S(2)}, u32[]{:S(2)}) collective-permute-start(bf16[512,768]{1,0:T(8,128)(2,1)} %collective-permute-done.6.refs_4_.refs_2_), channel_id=1, source_target_pairs={{8,0},{16,24},{9,1},{17,25},{10,2},{18,26},{11,3},{19,27},{12,4},{... | collective-permute-start | bytes 2359304 | tf_op jit(solution)/shard_map/ppermute | solution.py:354
  66.4 8.4 %collective-permute-start.10 = (bf16[48,2176]{1,0:T(8,128)(2,1)}, bf16[48,2176]{1,0:T(8,128)(2,1)}, u32[]{:S(2)}, u32[]{:S(2)}) collective-permute-start(bf16[48,2176]{1,0:T(8,128)(2,1)} %get-tuple-element.35), channel_id=1, source_target_pairs={{0,2},{1,3},{2,0},{3,1},{4,6},{5,7},{6,4},{7,5},{8,10},{9,11},{10,... | collective-permute-start | bytes 626696 | tf_op jit(solution)/shard_map/ppermute | solution.py:342
  67.1 29.7 %copy-start.19 = (bf16[48,2176]{1,0:T(8,128)(2,1)}, bf16[48,2176]{1,0:T(8,128)(2,1)S(1)}, u32[]{:S(2)}) copy-start(bf16[48,2176]{1,0:T(8,128)(2,1)S(1)} %collective-permute-done.9.refs_8_.refs_6_) | copy-start | bytes 626692
  67.1 10.3 %collective-permute-start.11 = (bf16[48,2176]{1,0:T(8,128)(2,1)}, bf16[48,2176]{1,0:T(8,128)(2,1)}, u32[]{:S(2)}, u32[]{:S(2)}) collective-permute-start(bf16[48,2176]{1,0:T(8,128)(2,1)} %get-tuple-element.36), channel_id=1, source_target_pairs={{0,3},{1,2},{2,1},{3,0},{4,7},{5,6},{6,5},{7,4},{8,11},{9,10},{10,... | collective-permute-start | bytes 626696 | tf_op jit(solution)/shard_map/ppermute | solution.py:342
  74.8 10.4 %collective-permute-start.12 = (bf16[48,2176]{1,0:T(8,128)(2,1)}, bf16[48,2176]{1,0:T(8,128)(2,1)}, u32[]{:S(2)}, u32[]{:S(2)}) collective-permute-start(bf16[48,2176]{1,0:T(8,128)(2,1)} %get-tuple-element.37), channel_id=1, source_target_pairs={{0,4},{1,5},{2,6},{3,7},{4,0},{5,1},{6,2},{7,3},{8,12},{9,13},{10,... | collective-permute-start | bytes 626696 | tf_op jit(solution)/shard_map/ppermute | solution.py:342
  77.4 10.6 %collective-permute-start.13 = (bf16[48,2176]{1,0:T(8,128)(2,1)}, bf16[48,2176]{1,0:T(8,128)(2,1)}, u32[]{:S(2)}, u32[]{:S(2)}) collective-permute-start(bf16[48,2176]{1,0:T(8,128)(2,1)} %get-tuple-element.38), channel_id=1, source_target_pairs={{0,5},{1,4},{2,7},{3,6},{4,1},{5,0},{6,3},{7,2},{8,13},{9,12},{10,... | collective-permute-start | bytes 626696 | tf_op jit(solution)/shard_map/ppermute | solution.py:342
  85.2 7.0 %collective-permute-start.14 = (bf16[48,2176]{1,0:T(8,128)(2,1)}, bf16[48,2176]{1,0:T(8,128)(2,1)S(1)}, u32[]{:S(2)}, u32[]{:S(2)}) collective-permute-start(bf16[48,2176]{1,0:T(8,128)(2,1)} %get-tuple-element.39), channel_id=1, source_target_pairs={{0,6},{1,7},{2,4},{3,5},{4,2},{5,3},{6,0},{7,1},{8,14},{9,15},{10,... | collective-permute-start | bytes 626696 | tf_op jit(solution)/shard_map/ppermute | solution.py:342
  88.0 8.1 %collective-permute-start.15 = (bf16[48,2176]{1,0:T(8,128)(2,1)}, bf16[48,2176]{1,0:T(8,128)(2,1)S(1)}, u32[]{:S(2)}, u32[]{:S(2)}) collective-permute-start(bf16[48,2176]{1,0:T(8,128)(2,1)} %get-tuple-element.40), channel_id=1, source_target_pairs={{0,7},{1,6},{2,5},{3,4},{4,3},{5,2},{6,1},{7,0},{8,15},{9,14},{10,... | collective-permute-start | bytes 626696 | tf_op jit(solution)/shard_map/ppermute | solution.py:342
  104.4 23.3 %collective-permute-start.17 = (bf16[512,768]{1,0:T(8,128)(2,1)}, bf16[512,768]{1,0:T(8,128)(2,1)}, u32[]{:S(2)}, u32[]{:S(2)}) collective-permute-start(bf16[512,768]{1,0:T(8,128)(2,1)} %get-tuple-element.46), channel_id=1, source_target_pairs={{0,8},{24,16},{1,9},{25,17},{2,10},{26,18},{3,11},{27,19},{4,12},{... | collective-permute-start | bytes 2359304 | tf_op jit(solution)/shard_map/ppermute | solution.py:363
  117.4 24.5 %all-to-all-start.1 = ((bf16[8,48,2048]{2,1,0:T(8,128)(2,1)}), bf16[8,48,2048]{2,1,0:T(8,128)(2,1)S(1)}, u32[]{:S(2)}, u32[]{:S(2)}) async-start(bf16[8,48,2048]{2,1,0:T(8,128)(2,1)} %bitcast.31), calls=%async_computation.1 | async-start | bytes 3145728 | tf_op jit(solution)/shard_map/all_to_all | solution.py:372
  121.0 20.9 %copy-start = (f32[128,2048]{1,0:T(8,128)S(1)}, f32[128,2048]{1,0:T(8,128)}, u32[]{:S(2)}) copy-start(f32[128,2048]{1,0:T(8,128)} %get-tuple-element.29.stream_ref) | copy-start | bytes 3145732
  121.0 24.6 %collective-permute-start.16 = (bf16[512,768]{1,0:T(8,128)(2,1)}, bf16[512,768]{1,0:T(8,128)(2,1)}, u32[]{:S(2)}, u32[]{:S(2)}) collective-permute-start(bf16[512,768]{1,0:T(8,128)(2,1)} %get-tuple-element.46), channel_id=1, source_target_pairs={{8,16},{16,8},{9,17},{17,9},{10,18},{18,10},{11,19},{19,11},{12,20... | collective-permute-start | bytes 2359304 | tf_op jit(solution)/shard_map/ppermute | solution.py:364
  122.7 27.6 %collective-permute-start.19 = (bf16[512,768]{1,0:T(8,128)(2,1)}, bf16[512,768]{1,0:T(8,128)(2,1)}, u32[]{:S(2)}, u32[]{:S(2)}) collective-permute-start(bf16[512,768]{1,0:T(8,128)(2,1)} %get-tuple-element.48), channel_id=1, source_target_pairs={{0,8},{8,0},{16,24},{24,16},{1,9},{9,1},{17,25},{25,17},{2,10},{10... | collective-permute-start | bytes 2359304 | tf_op jit(solution)/shard_map/ppermute | solution.py:342
  129.9 48.1 %collective-permute-start.18 = (bf16[512,768]{1,0:T(8,128)(2,1)}, bf16[512,768]{1,0:T(8,128)(2,1)}, u32[]{:S(2)}, u32[]{:S(2)}) collective-permute-start(bf16[512,768]{1,0:T(8,128)(2,1)} %add_convert_fusion), channel_id=1, source_target_pairs={{0,16},{8,24},{16,0},{24,8},{1,17},{9,25},{17,1},{25,9},{2,18},{10... | collective-permute-start | bytes 2359304 | tf_op jit(solution)/shard_map/ppermute | solution.py:342
  143.8 34.2 %copy-start.6 = (bf16[512,768]{1,0:T(8,128)(2,1)S(1)}, bf16[512,768]{1,0:T(8,128)(2,1)}, u32[]{:S(2)}) copy-start(bf16[512,768]{1,0:T(8,128)(2,1)} %copy-done.5) | copy-start | bytes 2359300
  (13 other events, 38.0 us)

commit v2 on v1

--- a/solution.py
+++ b/solution.py
@@ -177,103 +177,117 @@
         copy.wait()
 
 
-def expert_kernel(me_ref, router_ref, rows_hbm, *refs, groups, gathered, pieces, slots):
-    own, got, cots = refs[:3], refs[3 : 3 + gathered], refs[3 + gathered : 3 + gathered + pieces]
-    hidden_ref, gated_ref, delta_ref, term_ref = refs[3 + gathered + pieces : -4]
-    rows_ref, cot_ref, w_ref, sems = refs[-4:]
-    rows_n, width = rows_ref.shape
-    part = width // groups
-    ff = hidden_ref.shape[1]
+def load_weights(copies, own, got, groups, target, cuts):
+    loads = [[copies.start(x.at[0], target.at[0, :, c]) for x, c in zip(own, cuts[0])]]
+    for d in range(1, groups):
+        loads.append([copies.start(got[d - 1].at[:, cuts[1]], target.at[d])])
+    return loads
+
+
+def cot_kernel(me_ref, down_hbm, *refs, groups, pieces, slots):
+    got, cots = refs[: groups - 1], refs[groups - 1 : groups - 1 + pieces]
+    out_ref, tag_ref, cot_ref, w_ref, sems = refs[groups - 1 + pieces :]
+    part, ff = w_ref.shape[1:]
     copies = Copies(sems)
-    loads = []
-    for d in range(groups):
-        at = pl.ds(d * part, part)
-        load = [copies.start(rows_hbm.at[:, at], rows_ref.at[:, at])]
-        if d == 0:
-            for n in range(3):
-                load.append(copies.start(own[n].at[0], w_ref.at[0, :, pl.ds(n * ff, ff)]))
-        else:
-            load.append(copies.start(got[d - 1], w_ref.at[d]))
-            if d == groups - 1 and gathered == groups:
-                load.append(copies.start(got[d], w_ref.at[d + 1]))
-        loads.append(load)
     cot_loads = load_rows(copies, me_ref[0], cots, cot_ref, slots)
-    cuts = [pl.ds(n * ff, ff) for n in range(3)]
-    pre_gate, pre_up, d_hidden = (jnp.zeros((rows_n, ff), F32) for _ in range(3))
-    logits = jnp.zeros((rows_n, router_ref.shape[0]), F32)
-    for d in range(groups):
-        at = pl.ds(d * part, part)
-        for copy in loads[d]:
-            copy.wait()
-        if d == groups - 1 and gathered == groups:
-            w_ref[d] = w_ref[d] + w_ref[d + 1]
-        block = rows_ref[:, at]
-        pre_gate = pre_gate + dot(block, w_ref[d, :, cuts[0]])
-        pre_up = pre_up + dot(block, w_ref[d, :, cuts[1]])
-        logits = logits + dot(block, router_ref[:, at], LANES)
-    for copy in cot_loads:
-        copy.wait()
-    for d in range(groups):
-        d_hidden = d_hidden + dot(cot_ref[:, pl.ds(d * part, part)], w_ref[d, :, cuts[2]])
+    cuts = ([pl.ds(0, ff)], pl.ds(2 * ff, ff))
+    loads = load_weights(copies, [down_hbm], got, groups, w_ref, cuts)
+    for copy in cot_loads + [x for load in loads for x in load]:
+        copy.wait()
+    total = dot(cot_ref[:, :part], w_ref[0])
+    for d in range(1, groups):
+        total = total + dot(cot_ref[:, pl.ds(d * part, part)], w_ref[d])
+    out_ref[...] = total
+    tag_ref[...] = cot_ref[:, pl.ds(cot_ref.shape[1] - HD, HD)].astype(F32)
+
+
+def rows_kernel(me_ref, router_ref, tag_ref, rows_ref, gate_hbm, up_hbm, *refs, groups):
+    got = refs[: groups - 1]
+    out_ref, share_ref, w_ref, sems = refs[groups - 1 :]
+    part = w_ref.shape[1]
+    ff = w_ref.shape[2] // 2
+    copies = Copies(sems)
+    cuts = ([pl.ds(0, ff), pl.ds(ff, ff)], pl.ds(0, 2 * ff))
+    loads = load_weights(copies, [gate_hbm, up_hbm], got, groups, w_ref, cuts)
+    for copy in [x for load in loads for x in load]:
+        copy.wait()
+    total = dot(rows_ref[:, :part], w_ref[0])
+    for d in range(1, groups):
+        total = total + dot(rows_ref[:, pl.ds(d * part, part)], w_ref[d])
+    out_ref[...] = total
+    logits = dot(rows_ref[...], router_ref[...], LANES)
     lanes = lax.broadcasted_iota(jnp.int32, logits.shape, 1)
     me = me_ref[0]
-    other = cot_ref[:, pl.ds(width, HD)].astype(F32).astype(jnp.int32)[:, : logits.shape[1]] - me
+    other = tag_ref[...].astype(jnp.int32)[:, : logits.shape[1]] - me
     sig = 1.0 / (1.0 + jnp.exp(-logits))
     own_sig = jnp.sum(jnp.where(lanes == me, sig, 0.0), axis=1, keepdims=True)
     other_sig = jnp.sum(jnp.where(lanes == other, sig, 0.0), axis=1, keepdims=True)
-    gate = own_sig / (own_sig + other_sig)
-    d_hidden = d_hidden * gate
+    share_ref[...] = jnp.broadcast_to(own_sig / (own_sig + other_sig), share_ref.shape)
+
+
+def expert_kernel(
+    me_ref, pre_ref, back_ref, share_ref, rows_ref, *refs, groups, last, pieces, slots
+):
+    got, cots = refs[:last], refs[last : last + pieces]
+    hidden_ref, gated_ref, delta_ref, inner_ref, down_ref = refs[last + pieces : -2]
+    cot_ref, sems = refs[-2:]
+    part = cot_ref.shape[1]
+    ff = hidden_ref.shape[1]
+    copies = Copies(sems)
+    at = pl.ds((groups - 1) * part, part)
+    cot_loads = load_rows(copies, me_ref[0], [x.at[:, at] for x in cots], cot_ref, slots)
+    mats = got[0][...] if last == 1 else got[0][...] + got[1][...]
+    pre_gate = pre_ref[:, :ff] + dot(rows_ref[:, at], mats[:, :ff])
+    pre_up = pre_ref[:, ff:] + dot(rows_ref[:, at], mats[:, ff : 2 * ff])
+    gate = share_ref[:, 0:1]
     sigma = 1.0 / (1.0 + jnp.exp(-pre_gate))
     act = pre_gate * sigma
     hidden = act * pre_up
     hidden_ref[...] = hidden.astype(BF16)
     gated_ref[...] = (hidden * gate).astype(BF16)
+    for copy in cot_loads:
+        copy.wait()
+    down_ref[...] = dot(cot_ref[...], gated_ref[...], ROWS).astype(BF16)
+    d_hidden = (back_ref[...] + dot(cot_ref[...], mats[:, 2 * ff :])) * gate
     delta_ref[:, :ff] = (d_hidden * pre_up * sigma * (1.0 + pre_gate * (1.0 - sigma))).astype(BF16)
     delta_ref[:, ff:] = (d_hidden * act).astype(BF16)
-    term(rows_ref, cot_ref, delta_ref, gated_ref, term_ref, (groups - 1) * part)
-
-
-def term(rows_ref, cot_ref, delta_ref, gated_ref, out_ref, start):
-    part = out_ref.shape[0]
-    ff = gated_ref.shape[1]
-    at = pl.ds(start, part)
-    out_ref[:, : 2 * ff] = dot(rows_ref[:, at], delta_ref[...], ROWS).astype(BF16)
-    out_ref[:, 2 * ff :] = dot(cot_ref[:, at], gated_ref[...], ROWS).astype(BF16)
+    inner_ref[...] = dot(rows_ref[:, at], delta_ref[...], ROWS).astype(BF16)
 
 
 def output_kernel(
-    me_ref, hidden_ref, gated_ref, delta_ref, rows_hbm, *refs, groups, gathered, pieces, slots
+    me_ref, hidden_ref, gated_ref, delta_ref, rows_ref, *refs, groups, last, pieces, slots
 ):
-    own, got, cots = refs[:1], refs[1 : 1 + gathered], refs[1 + gathered : 1 + gathered + pieces]
-    out_hbm, near_hbm, *terms = refs[1 + gathered + pieces : -6]
-    rows_ref, cot_ref, w_ref, out_ref, near_ref, sems = refs[-6:]
-    _, width = rows_ref.shape
+    late, refs = refs[:last], refs[last:]
+    own, early, cots = refs[0], refs[1 : groups - 1], refs[groups - 1 : groups - 1 + pieces]
+    out_hbm, *terms = refs[groups - 1 + pieces : -4]
+    cot_ref, w_ref, out_ref, sems = refs[-4:]
+    width = rows_ref.shape[1]
     part = width // groups
     ff = hidden_ref.shape[1]
     copies = Copies(sems)
-    row_load = copies.start(rows_hbm, rows_ref)
     cot_loads = load_rows(copies, me_ref[0], cots, cot_ref, slots)
-    loads = [[copies.start(own[0].at[0], w_ref.at[0])]]
-    for d in range(1, groups):
-        at = pl.ds(2 * ff, ff)
-        load = [copies.start(got[d - 1].at[:, at], w_ref.at[d])]
-        if d == groups - 1 and gathered == groups:
-            load.append(copies.start(got[d].at[:, at], w_ref.at[d + 1]))
-        loads.append(load)
-    row_load.wait()
+    cuts = ([pl.ds(0, ff)], pl.ds(2 * ff, ff))
+    loads = load_weights(copies, [own], early, groups - 1, w_ref, cuts)
+    for d in range(groups - 1):
+        at = pl.ds(d * part, part)
+        terms[2 * d + 1][...] = dot(rows_ref[:, at], delta_ref[...], ROWS).astype(BF16)
     for copy in cot_loads:
         copy.wait()
-    term(rows_ref, cot_ref, delta_ref, gated_ref, near_ref, part)
-    stores = [copies.start(near_ref, near_hbm)]
-    for n, out in enumerate(terms):
-        term(rows_ref, cot_ref, delta_ref, gated_ref, out, (0 if n == 0 else n + 1) * part)
+    for d in range(groups - 1):
+        at = pl.ds(d * part, part)
+        terms[2 * d][...] = dot(cot_ref[:, at], gated_ref[...], ROWS).astype(BF16)
+    stores = []
     for d in range(groups):
-        for copy in loads[d]:
-            copy.wait()
-        if d == groups - 1 and gathered == groups:
-            w_ref[d] = w_ref[d] + w_ref[d + 1]
+        if d < groups - 1:
+            for copy in loads[d]:
+                copy.wait()
+            mats = w_ref[d]
+        else:
+            mats = late[0][:, 2 * ff :]
+            if last == 2:
+                mats = mats + late[1][:, 2 * ff :]
         at = pl.ds(d * part, part)
-        out_ref[:, at] = dot(hidden_ref[...], w_ref[d], LANES).astype(BF16)
+        out_ref[:, at] = dot(hidden_ref[...], mats, LANES).astype(BF16)
         stores.append(copies.start(out_ref.at[:, at], out_hbm.at[:, at]))
     for copy in stores:
         copy.wait()
@@ -305,8 +319,8 @@
         out_ref[0, :, at] = value.astype(BF16)
 
 
-def total_kernel(scale_ref, *refs):
-    parts, outs = refs[:-3], refs[-3:]
+def total_kernel(scale_ref, *refs, outputs):
+    parts, outs = refs[:-outputs], refs[-outputs:]
     ff = outs[0].shape[1]
     scale = jnp.where(scale_ref[0] > 0, 1.0, 0.0)
     for n, out in enumerate(outs):
@@ -437,7 +451,6 @@
         cots = [exchange(cot_send[0].reshape(experts, slots, -1)).reshape(cot_shape)]
 
     got = gather_xor(jnp.concatenate([w_gate[0], w_up[0], w_down[0]], axis=1), "dp")
-    own = [w_gate, w_up, w_down]
 
     (local,) = kernel_call(
         state_kernel,
@@ -475,54 +488,80 @@
     )(i, queries, prefix, intra, residual_in, attn_gain[None], moe_gain[None], put)
     rows = exchange(send_rows.reshape(experts, slots, width)).reshape(rows_n, width)
 
-    hidden, gated, delta, far_term = kernel_call(
+    early = got[: groups - 2]
+    late = got[groups - 2 :]
+    cot_part, tags = kernel_call(
+        cot_kernel,
+        "sh",
+        [("v", (rows_n, ff), F32), ("v", (rows_n, HD), F32)],
+        [
+            pltpu.VMEM((rows_n, width + HD), BF16),
+            pltpu.VMEM((groups - 1, part, ff), BF16),
+            pltpu.SemaphoreType.DMA((groups + pieces,)),
+        ],
+        groups=groups - 1,
+        pieces=pieces,
+        slots=slots,
+    )(me, w_down, *early, *cots)
+    row_part, share = kernel_call(
+        rows_kernel,
+        "svvvh",
+        [("v", (rows_n, 2 * ff), F32), ("v", (rows_n, HD), F32)],
+        [
+            pltpu.VMEM((groups - 1, part, 2 * ff), BF16),
+            pltpu.SemaphoreType.DMA((groups + 1,)),
+        ],
+        groups=groups - 1,
+    )(me, turned, tags, rows, w_gate, w_up, *early)
+    hidden, gated, delta, far_inner, far_down = kernel_call(
         expert_kernel,
-        "svh",
+        "svvvv" + "v" * len(late) + "h",
         [
             ("v", (rows_n, ff), BF16),
             ("v", (rows_n, ff), BF16),
             ("v", (rows_n, 2 * ff), BF16),
-            ("v", (part, 3 * ff), BF16),
-        ],
-        [
-            pltpu.VMEM((rows_n, width), BF16),
-            pltpu.VMEM((rows_n, width + HD), BF16),
-            pltpu.VMEM((len(got) + 1, part, 3 * ff), BF16),
-            pltpu.SemaphoreType.DMA((groups + len(got) + 3 + pieces,)),
+            ("v", (part, 2 * ff), BF16),
+            ("v", (part, ff), BF16),
+        ],
+        [
+            pltpu.VMEM((rows_n, part), BF16),
+            pltpu.SemaphoreType.DMA((pieces,)),
         ],
         groups=groups,
-        gathered=len(got),
+        last=len(late),
         pieces=pieces,
         slots=slots,
-    )(me, turned, rows, *own, *got, *cots)
-    expert_out, near_term, *terms = kernel_call(
+    )(me, row_part, cot_part, share, rows, *late, *cots)
+    expert_out, *terms = kernel_call(
         output_kernel,
-        "svvvh",
-        [("h", (rows_n, width), BF16), ("h", (part, 3 * ff), BF16)]
-        + [("v", (part, 3 * ff), BF16)] * (groups - 2),
-        [
+        "svvvv" + "v" * len(late) + "h",
+        [("h", (rows_n, width), BF16)]
+        + [("v", (part, ff), BF16), ("v", (part, 2 * ff), BF16)] * (groups - 1),
+        [
+            pltpu.VMEM((rows_n, width + HD), BF16),
+            pltpu.VMEM((groups - 1, part, ff), BF16),
             pltpu.VMEM((rows_n, width), BF16),
-            pltpu.VMEM((rows_n, width + HD), BF16),
-            pltpu.VMEM((len(got) + 1, part, ff), BF16),
-            pltpu.VMEM((rows_n, width), BF16),
-            pltpu.VMEM((part, 3 * ff), BF16),
-            pltpu.SemaphoreType.DMA((groups + len(got) + 3 + pieces,)),
+            pltpu.SemaphoreType.DMA((2 * groups + pieces,)),
         ],
         groups=groups,
-        gathered=len(got),
+        last=len(late),
         pieces=pieces,
         slots=slots,
-    )(me, hidden, gated, delta, rows, w_down, *got, *cots)
-    terms = [terms[0], near_term, *terms[1:]]
-    grads = kernel_call(total_kernel, "sv", [("v", (part, ff), F32)] * 3)(
-        trainable, *scatter_xor(terms + [far_term], "dp")
-    )
-
+    )(me, hidden, gated, delta, rows, *late, w_down, *early, *cots)
+    down_parts = scatter_xor(terms[0::2] + [far_down], "dp")
+    inner_parts = scatter_xor(terms[1::2] + [far_inner], "dp")
     back = exchange(expert_out.reshape(peers, slots, width)).reshape(rows_n, width)
     (mixed,) = kernel_call(
         combine_kernel, "sv", [("v", (1, tokens, width), BF16)], groups=groups
     )(i, stream, normed, router.T, expert_ids, slot, back)
-    return (mixed, grads[0][None], grads[1][None], grads[2][None])
+    mixed, *inner_parts = lax.optimization_barrier((mixed, *inner_parts))
+    (grad_down,) = kernel_call(
+        total_kernel, "sv", [("v", (part, ff), F32)], outputs=1
+    )(trainable, *down_parts)
+    grad_gate, grad_up = kernel_call(
+        total_kernel, "sv", [("v", (part, ff), F32)] * 2, outputs=2
+    )(trainable, *inner_parts)
+    return (mixed, grad_gate[None], grad_up[None], grad_down[None])
 
 
 def solution(mesh):

time: 182 us -> 183 us (level)
  waiting for transfers between devices: 89.2 us -> 76.7 us
  starting transfers between devices: 51.9 us -> 58.3 us
  Pallas kernels: 27.2 us -> 31.1 us
  local copies, waits for them, and re-layouts: 5.62 us -> 8.36 us
    ppermute x11 -> x13, waiting for transfers between devices: 74.6 us -> 64.7 us  [send_xor(): lax.ppermute(x, axis, [(j, j ^ d) for j in range(lax.axis_size(axis))])]
    all_to_all x2, waiting for transfers between devices: 3.96 us -> 0.01 us  [exchange(): return lax.all_to_all(x, 'seq', split_axis=0, concat_axis=0, tiled=True)]
    pallas_call x8 -> x11, Pallas kernels: 27.2 us -> 31.1 us  [call(): pl.pallas_call(functools.partial(body, **static), in_specs=[pl.BlockSpec(...]
    ppermute x1 -> x2, starting transfers between devices: 6.47 us -> 9.71 us  [scatter_xor(): relayed = lax.ppermute(parts[3], axis, ENDS)]
    unnamed x47 -> x75, local copies, waits for them, and re-layouts: 5.59 us -> 8.33 us
    ppermute x11 -> x13, starting transfers between devices: 22.9 us -> 25.2 us  [send_xor(): lax.ppermute(x, axis, [(j, j ^ d) for j in range(lax.axis_size(axis))])]
  transfers between devices with their start and end apart: 22 -> 26, of which waited for: 13 -> 12; matrix products, arithmetic and copies ran while one was open for 2% -> 2% of each run, Pallas kernels for 9% -> 13%
where the time goes in v2:
time: 183 us; the launch traced here: 182 us
  waiting for transfers between devices  76.7 us (42%)
  starting transfers between devices  58.3 us (32%)
  Pallas kernels  31.1 us (17%)
  local copies, waits for them, and re-layouts  8.36 us (5%)
  other arithmetic  5.75 us (3%)
    ppermute x13, waiting for transfers between devices, send_xor(): lax.ppermute(x, axis, [(j, j ^ d) for j in range(lax.axis_size(axis))])  64.7 us
    pallas_call x11, Pallas kernels, call(): pl.pallas_call(functools.partial(body, **static), in_specs=[pl.BlockSpec(...  31.1 us
    ppermute x13, starting transfers between devices, send_xor(): lax.ppermute(x, axis, [(j, j ^ d) for j in range(lax.axis_size(axis))])  25.2 us
    ppermute x3, starting transfers between devices, exclusive_prefix(): lax.ppermute(total, axis, [(j, j + d) for j in range(n - d)])  10.9 us
    ppermute x2, starting transfers between devices, scatter_xor(): relayed = lax.ppermute(parts[3], axis, ENDS)  9.71 us
    unnamed x75, local copies, waits for them, and re-layouts  8.33 us
    ppermute x3, waiting for transfers between devices, exclusive_prefix(): lax.ppermute(total, axis, [(j, j + d) for j in range(n - d)])  8.3 us
    all_to_all x2, starting transfers between devices, exchange(): return lax.all_to_all(x, 'seq', split_axis=0, concat_axis=0, tiled=True)  7.72 us
  transfers between devices with their start and end apart: 26, of which 12 were waited for; matrix products, arithmetic and copies ran while one was open for 2% of the time, Pallas kernels for 13%

profile of v2, /device:TPU:0, one launch (start us, length us, event | category | flops | bytes accessed | tf_op | source)
XLA Modules:
  0.0 182.0 jit_solution(4553447839812592198)
XLA Ops:
  0.6 1.9 %shard_map.156 = bf16[16,128,128]{2,1,0:T(8,128)(2,1)S(1)} custom-call(bf16[1,128,2048]{2,1,0:T(8,128)(2,1)} %k_ref.1, bf16[1,128,2048]{2,1,0:T(8,128)(2,1)} %v_ref.1), custom_call_target="tpu_custom_call" | custom-call | flops 1000000000 | bytes 4000000 | tf_op jit(solution)/shard_map/pallas_call | solution.py:32
  4.4 6.4 %collective-permute-start.3 = (bf16[8,128,128]{2,1,0:T(8,128)(2,1)S(1)}, bf16[8,128,128]{2,1,0:T(8,128)(2,1)}, u32[]{:S(2)}, u32[]{:S(2)}) collective-permute-start(bf16[8,128,128]{2,1,0:T(8,128)(2,1)S(1)} %fusion.2), channel_id=1, source_target_pairs={{0,6},{1,7},{8,14},{9,15},{16,22},{17,23},{24,30},{25,31}} | collective-permute-start | bytes 786440 | tf_op jit(solution)/shard_map/ppermute | solution.py:345
  10.9 2.0 %collective-permute-start.2 = (bf16[8,128,128]{2,1,0:T(8,128)(2,1)S(1)}, bf16[8,128,128]{2,1,0:T(8,128)(2,1)}, u32[]{:S(2)}, u32[]{:S(2)}) collective-permute-start(bf16[8,128,128]{2,1,0:T(8,128)(2,1)S(1)} %fusion.2), channel_id=1, source_target_pairs={{0,4},{1,5},{2,6},{3,7},{8,12},{9,13},{10,14},{11,15},{16,20},{17,... | collective-permute-start | bytes 786440 | tf_op jit(solution)/shard_map/ppermute | solution.py:345
  12.8 2.5 %collective-permute-start.1 = (bf16[8,128,128]{2,1,0:T(8,128)(2,1)S(1)}, bf16[8,128,128]{2,1,0:T(8,128)(2,1)}, u32[]{:S(2)}, u32[]{:S(2)}) collective-permute-start(bf16[8,128,128]{2,1,0:T(8,128)(2,1)S(1)} %fusion.2), channel_id=1, source_target_pairs={{0,2},{1,3},{2,4},{3,5},{4,6},{5,7},{8,10},{9,11},{10,12},{11,13},... | collective-permute-start | bytes 786440 | tf_op jit(solution)/shard_map/ppermute | solution.py:345
  16.9 6.7 %collective-permute-done.2 = bf16[8,128,128]{2,1,0:T(8,128)(2,1)} collective-permute-done((bf16[8,128,128]{2,1,0:T(8,128)(2,1)S(1)}, bf16[8,128,128]{2,1,0:T(8,128)(2,1)}, u32[]{:S(2)}, u32[]{:S(2)}) %collective-permute-start.2) | collective-permute-done | bytes 262176 | tf_op jit(solution)/shard_map/ppermute | solution.py:345
  23.6 2.0 %fusion.4 = (bf16[8,128,128]{2,1,0:T(8,128)(2,1)S(1)}, bf16[8,128,128]{2,1,0:T(8,128)(2,1)}) fusion(bf16[8,128,128]{2,1,0:T(8,128)(2,1)S(1)} %collective-permute-done, bf16[8,128,128]{2,1,0:T(8,128)(2,1)} %collective-permute-done.3, bf16[8,128,128]{2,1,0:T(8,128)(2,1)} %collective-permute-done.2, bf16[8,128,128]{2,1,0:T(8,128)(2,1)} %collective-permute-done.1, ...), kind=kLoop, calls=%fused_computation.9 | loop fusion | flops 1703936 | bytes 1835014 | tf_op jit(solution)/shard_map/convert_element_type | solution.py:351
  26.6 2.6 %collective-permute-start.6 = (bf16[512,768]{1,0:T(8,128)(2,1)}, bf16[512,768]{1,0:T(8,128)(2,1)}, u32[]{:S(2)}, u32[]{:S(2)}) collective-permute-start(bf16[512,768]{1,0:T(8,128)(2,1)} %pad_maximum_fusion), channel_id=1, source_target_pairs={{0,16},{8,24},{16,0},{24,8},{1,17},{9,25},{17,1},{25,9},{2,18},{10... | collective-permute-start | bytes 2359304 | tf_op jit(solution)/shard_map/ppermute | solution.py:356
  29.3 2.6 %shard_map.157.intra_ref = f32[128,2048]{1,0:T(8,128)S(1)} custom-call(bf16[1,128,2048]{2,1,0:T(8,128)(2,1)S(1)} %copy-done.16, bf16[1,128,2048]{2,1,0:T(8,128)(2,1)S(1)} %copy-done.14, bf16[1,128,2048]{2,1,0:T(8,128)(2,1)S(1)} %copy-done.15), custom_call_target="tpu_custom_call" | custom-call | flops 1000000000 | bytes 4000000 | tf_op jit(solution)/shard_map/pallas_call | solution.py:32
  32.0 3.5 %shard_map.158 = (bf16[128,384]{1,0:T(8,128)(2,1)S(1)}, s32[128,2]{1,0:T(8,128)S(1)}, bf16[48,2176]{1,0:T(8,128)(2,1)}, bf16[48,2176]{1,0:T(8,128)(2,1)}, bf16[4...) custom-call(s32[1]{0:T(128)} %bitcast.i_ref, ...), custom_call_target="tpu_custom_call" | custom-call | flops 1000000000 | bytes 4000000 | tf_op jit(solution)/shard_map/pallas_call | solution.py:32
  36.2 2.8 %shard_map.159 = (f32[128,2048]{1,0:T(8,128)}, bf16[128,2048]{1,0:T(8,128)(2,1)}, bf16[384,2048]{1,0:T(8,128)(2,1)}) custom-call(s32[1]{0:T(128)} %bitcast.i_ref, bf16[1,128,2048]{2,1,0:T(8,128)(2,1)S(1)} %copy-done.16, bf16[16,128,128]{2,1,0:T(8,128)(2,1)S(1)} %maximum_select_fusion.prefix_ref, f32[128,2048]{1,0:T(8,128)S(1)} %shard_map.157.intra_ref, ...), custom_call_target="tpu_custom_call" | custom-call | flops 1000000000 | bytes 4000000 | tf_op jit(solution)/shard_map/pallas_call | solution.py:32
  39.1 4.0 %all-to-all-start = ((bf16[8,48,2048]{2,1,0:T(8,128)(2,1)}), bf16[8,48,2048]{2,1,0:T(8,128)(2,1)S(1)}, u32[]{:S(2)}, u32[]{:S(2)}) async-start(bf16[8,48,2048]{2,1,0:T(8,128)(2,1)} %bitcast.30), calls=%async_computation | async-start | bytes 3145728 | tf_op jit(solution)/shard_map/all_to_all | solution.py:386
  47.5 17.7 %collective-permute-done.6.refs_1_.refs_4_ = bf16[512,768]{1,0:T(8,128)(2,1)} collective-permute-done((bf16[512,768]{1,0:T(8,128)(2,1)}, bf16[512,768]{1,0:T(8,128)(2,1)}, u32[]{:S(2)}, u32[]{:S(2)}) %collective-permute-start.6) | collective-permute-done | bytes 786464 | tf_op jit(solution)/shard_map/ppermute | solution.py:356
  66.4 1.9 %collective-permute-done.8.refs_4_.refs_7_ = bf16[48,2176]{1,0:T(8,128)(2,1)} collective-permute-done((bf16[48,2176]{1,0:T(8,128)(2,1)S(1)}, bf16[48,2176]{1,0:T(8,128)(2,1)}, u32[]{:S(2)}, u32[]{:S(2)}) %collective-permute-start.8) | collective-permute-done | bytes 208928 | tf_op jit(solution)/shard_map/ppermute | solution.py:356
  74.6 1.9 %collective-permute-start.12 = (bf16[48,2176]{1,0:T(8,128)(2,1)}, bf16[48,2176]{1,0:T(8,128)(2,1)S(1)}, u32[]{:S(2)}, u32[]{:S(2)}) collective-permute-start(bf16[48,2176]{1,0:T(8,128)(2,1)} %get-tuple-element.50), channel_id=1, source_target_pairs={{0,6},{1,7},{2,4},{3,5},{4,2},{5,3},{6,0},{7,1},{8,14},{9,15},{10,... | collective-permute-start | bytes 626696 | tf_op jit(solution)/shard_map/ppermute | solution.py:356
  76.5 6.6 %collective-permute-done.11.refs_7_.refs_10_ = bf16[48,2176]{1,0:T(8,128)(2,1)} collective-permute-done((bf16[48,2176]{1,0:T(8,128)(2,1)}, bf16[48,2176]{1,0:T(8,128)(2,1)}, u32[]{:S(2)}, u32[]{:S(2)}) %collective-permute-start.11) | collective-permute-done | bytes 208928 | tf_op jit(solution)/shard_map/ppermute | solution.py:356
  83.1 2.3 %collective-permute-start.13 = (bf16[48,2176]{1,0:T(8,128)(2,1)}, bf16[48,2176]{1,0:T(8,128)(2,1)S(1)}, u32[]{:S(2)}, u32[]{:S(2)}) collective-permute-start(bf16[48,2176]{1,0:T(8,128)(2,1)} %get-tuple-element.51), channel_id=1, source_target_pairs={{0,7},{1,6},{2,5},{3,4},{4,3},{5,2},{6,1},{7,0},{8,15},{9,14},{10,... | collective-permute-start | bytes 626696 | tf_op jit(solution)/shard_map/ppermute | solution.py:356
  86.0 4.6 %collective-permute-done.13.refs_9_.refs_12_ = bf16[48,2176]{1,0:T(8,128)(2,1)S(1)} collective-permute-done((bf16[48,2176]{1,0:T(8,128)(2,1)}, bf16[48,2176]{1,0:T(8,128)(2,1)S(1)}, u32[]{:S(2)}, u32[]{:S(2)}) %collective-permute-start.13) | collective-permute-done | bytes 208928 | tf_op jit(solution)/shard_map/ppermute | solution.py:356
  91.3 2.3 %shard_map.160 = (f32[384,256]{1,0:T(8,128)S(1)}, f32[384,128]{1,0:T(8,128)S(1)}) custom-call(s32[1]{0:T(128)} %bitcast.3.me_ref, bf16[1,512,256]{2,1,0:T(8,128)(2,1)} %refs_2_.1, bf16[512,768]{1,0:T(8,128)(2,1)} %collective-permute-done.5.refs_0_.refs_3_, bf16[512,768]{1,0:T(8,128)(2,1)} %collective-permute-done.6.refs_1_.refs_4_, ...), custom_call_target="tpu_custom_call" | custom-call | flops 1000000000 | bytes 4000000 | tf_op jit(solution)/shard_map/pallas_call | solution.py:32
  96.2 2.7 %shard_map.161 = (f32[384,512]{1,0:T(8,128)S(1)}, f32[384,128]{1,0:T(8,128)S(1)}) custom-call(s32[1]{0:T(128)} %bitcast.3.me_ref, bf16[8,2048]{1,0:T(8,128)(2,1)S(1)} %copy-done.11, f32[384,128]{1,0:T(8,128)S(1)} %copy-done.8, bf16[384,2048]{1,0:T(8,128)(2,1)S(1)} %bitcast.23, bf16[1,512,256]{2,1,0:T(8,128)(2,1)} %gate_hbm.1, bf16[1,512,256]{2,1,0:T(8,128)(2,1)} %up_hbm.1, ...), custom_call_target="tpu_custom_call" | custom-call | flops 1000000000 | bytes 4000000 | tf_op jit(solution)/shard_map/pallas_call | solution.py:32
  98.9 2.9 %shard_map.162 = (bf16[384,256]{1,0:T(8,128)(2,1)S(1)}, bf16[384,256]{1,0:T(8,128)(2,1)S(1)}, bf16[384,512]{1,0:T(8,128)(2,1)S(1)}, bf16[512,512]{1,0:T(8,128)(2,1)}, bf16[512,256]{1,0:T(8,128)(2,1)S(1)}) custom-call(s32[1]{0:T(128)} %bitcast.3.me_ref, f32[384,512]{1,0:T(8,128)S(1)} %get-tuple-element.54.pre_ref, f32[384,256]{1,0:T(8,128)S(1)} %get-tuple-element.55.back_ref, ...), custom_call_target="tpu_custom_call" | custom-call | flops 1000000000 | bytes 4000000 | tf_op jit(solution)/shard_map/pallas_call | solution.py:32
  102.5 4.6 %collective-permute-start.17 = (bf16[512,512]{1,0:T(8,128)(2,1)}, bf16[512,512]{1,0:T(8,128)(2,1)}, u32[]{:S(2)}, u32[]{:S(2)}) collective-permute-start(bf16[512,512]{1,0:T(8,128)(2,1)} %get-tuple-element.62), channel_id=1, source_target_pairs={{0,8},{24,16},{1,9},{25,17},{2,10},{26,18},{3,11},{27,19},{4,12},{... | collective-permute-start | bytes 1572872 | tf_op jit(solution)/shard_map/ppermute | solution.py:377
  107.0 7.2 %shard_map.163 = (bf16[384,2048]{1,0:T(8,128)(2,1)}, bf16[512,256]{1,0:T(8,128)(2,1)S(1)}, bf16[512,512]{1,0:T(8,128)(2,1)S(1)}, bf16[512,256]{1,0:T(8,128)(2,1)...) custom-call(s32[1]{0:T(128)} %bitcast.3.me_ref, ...), custom_call_target="tpu_custom_call" | custom-call | flops 1000000000 | bytes 4000000 | tf_op jit(solution)/shard_map/pallas_call | solution.py:32
  117.3 3.7 %all-to-all-start.1 = ((bf16[8,48,2048]{2,1,0:T(8,128)(2,1)}), bf16[8,48,2048]{2,1,0:T(8,128)(2,1)S(1)}, u32[]{:S(2)}, u32[]{:S(2)}) async-start(bf16[8,48,2048]{2,1,0:T(8,128)(2,1)} %bitcast.31), calls=%async_computation.1 | async-start | bytes 3145728 | tf_op jit(solution)/shard_map/all_to_all | solution.py:386
  123.3 5.1 %collective-permute-start.21 = (bf16[512,256]{1,0:T(8,128)(2,1)S(1)}, bf16[512,256]{1,0:T(8,128)(2,1)S(1)}, u32[]{:S(2)}, u32[]{:S(2)}) collective-permute-start(bf16[512,256]{1,0:T(8,128)(2,1)S(1)} %copy-done.23), channel_id=1, source_target_pairs={{0,8},{24,16},{1,9},{25,17},{2,10},{26,18},{3,11},{27,19},{4,12},{... | collective-permute-start | bytes 786440 | tf_op jit(solution)/shard_map/ppermute | solution.py:377
  128.5 2.0 %collective-permute-start.23 = (bf16[512,256]{1,0:T(8,128)(2,1)S(1)}, bf16[512,256]{1,0:T(8,128)(2,1)S(1)}, u32[]{:S(2)}, u32[]{:S(2)}) collective-permute-start(bf16[512,256]{1,0:T(8,128)(2,1)S(1)} %copy-done.25), channel_id=1, source_target_pairs={{0,8},{8,0},{16,24},{24,16},{1,9},{9,1},{17,25},{25,17},{2,10},{10... | collective-permute-start | bytes 786440 | tf_op jit(solution)/shard_map/ppermute | solution.py:356
  130.5 2.0 %add_convert_fusion = bf16[512,512]{1,0:T(8,128)(2,1)} fusion(bf16[512,512]{1,0:T(8,128)(2,1)} %collective-permute-done.17, bf16[512,512]{1,0:T(8,128)(2,1)S(1)} %copy-done.3), kind=kLoop, calls=%fused_computation | loop fusion | flops 1048576 | bytes 1572864 | tf_op jit(solution)/shard_map/convert_element_type | solution.py:379
  132.5 2.6 %collective-permute-done.21 = bf16[512,256]{1,0:T(8,128)(2,1)S(1)} collective-permute-done((bf16[512,256]{1,0:T(8,128)(2,1)S(1)}, bf16[512,256]{1,0:T(8,128)(2,1)S(1)}, u32[]{:S(2)}, u32[]{:S(2)}) %collective-permute-start.21) | collective-permute-done | bytes 262176 | tf_op jit(solution)/shard_map/ppermute | solution.py:377
  135.1 3.9 %collective-permute-start.18 = (bf16[512,512]{1,0:T(8,128)(2,1)}, bf16[512,512]{1,0:T(8,128)(2,1)}, u32[]{:S(2)}, u32[]{:S(2)}) collective-permute-start(bf16[512,512]{1,0:T(8,128)(2,1)} %add_convert_fusion), channel_id=1, source_target_pairs={{0,16},{8,24},{16,0},{24,8},{1,17},{9,25},{17,1},{25,9},{2,18},{10... | collective-permute-start | bytes 1572872 | tf_op jit(solution)/shard_map/ppermute | solution.py:356
  139.1 5.5 %collective-permute-start.22 = (bf16[512,256]{1,0:T(8,128)(2,1)S(1)}, bf16[512,256]{1,0:T(8,128)(2,1)S(1)}, u32[]{:S(2)}, u32[]{:S(2)}) collective-permute-start(bf16[512,256]{1,0:T(8,128)(2,1)S(1)} %add_convert_fusion.1), channel_id=1, source_target_pairs={{0,16},{8,24},{16,0},{24,8},{1,17},{9,25},{17,1},{25,9},{2,18},{10... | collective-permute-start | bytes 786440 | tf_op jit(solution)/shard_map/ppermute | solution.py:356
  145.3 14.8 %collective-permute-done.23.refs_3_ = bf16[512,256]{1,0:T(8,128)(2,1)S(1)} collective-permute-done((bf16[512,256]{1,0:T(8,128)(2,1)S(1)}, bf16[512,256]{1,0:T(8,128)(2,1)S(1)}, u32[]{:S(2)}, u32[]{:S(2)}) %collective-permute-start.23) | collective-permute-done | bytes 262176 | tf_op jit(solution)/shard_map/ppermute | solution.py:356
  160.1 16.1 %collective-permute-done.22.refs_2_ = bf16[512,256]{1,0:T(8,128)(2,1)S(1)} collective-permute-done((bf16[512,256]{1,0:T(8,128)(2,1)S(1)}, bf16[512,256]{1,0:T(8,128)(2,1)S(1)}, u32[]{:S(2)}, u32[]{:S(2)}) %collective-permute-start.22) | collective-permute-done | bytes 262176 | tf_op jit(solution)/shard_map/ppermute | solution.py:356
  179.6 2.5 %shard_map.165 = (f32[512,256]{1,0:T(8,128)}, f32[512,256]{1,0:T(8,128)}) custom-call(s32[1]{0:T(128)S(6)} %copy.19.scale_ref, bf16[512,512]{1,0:T(8,128)(2,1)S(1)} %copy-done.19, bf16[512,512]{1,0:T(8,128)(2,1)} %collective-permute-done.16.refs_1_, bf16[512,512]{1,0:T(8,128)(2,1)} %collective-permute-done.18.refs_2_, ...), custom_call_target="tpu_custom_call" | custom-call | flops 1000000000 | bytes 4000000 | tf_op jit(solution)/shard_map/pallas_call | solution.py:32
  (115 shorter events, 30.4 us)
Async XLA Ops:
  2.6 23.1 %copy-start.28 = (bf16[1,512,256]{2,1,0:T(8,128)(2,1)S(1)}, bf16[1,512,256]{2,1,0:T(8,128)(2,1)}, u32[]{:S(2)}) copy-start(bf16[1,512,256]{2,1,0:T(8,128)(2,1)} %up_hbm.1) | copy-start | bytes 786436
  2.6 23.1 %copy-start.29 = (bf16[1,512,256]{2,1,0:T(8,128)(2,1)S(1)}, bf16[1,512,256]{2,1,0:T(8,128)(2,1)}, u32[]{:S(2)}) copy-start(bf16[1,512,256]{2,1,0:T(8,128)(2,1)} %gate_hbm.1) | copy-start | bytes 786436
  2.6 23.1 %copy-start.30 = (bf16[1,512,256]{2,1,0:T(8,128)(2,1)S(1)}, bf16[1,512,256]{2,1,0:T(8,128)(2,1)}, u32[]{:S(2)}) copy-start(bf16[1,512,256]{2,1,0:T(8,128)(2,1)} %refs_2_.1) | copy-start | bytes 786436
  2.6 1.7 collective-permute-start
  4.4 12.4 %collective-permute-start.3 = (bf16[8,128,128]{2,1,0:T(8,128)(2,1)S(1)}, bf16[8,128,128]{2,1,0:T(8,128)(2,1)}, u32[]{:S(2)}, u32[]{:S(2)}) collective-permute-start(bf16[8,128,128]{2,1,0:T(8,128)(2,1)S(1)} %fusion.2), channel_id=1, source_target_pairs={{0,6},{1,7},{8,14},{9,15},{16,22},{17,23},{24,30},{25,31}} | collective-permute-start | bytes 786440 | tf_op jit(solution)/shard_map/ppermute | solution.py:345
  10.9 12.8 %collective-permute-start.2 = (bf16[8,128,128]{2,1,0:T(8,128)(2,1)S(1)}, bf16[8,128,128]{2,1,0:T(8,128)(2,1)}, u32[]{:S(2)}, u32[]{:S(2)}) collective-permute-start(bf16[8,128,128]{2,1,0:T(8,128)(2,1)S(1)} %fusion.2), channel_id=1, source_target_pairs={{0,4},{1,5},{2,6},{3,7},{8,12},{9,13},{10,14},{11,15},{16,20},{17,... | collective-permute-start | bytes 786440 | tf_op jit(solution)/shard_map/ppermute | solution.py:345
  12.8 10.8 %collective-permute-start.1 = (bf16[8,128,128]{2,1,0:T(8,128)(2,1)S(1)}, bf16[8,128,128]{2,1,0:T(8,128)(2,1)}, u32[]{:S(2)}, u32[]{:S(2)}) collective-permute-start(bf16[8,128,128]{2,1,0:T(8,128)(2,1)S(1)} %fusion.2), channel_id=1, source_target_pairs={{0,2},{1,3},{2,4},{3,5},{4,6},{5,7},{8,10},{9,11},{10,12},{11,13},... | collective-permute-start | bytes 786440 | tf_op jit(solution)/shard_map/ppermute | solution.py:345
  25.7 10.5 %collective-permute-start.4 = (bf16[8,128,128]{2,1,0:T(8,128)(2,1)}, bf16[8,128,128]{2,1,0:T(8,128)(2,1)S(1)}, u32[]{:S(2)}, u32[]{:S(2)}) collective-permute-start(bf16[8,128,128]{2,1,0:T(8,128)(2,1)} %get-tuple-element.77), channel_id=1, source_target_pairs={{0,1},{1,0},{2,3},{3,2},{4,5},{5,4},{6,7},{7,6},{8,9},{9,8},{10,11... | collective-permute-start | bytes 786440 | tf_op jit(solution)/shard_map/ppermute | solution.py:350
  26.6 38.5 %collective-permute-start.6 = (bf16[512,768]{1,0:T(8,128)(2,1)}, bf16[512,768]{1,0:T(8,128)(2,1)}, u32[]{:S(2)}, u32[]{:S(2)}) collective-permute-start(bf16[512,768]{1,0:T(8,128)(2,1)} %pad_maximum_fusion), channel_id=1, source_target_pairs={{0,16},{8,24},{16,0},{24,8},{1,17},{9,25},{17,1},{25,9},{2,18},{10... | collective-permute-start | bytes 2359304 | tf_op jit(solution)/shard_map/ppermute | solution.py:356
  39.1 34.4 %copy-start.9 = (bf16[2048,8]{0,1:T(8,128)(2,1)S(1)}, bf16[2048,8]{0,1:T(8,128)(2,1)}, u32[]{:S(2)}) copy-start(bf16[2048,8]{0,1:T(8,128)(2,1)} %param.19) | copy-start | bytes 98308
  39.1 55.2 %all-to-all-start = ((bf16[8,48,2048]{2,1,0:T(8,128)(2,1)}), bf16[8,48,2048]{2,1,0:T(8,128)(2,1)S(1)}, u32[]{:S(2)}, u32[]{:S(2)}) async-start(bf16[8,48,2048]{2,1,0:T(8,128)(2,1)} %bitcast.30), calls=%async_computation | async-start | bytes 3145728 | tf_op jit(solution)/shard_map/all_to_all | solution.py:386
  43.1 3.7 %collective-permute-start.7 = (bf16[48,2176]{1,0:T(8,128)(2,1)S(1)}, bf16[48,2176]{1,0:T(8,128)(2,1)}, u32[]{:S(2)}, u32[]{:S(2)}) collective-permute-start(bf16[48,2176]{1,0:T(8,128)(2,1)S(1)} %copy-done.36), channel_id=1, source_target_pairs={{0,1},{1,0},{2,3},{3,2},{4,5},{5,4},{6,7},{7,6},{8,9},{9,8},{10,11... | collective-permute-start | bytes 626696 | tf_op jit(solution)/shard_map/ppermute | solution.py:356
  43.6 47.0 %collective-permute-start.5 = (bf16[512,768]{1,0:T(8,128)(2,1)}, bf16[512,768]{1,0:T(8,128)(2,1)}, u32[]{:S(2)}, u32[]{:S(2)}) collective-permute-start(bf16[512,768]{1,0:T(8,128)(2,1)} %pad_maximum_fusion), channel_id=1, source_target_pairs={{0,8},{8,0},{16,24},{24,16},{1,9},{9,1},{17,25},{25,17},{2,10},{10... | collective-permute-start | bytes 2359304 | tf_op jit(solution)/shard_map/ppermute | solution.py:356
  45.1 23.2 %collective-permute-start.8 = (bf16[48,2176]{1,0:T(8,128)(2,1)S(1)}, bf16[48,2176]{1,0:T(8,128)(2,1)}, u32[]{:S(2)}, u32[]{:S(2)}) collective-permute-start(bf16[48,2176]{1,0:T(8,128)(2,1)S(1)} %copy-done.35), channel_id=1, source_target_pairs={{0,2},{1,3},{2,0},{3,1},{4,6},{5,7},{6,4},{7,5},{8,10},{9,11},{10,... | collective-permute-start | bytes 626696 | tf_op jit(solution)/shard_map/ppermute | solution.py:356
  46.8 24.9 %collective-permute-start.9 = (bf16[48,2176]{1,0:T(8,128)(2,1)}, bf16[48,2176]{1,0:T(8,128)(2,1)}, u32[]{:S(2)}, u32[]{:S(2)}) collective-permute-start(bf16[48,2176]{1,0:T(8,128)(2,1)} %get-tuple-element.47), channel_id=1, source_target_pairs={{0,3},{1,2},{2,1},{3,0},{4,7},{5,6},{6,5},{7,4},{8,11},{9,10},{10,... | collective-permute-start | bytes 626696 | tf_op jit(solution)/shard_map/ppermute | solution.py:356
  46.8 52.1 %collective-permute-start.15 = (bf16[512,768]{1,0:T(8,128)(2,1)}, bf16[512,768]{1,0:T(8,128)(2,1)S(1)}, u32[]{:S(2)}, u32[]{:S(2)}) collective-permute-start(bf16[512,768]{1,0:T(8,128)(2,1)} %pad_maximum_fusion), channel_id=1, source_target_pairs={{8,16},{16,8},{9,17},{17,9},{10,18},{18,10},{11,19},{19,11},{12,20... | collective-permute-start | bytes 2359304 | tf_op jit(solution)/shard_map/ppermute | solution.py:369
  65.1 33.7 %collective-permute-start.14 = (bf16[512,768]{1,0:T(8,128)(2,1)}, bf16[512,768]{1,0:T(8,128)(2,1)S(1)}, u32[]{:S(2)}, u32[]{:S(2)}) collective-permute-start(bf16[512,768]{1,0:T(8,128)(2,1)} %collective-permute-done.6.refs_1_.refs_4_), channel_id=1, source_target_pairs={{8,0},{16,24},{9,1},{17,25},{10,2},{18,26},{11,3},{19,27},{12,4},{... | collective-permute-start | bytes 2359304 | tf_op jit(solution)/shard_map/ppermute | solution.py:368
  68.3 6.2 %collective-permute-start.10 = (bf16[48,2176]{1,0:T(8,128)(2,1)}, bf16[48,2176]{1,0:T(8,128)(2,1)S(1)}, u32[]{:S(2)}, u32[]{:S(2)}) collective-permute-start(bf16[48,2176]{1,0:T(8,128)(2,1)} %get-tuple-element.48), channel_id=1, source_target_pairs={{0,4},{1,5},{2,6},{3,7},{4,0},{5,1},{6,2},{7,3},{8,12},{9,13},{10,... | collective-permute-start | bytes 626696 | tf_op jit(solution)/shard_map/ppermute | solution.py:356
  71.6 11.4 %collective-permute-start.11 = (bf16[48,2176]{1,0:T(8,128)(2,1)}, bf16[48,2176]{1,0:T(8,128)(2,1)}, u32[]{:S(2)}, u32[]{:S(2)}) collective-permute-start(bf16[48,2176]{1,0:T(8,128)(2,1)} %get-tuple-element.49), channel_id=1, source_target_pairs={{0,5},{1,4},{2,7},{3,6},{4,1},{5,0},{6,3},{7,2},{8,13},{9,12},{10,... | collective-permute-start | bytes 626696 | tf_op jit(solution)/shard_map/ppermute | solution.py:356
  74.6 16.0 %copy-start.31 = (bf16[48,2176]{1,0:T(8,128)(2,1)}, bf16[48,2176]{1,0:T(8,128)(2,1)S(1)}, u32[]{:S(2)}) copy-start(bf16[48,2176]{1,0:T(8,128)(2,1)S(1)} %collective-permute-done.10.refs_6_.refs_9_) | copy-start | bytes 626692
  74.6 11.4 %collective-permute-start.12 = (bf16[48,2176]{1,0:T(8,128)(2,1)}, bf16[48,2176]{1,0:T(8,128)(2,1)S(1)}, u32[]{:S(2)}, u32[]{:S(2)}) collective-permute-start(bf16[48,2176]{1,0:T(8,128)(2,1)} %get-tuple-element.50), channel_id=1, source_target_pairs={{0,6},{1,7},{2,4},{3,5},{4,2},{5,3},{6,0},{7,1},{8,14},{9,15},{10,... | collective-permute-start | bytes 626696 | tf_op jit(solution)/shard_map/ppermute | solution.py:356
  83.1 7.5 %collective-permute-start.13 = (bf16[48,2176]{1,0:T(8,128)(2,1)}, bf16[48,2176]{1,0:T(8,128)(2,1)S(1)}, u32[]{:S(2)}, u32[]{:S(2)}) collective-permute-start(bf16[48,2176]{1,0:T(8,128)(2,1)} %get-tuple-element.51), channel_id=1, source_target_pairs={{0,7},{1,6},{2,5},{3,4},{4,3},{5,2},{6,1},{7,0},{8,15},{9,14},{10,... | collective-permute-start | bytes 626696 | tf_op jit(solution)/shard_map/ppermute | solution.py:356
  102.5 26.1 %collective-permute-start.17 = (bf16[512,512]{1,0:T(8,128)(2,1)}, bf16[512,512]{1,0:T(8,128)(2,1)}, u32[]{:S(2)}, u32[]{:S(2)}) collective-permute-start(bf16[512,512]{1,0:T(8,128)(2,1)} %get-tuple-element.62), channel_id=1, source_target_pairs={{0,8},{24,16},{1,9},{25,17},{2,10},{26,18},{3,11},{27,19},{4,12},{... | collective-permute-start | bytes 1572872 | tf_op jit(solution)/shard_map/ppermute | solution.py:377
  117.3 59.9 %all-to-all-start.1 = ((bf16[8,48,2048]{2,1,0:T(8,128)(2,1)}), bf16[8,48,2048]{2,1,0:T(8,128)(2,1)S(1)}, u32[]{:S(2)}, u32[]{:S(2)}) async-start(bf16[8,48,2048]{2,1,0:T(8,128)(2,1)} %bitcast.31), calls=%async_computation.1 | async-start | bytes 3145728 | tf_op jit(solution)/shard_map/all_to_all | solution.py:386
  121.0 55.2 %copy-start.21 = (bf16[512,256]{1,0:T(8,128)(2,1)S(1)}, bf16[512,256]{1,0:T(8,128)(2,1)}, u32[]{:S(2)}) copy-start(bf16[512,256]{1,0:T(8,128)(2,1)} %copy-done.20) | copy-start | bytes 786436
  121.0 58.5 %collective-permute-start.16 = (bf16[512,512]{1,0:T(8,128)(2,1)}, bf16[512,512]{1,0:T(8,128)(2,1)}, u32[]{:S(2)}, u32[]{:S(2)}) collective-permute-start(bf16[512,512]{1,0:T(8,128)(2,1)} %get-tuple-element.62), channel_id=1, source_target_pairs={{8,16},{16,8},{9,17},{17,9},{10,18},{18,10},{11,19},{19,11},{12,20... | collective-permute-start | bytes 1572872 | tf_op jit(solution)/shard_map/ppermute | solution.py:378
  122.6 16.5 %collective-permute-start.20 = (bf16[512,256]{1,0:T(8,128)(2,1)S(1)}, bf16[512,256]{1,0:T(8,128)(2,1)S(1)}, u32[]{:S(2)}, u32[]{:S(2)}) collective-permute-start(bf16[512,256]{1,0:T(8,128)(2,1)S(1)} %copy-done.23), channel_id=1, source_target_pairs={{8,16},{16,8},{9,17},{17,9},{10,18},{18,10},{11,19},{19,11},{12,20... | collective-permute-start | bytes 786440 | tf_op jit(solution)/shard_map/ppermute | solution.py:378
  123.3 11.8 %collective-permute-start.21 = (bf16[512,256]{1,0:T(8,128)(2,1)S(1)}, bf16[512,256]{1,0:T(8,128)(2,1)S(1)}, u32[]{:S(2)}, u32[]{:S(2)}) collective-permute-start(bf16[512,256]{1,0:T(8,128)(2,1)S(1)} %copy-done.23), channel_id=1, source_target_pairs={{0,8},{24,16},{1,9},{25,17},{2,10},{26,18},{3,11},{27,19},{4,12},{... | collective-permute-start | bytes 786440 | tf_op jit(solution)/shard_map/ppermute | solution.py:377
  128.4 51.1 %collective-permute-start.19 = (bf16[512,512]{1,0:T(8,128)(2,1)}, bf16[512,512]{1,0:T(8,128)(2,1)}, u32[]{:S(2)}, u32[]{:S(2)}) collective-permute-start(bf16[512,512]{1,0:T(8,128)(2,1)} %get-tuple-element.64), channel_id=1, source_target_pairs={{0,8},{8,0},{16,24},{24,16},{1,9},{9,1},{17,25},{25,17},{2,10},{10... | collective-permute-start | bytes 1572872 | tf_op jit(solution)/shard_map/ppermute | solution.py:356
  128.5 31.5 %collective-permute-start.23 = (bf16[512,256]{1,0:T(8,128)(2,1)S(1)}, bf16[512,256]{1,0:T(8,128)(2,1)S(1)}, u32[]{:S(2)}, u32[]{:S(2)}) collective-permute-start(bf16[512,256]{1,0:T(8,128)(2,1)S(1)} %copy-done.25), channel_id=1, source_target_pairs={{0,8},{8,0},{16,24},{24,16},{1,9},{9,1},{17,25},{25,17},{2,10},{10... | collective-permute-start | bytes 786440 | tf_op jit(solution)/shard_map/ppermute | solution.py:356
  135.1 44.5 %collective-permute-start.18 = (bf16[512,512]{1,0:T(8,128)(2,1)}, bf16[512,512]{1,0:T(8,128)(2,1)}, u32[]{:S(2)}, u32[]{:S(2)}) collective-permute-start(bf16[512,512]{1,0:T(8,128)(2,1)} %add_convert_fusion), channel_id=1, source_target_pairs={{0,16},{8,24},{16,0},{24,8},{1,17},{9,25},{17,1},{25,9},{2,18},{10... | collective-permute-start | bytes 1572872 | tf_op jit(solution)/shard_map/ppermute | solution.py:356
  139.1 37.1 %collective-permute-start.22 = (bf16[512,256]{1,0:T(8,128)(2,1)S(1)}, bf16[512,256]{1,0:T(8,128)(2,1)S(1)}, u32[]{:S(2)}, u32[]{:S(2)}) collective-permute-start(bf16[512,256]{1,0:T(8,128)(2,1)S(1)} %add_convert_fusion.1), channel_id=1, source_target_pairs={{0,16},{8,24},{16,0},{24,8},{1,17},{9,25},{17,1},{25,9},{2,18},{10... | collective-permute-start | bytes 786440 | tf_op jit(solution)/shard_map/ppermute | solution.py:356
  (31 other events, 137.5 us)

commit v3 on v2

--- a/solution.py
+++ b/solution.py
@@ -39,10 +39,17 @@
             ],
             scratch_shapes=list(scratch),
             cost_estimate=pl.CostEstimate(flops=flops, bytes_accessed=4_000_000, transcendentals=0),
-            compiler_params=pltpu.CompilerParams(vmem_limit_bytes=48 * 1024 * 1024),
+            compiler_params=pltpu.CompilerParams(vmem_limit_bytes=24 * 1024 * 1024),
         )(*operands)
 
     return call
+
+
+def block_at(i, d, n):
+    if n != 4 or d in (0, 3):
+        return i ^ d
+    inside = ((i >> 1) ^ i) & 1
+    return i ^ (1 + inside if d == 1 else 2 - inside)
 
 
 class Copies:
@@ -66,7 +73,7 @@
     copies = Copies(sems)
     loads = []
     for d in range(groups):
-        source = pl.multiple_of((i_ref[0] ^ d) * part, HD)
+        source = pl.multiple_of(block_at(i_ref[0], d, groups) * part, HD)
         loads.append(
             copies.start(
                 cot_hbm.at[0, :, pl.ds(source, part)], cot_ref.at[:, pl.ds(d * part, part)]
@@ -168,7 +175,7 @@
     put = put_ref[...]
     for d in range(groups):
         at = pl.ds(d * part, part)
-        source = pl.multiple_of((i_ref[0] ^ d) * part, HD)
+        source = pl.multiple_of(block_at(i_ref[0], d, groups) * part, HD)
         send_ref[:, at] = dot(put, normed_ref[:, pl.ds(source, part)], ROWS).astype(BF16)
         started.append(copies.start(send_ref.at[:, at], send_out.at[:, at]))
     started.append(copies.start(normed_ref, normed_out))
@@ -186,36 +193,45 @@
 
 def cot_kernel(me_ref, down_hbm, *refs, groups, pieces, slots):
     got, cots = refs[: groups - 1], refs[groups - 1 : groups - 1 + pieces]
-    out_ref, tag_ref, cot_ref, w_ref, sems = refs[groups - 1 + pieces :]
+    out_ref, tag_hbm, cot_ref, tag_ref, w_ref, sems = refs[groups - 1 + pieces :]
     part, ff = w_ref.shape[1:]
     copies = Copies(sems)
     cot_loads = load_rows(copies, me_ref[0], cots, cot_ref, slots)
     cuts = ([pl.ds(0, ff)], pl.ds(2 * ff, ff))
     loads = load_weights(copies, [down_hbm], got, groups, w_ref, cuts)
-    for copy in cot_loads + [x for load in loads for x in load]:
+    for copy in cot_loads:
+        copy.wait()
+    tag_ref[...] = cot_ref[:, pl.ds(cot_ref.shape[1] - HD, HD)].astype(F32)
+    store = copies.start(tag_ref, tag_hbm)
+    for copy in [x for load in loads for x in load]:
         copy.wait()
     total = dot(cot_ref[:, :part], w_ref[0])
     for d in range(1, groups):
         total = total + dot(cot_ref[:, pl.ds(d * part, part)], w_ref[d])
     out_ref[...] = total
-    tag_ref[...] = cot_ref[:, pl.ds(cot_ref.shape[1] - HD, HD)].astype(F32)
-
-
-def rows_kernel(me_ref, router_ref, tag_ref, rows_ref, gate_hbm, up_hbm, *refs, groups):
+    store.wait()
+
+
+def rows_kernel(me_ref, rows_ref, router_hbm, tag_hbm, gate_hbm, up_hbm, *refs, groups):
     got = refs[: groups - 1]
-    out_ref, share_ref, w_ref, sems = refs[groups - 1 :]
+    out_ref, share_ref, router_ref, tag_ref, w_ref, sems = refs[groups - 1 :]
     part = w_ref.shape[1]
     ff = w_ref.shape[2] // 2
     copies = Copies(sems)
+    router_load = copies.start(router_hbm, router_ref)
     cuts = ([pl.ds(0, ff), pl.ds(ff, ff)], pl.ds(0, 2 * ff))
     loads = load_weights(copies, [gate_hbm, up_hbm], got, groups, w_ref, cuts)
-    for copy in [x for load in loads for x in load]:
-        copy.wait()
-    total = dot(rows_ref[:, :part], w_ref[0])
-    for d in range(1, groups):
-        total = total + dot(rows_ref[:, pl.ds(d * part, part)], w_ref[d])
+    tag_load = copies.start(tag_hbm, tag_ref)
+    router_load.wait()
+    logits = dot(rows_ref[...], router_ref[...], LANES)
+    total = None
+    for d in range(groups):
+        for copy in loads[d]:
+            copy.wait()
+        value = dot(rows_ref[:, pl.ds(d * part, part)], w_ref[d])
+        total = value if total is None else total + value
     out_ref[...] = total
-    logits = dot(rows_ref[...], router_ref[...], LANES)
+    tag_load.wait()
     lanes = lax.broadcasted_iota(jnp.int32, logits.shape, 1)
     me = me_ref[0]
     other = tag_ref[...].astype(jnp.int32)[:, : logits.shape[1]] - me
@@ -314,21 +330,53 @@
     ).astype(BF16)
     part = width // groups
     for d in range(groups):
-        at = pl.ds(pl.multiple_of((i_ref[0] ^ d) * part, HD), part)
+        at = pl.ds(pl.multiple_of(block_at(i_ref[0], d, groups) * part, HD), part)
         value = stream_ref[:, at] + dot(take, back_ref[:, pl.ds(d * part, part)])
         out_ref[0, :, at] = value.astype(BF16)
 
 
-def total_kernel(scale_ref, *refs, outputs):
-    parts, outs = refs[:-outputs], refs[-outputs:]
+def total_kernel(scale_ref, *refs, outputs, parts_n, chunks):
+    parts, outs = refs[:parts_n], refs[parts_n : parts_n + outputs]
+    part_ref, out_ref, sems = refs[parts_n + outputs :]
+    copies = Copies(sems)
+    rows_n = out_ref.shape[0]
+    size = rows_n // chunks
     ff = outs[0].shape[1]
     scale = jnp.where(scale_ref[0] > 0, 1.0, 0.0)
-    for n, out in enumerate(outs):
-        at = pl.ds(n * ff, ff)
-        value = parts[0][:, at].astype(F32)
-        for other in parts[1:]:
-            value = value + other[:, at].astype(F32)
-        out[...] = value * scale
+    loads, stores = [], []
+    for c in range(chunks):
+        at = pl.ds(c * size, size)
+        loads.append([copies.start(x.at[at], part_ref.at[n, at]) for n, x in enumerate(parts)])
+    for c in range(chunks):
+        at = pl.ds(c * size, size)
+        for copy in loads[c]:
+            copy.wait()
+        value = part_ref[0, at].astype(F32)
+        for n in range(1, parts_n):
+            value = value + part_ref[n, at].astype(F32)
+        out_ref[at] = value * scale
+        for n, out in enumerate(outs):
+            stores.append(copies.start(out_ref.at[at, pl.ds(n * ff, ff)], out.at[at]))
+    for copy in stores:
+        copy.wait()
+
+
+def total_call(trainable, parts, outputs):
+    rows_n, columns = parts[0].shape
+    chunks = 4
+    return kernel_call(
+        total_kernel,
+        "sh",
+        [("h", (rows_n, columns // outputs), F32)] * outputs,
+        [
+            pltpu.VMEM((len(parts), rows_n, columns), BF16),
+            pltpu.VMEM((rows_n, columns), F32),
+            pltpu.SemaphoreType.DMA((chunks * (len(parts) + outputs),)),
+        ],
+        outputs=outputs,
+        parts_n=len(parts),
+        chunks=chunks,
+    )(trainable, *parts)
 
 
 def exclusive_prefix(local, axis):
@@ -358,28 +406,31 @@
 
 ENDS = [(0, 1), (3, 2)]
 MIDDLE = [(1, 2), (2, 1)]
-
-
-def gather_xor(x, axis):
+FIRST = [(0, 2), (3, 1), (1, 0), (2, 3)]
+SECOND = [(1, 3), (2, 0), (0, 1), (3, 2)]
+
+
+def gather_line(x, axis):
     n = lax.axis_size(axis)
     if n != 4:
         return [send_xor(x, axis, d) for d in range(1, n)]
-    near, across = send_xor(x, axis, 1), send_xor(x, axis, 2)
-    relayed = lax.ppermute(across, axis, [(b, a) for a, b in ENDS])
+    first = lax.ppermute(x, axis, FIRST)
+    second = lax.ppermute(x, axis, SECOND)
+    relayed = lax.ppermute(first, axis, [(b, a) for a, b in ENDS])
     middle = lax.ppermute(x, axis, MIDDLE)
-    return [near, across, relayed, middle]
-
-
-def scatter_xor(parts, axis):
+    return [first, second, relayed, middle]
+
+
+def scatter_line(parts, axis):
     n = lax.axis_size(axis)
     if n != 4:
         return [parts[0]] + [send_xor(parts[d], axis, d) for d in range(1, n)]
     relayed = lax.ppermute(parts[3], axis, ENDS)
     middle = lax.ppermute(parts[3], axis, MIDDLE)
-    merged = (parts[2].astype(F32) + relayed.astype(F32)).astype(BF16)
-    across = send_xor(merged, axis, 2)
-    near = send_xor(parts[1], axis, 1)
-    return [parts[0], middle, across, near]
+    second = lax.ppermute(parts[2], axis, [(b, a) for a, b in SECOND])
+    merged = (parts[1].astype(F32) + relayed.astype(F32)).astype(BF16)
+    first = lax.ppermute(merged, axis, [(b, a) for a, b in FIRST])
+    return [parts[0], middle, second, first]
 
 
 def exchange(x):
@@ -396,7 +447,7 @@
     n, i = lax.axis_size(axis), lax.axis_index(axis)
     size = x.shape[dim] // n
     return jnp.concatenate(
-        [lax.dynamic_slice_in_dim(x, (i ^ d) * size, size, dim) for d in range(n)], axis=dim
+        [lax.dynamic_slice_in_dim(x, block_at(i, d, n) * size, size, dim) for d in range(n)], axis=dim
     )
 
 
@@ -450,7 +501,7 @@
     else:
         cots = [exchange(cot_send[0].reshape(experts, slots, -1)).reshape(cot_shape)]
 
-    got = gather_xor(jnp.concatenate([w_gate[0], w_up[0], w_down[0]], axis=1), "dp")
+    got = gather_line(jnp.concatenate([w_gate[0], w_up[0], w_down[0]], axis=1), "dp")
 
     (local,) = kernel_call(
         state_kernel,
@@ -493,11 +544,12 @@
     cot_part, tags = kernel_call(
         cot_kernel,
         "sh",
-        [("v", (rows_n, ff), F32), ("v", (rows_n, HD), F32)],
+        [("v", (rows_n, ff), F32), ("h", (rows_n, HD), F32)],
         [
             pltpu.VMEM((rows_n, width + HD), BF16),
+            pltpu.VMEM((rows_n, HD), F32),
             pltpu.VMEM((groups - 1, part, ff), BF16),
-            pltpu.SemaphoreType.DMA((groups + pieces,)),
+            pltpu.SemaphoreType.DMA((groups + 1 + pieces,)),
         ],
         groups=groups - 1,
         pieces=pieces,
@@ -505,14 +557,16 @@
     )(me, w_down, *early, *cots)
     row_part, share = kernel_call(
         rows_kernel,
-        "svvvh",
+        "svh",
         [("v", (rows_n, 2 * ff), F32), ("v", (rows_n, HD), F32)],
         [
+            pltpu.VMEM((experts, width), BF16),
+            pltpu.VMEM((rows_n, HD), F32),
             pltpu.VMEM((groups - 1, part, 2 * ff), BF16),
-            pltpu.SemaphoreType.DMA((groups + 1,)),
+            pltpu.SemaphoreType.DMA((groups + 2,)),
         ],
         groups=groups - 1,
-    )(me, turned, tags, rows, w_gate, w_up, *early)
+    )(me, rows, turned, tags, w_gate, w_up, *early)
     hidden, gated, delta, far_inner, far_down = kernel_call(
         expert_kernel,
         "svvvv" + "v" * len(late) + "h",
@@ -548,19 +602,15 @@
         pieces=pieces,
         slots=slots,
     )(me, hidden, gated, delta, rows, *late, w_down, *early, *cots)
-    down_parts = scatter_xor(terms[0::2] + [far_down], "dp")
-    inner_parts = scatter_xor(terms[1::2] + [far_inner], "dp")
+    down_parts = scatter_line(terms[0::2] + [far_down], "dp")
+    inner_parts = scatter_line(terms[1::2] + [far_inner], "dp")
     back = exchange(expert_out.reshape(peers, slots, width)).reshape(rows_n, width)
     (mixed,) = kernel_call(
         combine_kernel, "sv", [("v", (1, tokens, width), BF16)], groups=groups
     )(i, stream, normed, router.T, expert_ids, slot, back)
     mixed, *inner_parts = lax.optimization_barrier((mixed, *inner_parts))
-    (grad_down,) = kernel_call(
-        total_kernel, "sv", [("v", (part, ff), F32)], outputs=1
-    )(trainable, *down_parts)
-    grad_gate, grad_up = kernel_call(
-        total_kernel, "sv", [("v", (part, ff), F32)] * 2, outputs=2
-    )(trainable, *inner_parts)
+    (grad_down,) = total_call(trainable, down_parts, 1)
+    grad_gate, grad_up = total_call(trainable, inner_parts, 2)
     return (mixed, grad_gate[None], grad_up[None], grad_down[None])
 
 

time: 183 us -> 178 us (0.973)
  waiting for transfers between devices: 76.7 us -> 62 us
  starting transfers between devices: 58.3 us -> 70.6 us
  local copies, waits for them, and re-layouts: 8.36 us -> 5.97 us
    ppermute x13 -> x7, waiting for transfers between devices: 64.7 us -> 34.5 us  [send_xor(): lax.ppermute(x, axis, [(j, j ^ d) for j in range(lax.axis_size(axis))])]
    ppermute x6 -> x12, starting transfers between devices: 14 us -> 42.1 us  [the longest x2 24.8 us: scatter_line(): first = lax.ppermute(merged, axis, [(b, a) for a, b in FIRST])]
    ppermute x13 -> x7, starting transfers between devices: 25.2 us -> 9.3 us  [send_xor(): lax.ppermute(x, axis, [(j, j ^ d) for j in range(lax.axis_size(axis))])]
    ppermute x6 -> x12, waiting for transfers between devices: 2.61 us -> 18.1 us  [the longest x2 15.5 us: scatter_line(): first = lax.ppermute(merged, axis, [(b, a) for a, b in FIRST])]
    unnamed x75 -> x69, local copies, waits for them, and re-layouts: 8.33 us -> 5.94 us
  transfers between devices with their start and end apart: 26 -> 26, of which waited for: 12 -> 11; matrix products, arithmetic and copies ran while one was open for 2% -> 2% of each run, Pallas kernels for 13% -> 14%
where the time goes in v3:
time: 178 us
  starting transfers between devices  70.6 us (40%)
  waiting for transfers between devices  62 us (35%)
  Pallas kernels  31.6 us (18%)
  local copies, waits for them, and re-layouts  5.97 us (3%)
  other arithmetic  5.77 us (3%)
    ppermute x7, waiting for transfers between devices, send_xor(): lax.ppermute(x, axis, [(j, j ^ d) for j in range(lax.axis_size(axis))])  34.5 us
    pallas_call x11, Pallas kernels, call(): pl.pallas_call(functools.partial(body, **static), in_specs=[pl.BlockSpec(...  31.6 us
    ppermute x2, starting transfers between devices, scatter_line(): first = lax.ppermute(merged, axis, [(b, a) for a, b in FIRST])  24.8 us
    ppermute x2, waiting for transfers between devices, scatter_line(): first = lax.ppermute(merged, axis, [(b, a) for a, b in FIRST])  15.5 us
    ppermute x3, starting transfers between devices, exclusive_prefix(): lax.ppermute(total, axis, [(j, j + d) for j in range(n - d)])  10.9 us
    ppermute x7, starting transfers between devices, send_xor(): lax.ppermute(x, axis, [(j, j ^ d) for j in range(lax.axis_size(axis))])  9.3 us
    ppermute x3, waiting for transfers between devices, exclusive_prefix(): lax.ppermute(total, axis, [(j, j + d) for j in range(n - d)])  8.3 us
    all_to_all x2, starting transfers between devices, exchange(): return lax.all_to_all(x, 'seq', split_axis=0, concat_axis=0, tiled=True)  7.73 us
  transfers between devices with their start and end apart: 26, of which 11 were waited for; matrix products, arithmetic and copies ran while one was open for 2% of the time, Pallas kernels for 14%

profile of v3, /device:TPU:0, one launch (start us, length us, event | category | flops | bytes accessed | tf_op | source)
XLA Modules:
  0.0 177.7 jit_solution(15808468536622791850)
XLA Ops:
  0.6 1.9 %shard_map.156 = bf16[16,128,128]{2,1,0:T(8,128)(2,1)S(1)} custom-call(bf16[1,128,2048]{2,1,0:T(8,128)(2,1)} %k_ref.1, bf16[1,128,2048]{2,1,0:T(8,128)(2,1)} %v_ref.1), custom_call_target="tpu_custom_call" | custom-call | flops 1000000000 | bytes 4000000 | tf_op jit(solution)/shard_map/pallas_call | solution.py:32
  4.4 6.4 %collective-permute-start.3 = (bf16[8,128,128]{2,1,0:T(8,128)(2,1)S(1)}, bf16[8,128,128]{2,1,0:T(8,128)(2,1)}, u32[]{:S(2)}, u32[]{:S(2)}) collective-permute-start(bf16[8,128,128]{2,1,0:T(8,128)(2,1)S(1)} %fusion.2), channel_id=1, source_target_pairs={{0,6},{1,7},{8,14},{9,15},{16,22},{17,23},{24,30},{25,31}} | collective-permute-start | bytes 786440 | tf_op jit(solution)/shard_map/ppermute | solution.py:393
  10.9 2.0 %collective-permute-start.2 = (bf16[8,128,128]{2,1,0:T(8,128)(2,1)S(1)}, bf16[8,128,128]{2,1,0:T(8,128)(2,1)}, u32[]{:S(2)}, u32[]{:S(2)}) collective-permute-start(bf16[8,128,128]{2,1,0:T(8,128)(2,1)S(1)} %fusion.2), channel_id=1, source_target_pairs={{0,4},{1,5},{2,6},{3,7},{8,12},{9,13},{10,14},{11,15},{16,20},{17,... | collective-permute-start | bytes 786440 | tf_op jit(solution)/shard_map/ppermute | solution.py:393
  12.8 2.5 %collective-permute-start.1 = (bf16[8,128,128]{2,1,0:T(8,128)(2,1)S(1)}, bf16[8,128,128]{2,1,0:T(8,128)(2,1)}, u32[]{:S(2)}, u32[]{:S(2)}) collective-permute-start(bf16[8,128,128]{2,1,0:T(8,128)(2,1)S(1)} %fusion.2), channel_id=1, source_target_pairs={{0,2},{1,3},{2,4},{3,5},{4,6},{5,7},{8,10},{9,11},{10,12},{11,13},... | collective-permute-start | bytes 786440 | tf_op jit(solution)/shard_map/ppermute | solution.py:393
  16.9 6.7 %collective-permute-done.2 = bf16[8,128,128]{2,1,0:T(8,128)(2,1)} collective-permute-done((bf16[8,128,128]{2,1,0:T(8,128)(2,1)S(1)}, bf16[8,128,128]{2,1,0:T(8,128)(2,1)}, u32[]{:S(2)}, u32[]{:S(2)}) %collective-permute-start.2) | collective-permute-done | bytes 262176 | tf_op jit(solution)/shard_map/ppermute | solution.py:393
  23.6 2.0 %fusion.4 = (bf16[8,128,128]{2,1,0:T(8,128)(2,1)S(1)}, bf16[8,128,128]{2,1,0:T(8,128)(2,1)}) fusion(bf16[8,128,128]{2,1,0:T(8,128)(2,1)S(1)} %collective-permute-done, bf16[8,128,128]{2,1,0:T(8,128)(2,1)} %collective-permute-done.3, bf16[8,128,128]{2,1,0:T(8,128)(2,1)} %collective-permute-done.2, bf16[8,128,128]{2,1,0:T(8,128)(2,1)} %collective-permute-done.1, ...), kind=kLoop, calls=%fused_computation.9 | loop fusion | flops 1703936 | bytes 1835014 | tf_op jit(solution)/shard_map/convert_element_type | solution.py:399
  26.6 2.6 %collective-permute-start.5 = (bf16[512,768]{1,0:T(8,128)(2,1)}, bf16[512,768]{1,0:T(8,128)(2,1)}, u32[]{:S(2)}, u32[]{:S(2)}) collective-permute-start(bf16[512,768]{1,0:T(8,128)(2,1)} %pad_maximum_fusion), channel_id=1, source_target_pairs={{0,16},{24,8},{8,0},{16,24},{1,17},{25,9},{9,1},{17,25},{2,18},{26... | collective-permute-start | bytes 2359304 | tf_op jit(solution)/shard_map/ppermute | solution.py:417
  29.3 2.6 %shard_map.157.intra_ref = f32[128,2048]{1,0:T(8,128)S(1)} custom-call(bf16[1,128,2048]{2,1,0:T(8,128)(2,1)S(1)} %copy-done.12, bf16[1,128,2048]{2,1,0:T(8,128)(2,1)S(1)} %copy-done.10, bf16[1,128,2048]{2,1,0:T(8,128)(2,1)S(1)} %copy-done.11), custom_call_target="tpu_custom_call" | custom-call | flops 1000000000 | bytes 4000000 | tf_op jit(solution)/shard_map/pallas_call | solution.py:32
  32.0 3.6 %shard_map.158 = (bf16[128,384]{1,0:T(8,128)(2,1)S(1)}, s32[128,2]{1,0:T(8,128)S(1)}, bf16[48,2176]{1,0:T(8,128)(2,1)}, bf16[48,2176]{1,0:T(8,128)(2,1)}, bf16[4...) custom-call(s32[1]{0:T(128)} %bitcast.i_ref, ...), custom_call_target="tpu_custom_call" | custom-call | flops 1000000000 | bytes 4000000 | tf_op jit(solution)/shard_map/pallas_call | solution.py:32
  36.4 2.7 %shard_map.159 = (f32[128,2048]{1,0:T(8,128)}, bf16[128,2048]{1,0:T(8,128)(2,1)}, bf16[384,2048]{1,0:T(8,128)(2,1)}) custom-call(s32[1]{0:T(128)} %bitcast.i_ref, bf16[1,128,2048]{2,1,0:T(8,128)(2,1)S(1)} %copy-done.12, bf16[16,128,128]{2,1,0:T(8,128)(2,1)S(1)} %maximum_select_fusion.prefix_ref, f32[128,2048]{1,0:T(8,128)S(1)} %shard_map.157.intra_ref, ...), custom_call_target="tpu_custom_call" | custom-call | flops 1000000000 | bytes 4000000 | tf_op jit(solution)/shard_map/pallas_call | solution.py:32
  39.1 4.0 %all-to-all-start = ((bf16[8,48,2048]{2,1,0:T(8,128)(2,1)}), bf16[8,48,2048]{2,1,0:T(8,128)(2,1)S(1)}, u32[]{:S(2)}, u32[]{:S(2)}) async-start(bf16[8,48,2048]{2,1,0:T(8,128)(2,1)} %bitcast.30), calls=%async_computation | async-start | bytes 3145728 | tf_op jit(solution)/shard_map/all_to_all | solution.py:437
  48.8 19.6 %collective-permute-done.8.refs_4_.refs_7_ = bf16[48,2176]{1,0:T(8,128)(2,1)} collective-permute-done((bf16[48,2176]{1,0:T(8,128)(2,1)S(1)}, bf16[48,2176]{1,0:T(8,128)(2,1)}, u32[]{:S(2)}, u32[]{:S(2)}) %collective-permute-start.8) | collective-permute-done | bytes 208928 | tf_op jit(solution)/shard_map/ppermute | solution.py:404
  69.9 1.9 %collective-permute-done.9.refs_5_.refs_8_ = bf16[48,2176]{1,0:T(8,128)(2,1)} collective-permute-done((bf16[48,2176]{1,0:T(8,128)(2,1)}, bf16[48,2176]{1,0:T(8,128)(2,1)}, u32[]{:S(2)}, u32[]{:S(2)}) %collective-permute-start.9) | collective-permute-done | bytes 208928 | tf_op jit(solution)/shard_map/ppermute | solution.py:404
  74.7 1.9 %collective-permute-start.12 = (bf16[48,2176]{1,0:T(8,128)(2,1)}, bf16[48,2176]{1,0:T(8,128)(2,1)S(1)}, u32[]{:S(2)}, u32[]{:S(2)}) collective-permute-start(bf16[48,2176]{1,0:T(8,128)(2,1)} %get-tuple-element.51), channel_id=1, source_target_pairs={{0,6},{1,7},{2,4},{3,5},{4,2},{5,3},{6,0},{7,1},{8,14},{9,15},{10,... | collective-permute-start | bytes 626696 | tf_op jit(solution)/shard_map/ppermute | solution.py:404
  76.5 6.7 %collective-permute-done.11.refs_7_.refs_10_ = bf16[48,2176]{1,0:T(8,128)(2,1)} collective-permute-done((bf16[48,2176]{1,0:T(8,128)(2,1)}, bf16[48,2176]{1,0:T(8,128)(2,1)}, u32[]{:S(2)}, u32[]{:S(2)}) %collective-permute-start.11) | collective-permute-done | bytes 208928 | tf_op jit(solution)/shard_map/ppermute | solution.py:404
  83.2 2.1 %collective-permute-start.13 = (bf16[48,2176]{1,0:T(8,128)(2,1)}, bf16[48,2176]{1,0:T(8,128)(2,1)S(1)}, u32[]{:S(2)}, u32[]{:S(2)}) collective-permute-start(bf16[48,2176]{1,0:T(8,128)(2,1)} %get-tuple-element.52), channel_id=1, source_target_pairs={{0,7},{1,6},{2,5},{3,4},{4,3},{5,2},{6,1},{7,0},{8,15},{9,14},{10,... | collective-permute-start | bytes 626696 | tf_op jit(solution)/shard_map/ppermute | solution.py:404
  85.9 5.1 %collective-permute-done.13.refs_9_.refs_12_ = bf16[48,2176]{1,0:T(8,128)(2,1)S(1)} collective-permute-done((bf16[48,2176]{1,0:T(8,128)(2,1)}, bf16[48,2176]{1,0:T(8,128)(2,1)S(1)}, u32[]{:S(2)}, u32[]{:S(2)}) %collective-permute-start.13) | collective-permute-done | bytes 208928 | tf_op jit(solution)/shard_map/ppermute | solution.py:404
  91.7 2.3 %shard_map.160 = (f32[384,256]{1,0:T(8,128)S(1)}, f32[384,128]{1,0:T(8,128)}) custom-call(s32[1]{0:T(128)} %bitcast.3.me_ref, bf16[1,512,256]{2,1,0:T(8,128)(2,1)} %refs_2_.1, bf16[512,768]{1,0:T(8,128)(2,1)} %collective-permute-done.5.refs_0_.refs_3_, bf16[512,768]{1,0:T(8,128)(2,1)} %collective-permute-done.6.refs_1_.refs_4_, ...), custom_call_target="tpu_custom_call" | custom-call | flops 1000000000 | bytes 4000000 | tf_op jit(solution)/shard_map/pallas_call | solution.py:32
  94.0 3.2 %shard_map.161 = (f32[384,512]{1,0:T(8,128)S(1)}, f32[384,128]{1,0:T(8,128)S(1)}) custom-call(s32[1]{0:T(128)} %bitcast.3.me_ref, bf16[384,2048]{1,0:T(8,128)(2,1)S(1)} %bitcast.23, bf16[8,2048]{1,0:T(8,128)(2,1)} %pad_maximum_fusion.1.router_hbm, f32[384,128]{1,0:T(8,128)} %get-tuple-element.53.tag_hbm, bf16[1,512,256]{2,1,0:T(8,128)(2,1)} %gate_hbm.1, ...), custom_call_target="tpu_custom_call" | custom-call | flops 1000000000 | bytes 4000000 | tf_op jit(solution)/shard_map/pallas_call | solution.py:32
  97.3 2.9 %shard_map.162 = (bf16[384,256]{1,0:T(8,128)(2,1)S(1)}, bf16[384,256]{1,0:T(8,128)(2,1)S(1)}, bf16[384,512]{1,0:T(8,128)(2,1)S(1)}, bf16[512,512]{1,0:T(8,128)(2,1)}, bf16[512,256]{1,0:T(8,128)(2,1)S(1)}) custom-call(s32[1]{0:T(128)} %bitcast.3.me_ref, f32[384,512]{1,0:T(8,128)S(1)} %get-tuple-element.54.pre_ref, f32[384,256]{1,0:T(8,128)S(1)} %get-tuple-element.55.back_ref, ...), custom_call_target="tpu_custom_call" | custom-call | flops 1000000000 | bytes 4000000 | tf_op jit(solution)/shard_map/pallas_call | solution.py:32
  100.9 2.1 %collective-permute-start.18 = (bf16[512,512]{1,0:T(8,128)(2,1)}, bf16[512,512]{1,0:T(8,128)(2,1)}, u32[]{:S(2)}, u32[]{:S(2)}) collective-permute-start(bf16[512,512]{1,0:T(8,128)(2,1)} %get-tuple-element.62), channel_id=1, source_target_pairs={{0,8},{24,16},{1,9},{25,17},{2,10},{26,18},{3,11},{27,19},{4,12},{... | collective-permute-start | bytes 1572872 | tf_op jit(solution)/shard_map/ppermute | solution.py:428
  103.0 5.7 %shard_map.163 = (bf16[384,2048]{1,0:T(8,128)(2,1)}, bf16[512,256]{1,0:T(8,128)(2,1)S(1)}, bf16[512,512]{1,0:T(8,128)(2,1)S(1)}, bf16[512,256]{1,0:T(8,128)(2,1)...) custom-call(s32[1]{0:T(128)} %bitcast.3.me_ref, ...), custom_call_target="tpu_custom_call" | custom-call | flops 1000000000 | bytes 4000000 | tf_op jit(solution)/shard_map/pallas_call | solution.py:32
  111.8 3.7 %all-to-all-start.1 = ((bf16[8,48,2048]{2,1,0:T(8,128)(2,1)}), bf16[8,48,2048]{2,1,0:T(8,128)(2,1)S(1)}, u32[]{:S(2)}, u32[]{:S(2)}) async-start(bf16[8,48,2048]{2,1,0:T(8,128)(2,1)} %bitcast.31), calls=%async_computation.1 | async-start | bytes 3145728 | tf_op jit(solution)/shard_map/all_to_all | solution.py:437
  117.6 4.9 %collective-permute-start.22 = (bf16[512,256]{1,0:T(8,128)(2,1)S(1)}, bf16[512,256]{1,0:T(8,128)(2,1)S(1)}, u32[]{:S(2)}, u32[]{:S(2)}) collective-permute-start(bf16[512,256]{1,0:T(8,128)(2,1)S(1)} %copy-done.17), channel_id=1, source_target_pairs={{0,8},{24,16},{1,9},{25,17},{2,10},{26,18},{3,11},{27,19},{4,12},{... | collective-permute-start | bytes 786440 | tf_op jit(solution)/shard_map/ppermute | solution.py:428
  123.4 2.7 %collective-permute-start.21 = (bf16[512,256]{1,0:T(8,128)(2,1)S(1)}, bf16[512,256]{1,0:T(8,128)(2,1)S(1)}, u32[]{:S(2)}, u32[]{:S(2)}) collective-permute-start(bf16[512,256]{1,0:T(8,128)(2,1)S(1)} %copy-done.19), channel_id=1, source_target_pairs={{24,8},{0,16},{8,0},{16,24},{25,9},{1,17},{9,1},{17,25},{26,10},{2... | collective-permute-start | bytes 786440 | tf_op jit(solution)/shard_map/ppermute | solution.py:430
  126.1 2.0 %add_convert_fusion = bf16[512,512]{1,0:T(8,128)(2,1)} fusion(bf16[512,512]{1,0:T(8,128)(2,1)} %collective-permute-done.18, bf16[512,512]{1,0:T(8,128)(2,1)S(1)} %copy-done.2), kind=kLoop, calls=%fused_computation | loop fusion | flops 1048576 | bytes 1572864 | tf_op jit(solution)/shard_map/convert_element_type | solution.py:431
  129.2 2.5 %collective-permute-start.19 = (bf16[512,512]{1,0:T(8,128)(2,1)}, bf16[512,512]{1,0:T(8,128)(2,1)}, u32[]{:S(2)}, u32[]{:S(2)}) collective-permute-start(bf16[512,512]{1,0:T(8,128)(2,1)} %add_convert_fusion), channel_id=1, source_target_pairs={{16,0},{8,24},{0,8},{24,16},{17,1},{9,25},{1,9},{25,17},{18,2},{10... | collective-permute-start | bytes 1572872 | tf_op jit(solution)/shard_map/ppermute | solution.py:432
  131.8 22.3 %collective-permute-start.23 = (bf16[512,256]{1,0:T(8,128)(2,1)S(1)}, bf16[512,256]{1,0:T(8,128)(2,1)S(1)}, u32[]{:S(2)}, u32[]{:S(2)}) collective-permute-start(bf16[512,256]{1,0:T(8,128)(2,1)S(1)} %add_convert_fusion.1), channel_id=1, source_target_pairs={{16,0},{8,24},{0,8},{24,16},{17,1},{9,25},{1,9},{25,17},{18,2},{10... | collective-permute-start | bytes 786440 | tf_op jit(solution)/shard_map/ppermute | solution.py:432
  154.8 15.5 %collective-permute-done.23.refs_3_ = bf16[512,256]{1,0:T(8,128)(2,1)S(1)} collective-permute-done((bf16[512,256]{1,0:T(8,128)(2,1)S(1)}, bf16[512,256]{1,0:T(8,128)(2,1)S(1)}, u32[]{:S(2)}, u32[]{:S(2)}) %collective-permute-start.23) | collective-permute-done | bytes 262176 | tf_op jit(solution)/shard_map/ppermute | solution.py:432
  171.0 2.2 %shard_map.166 = f32[512,256]{1,0:T(8,128)} custom-call(s32[1]{0:T(128)S(6)} %copy.19.scale_ref, bf16[512,256]{1,0:T(8,128)(2,1)} %copy-done.15, bf16[512,256]{1,0:T(8,128)(2,1)} %copy-done.29, bf16[512,256]{1,0:T(8,128)(2,1)} %copy-done.30, bf16[512,256]{1,0:T(8,128)(2,1)} %copy-done.31), custom_call_target="tpu_custom_call" | custom-call | flops 1000000000 | bytes 4000000 | tf_op jit(solution)/shard_map/pallas_call | solution.py:32
  173.3 1.8 %shard_map.164 = bf16[1,128,2048]{2,1,0:T(8,128)(2,1)} custom-call(s32[1]{0:T(128)} %bitcast.i_ref, f32[128,2048]{1,0:T(8,128)S(1)} %copy-done, bf16[128,2048]{1,0:T(8,128)(2,1)S(1)} %copy-done.3, bf16[8,2048]{1,0:T(8,128)(2,1)S(1)} %bitcast.27, s32[1,128,2]{2,1,0:T(8,128)S(1)} %copy-done.5, s32[128,2]{1,0:T(8,128)S(1)} %copy-done.9, ...), custom_call_target="tpu_custom_call" | custom-call | flops 1000000000 | bytes 4000000 | tf_op jit(solution)/shard_map/pallas_call | solution.py:32
  175.1 2.6 %shard_map.165 = (f32[512,256]{1,0:T(8,128)}, f32[512,256]{1,0:T(8,128)}) custom-call(s32[1]{0:T(128)S(6)} %copy.19.scale_ref, bf16[512,512]{1,0:T(8,128)(2,1)} %copy-done.14, bf16[512,512]{1,0:T(8,128)(2,1)} %collective-permute-done.16.refs_1_, bf16[512,512]{1,0:T(8,128)(2,1)} %collective-permute-done.17.refs_2_, ...), custom_call_target="tpu_custom_call" | custom-call | flops 1000000000 | bytes 4000000 | tf_op jit(solution)/shard_map/pallas_call | solution.py:32
  (109 shorter events, 25.2 us)
Async XLA Ops:
  2.6 23.1 %copy-start.22 = (bf16[1,512,256]{2,1,0:T(8,128)(2,1)S(1)}, bf16[1,512,256]{2,1,0:T(8,128)(2,1)}, u32[]{:S(2)}) copy-start(bf16[1,512,256]{2,1,0:T(8,128)(2,1)} %up_hbm.1) | copy-start | bytes 786436
  2.6 23.1 %copy-start.23 = (bf16[1,512,256]{2,1,0:T(8,128)(2,1)S(1)}, bf16[1,512,256]{2,1,0:T(8,128)(2,1)}, u32[]{:S(2)}) copy-start(bf16[1,512,256]{2,1,0:T(8,128)(2,1)} %gate_hbm.1) | copy-start | bytes 786436
  2.6 23.1 %copy-start.24 = (bf16[1,512,256]{2,1,0:T(8,128)(2,1)S(1)}, bf16[1,512,256]{2,1,0:T(8,128)(2,1)}, u32[]{:S(2)}) copy-start(bf16[1,512,256]{2,1,0:T(8,128)(2,1)} %refs_2_.1) | copy-start | bytes 786436
  2.6 1.7 collective-permute-start
  4.4 12.4 %collective-permute-start.3 = (bf16[8,128,128]{2,1,0:T(8,128)(2,1)S(1)}, bf16[8,128,128]{2,1,0:T(8,128)(2,1)}, u32[]{:S(2)}, u32[]{:S(2)}) collective-permute-start(bf16[8,128,128]{2,1,0:T(8,128)(2,1)S(1)} %fusion.2), channel_id=1, source_target_pairs={{0,6},{1,7},{8,14},{9,15},{16,22},{17,23},{24,30},{25,31}} | collective-permute-start | bytes 786440 | tf_op jit(solution)/shard_map/ppermute | solution.py:393
  10.9 12.8 %collective-permute-start.2 = (bf16[8,128,128]{2,1,0:T(8,128)(2,1)S(1)}, bf16[8,128,128]{2,1,0:T(8,128)(2,1)}, u32[]{:S(2)}, u32[]{:S(2)}) collective-permute-start(bf16[8,128,128]{2,1,0:T(8,128)(2,1)S(1)} %fusion.2), channel_id=1, source_target_pairs={{0,4},{1,5},{2,6},{3,7},{8,12},{9,13},{10,14},{11,15},{16,20},{17,... | collective-permute-start | bytes 786440 | tf_op jit(solution)/shard_map/ppermute | solution.py:393
  12.8 10.8 %collective-permute-start.1 = (bf16[8,128,128]{2,1,0:T(8,128)(2,1)S(1)}, bf16[8,128,128]{2,1,0:T(8,128)(2,1)}, u32[]{:S(2)}, u32[]{:S(2)}) collective-permute-start(bf16[8,128,128]{2,1,0:T(8,128)(2,1)S(1)} %fusion.2), channel_id=1, source_target_pairs={{0,2},{1,3},{2,4},{3,5},{4,6},{5,7},{8,10},{9,11},{10,12},{11,13},... | collective-permute-start | bytes 786440 | tf_op jit(solution)/shard_map/ppermute | solution.py:393
  25.7 10.6 %collective-permute-start.4 = (bf16[8,128,128]{2,1,0:T(8,128)(2,1)}, bf16[8,128,128]{2,1,0:T(8,128)(2,1)S(1)}, u32[]{:S(2)}, u32[]{:S(2)}) collective-permute-start(bf16[8,128,128]{2,1,0:T(8,128)(2,1)} %get-tuple-element.77), channel_id=1, source_target_pairs={{0,1},{1,0},{2,3},{3,2},{4,5},{5,4},{6,7},{7,6},{8,9},{9,8},{10,11... | collective-permute-start | bytes 786440 | tf_op jit(solution)/shard_map/ppermute | solution.py:398
  26.6 20.9 %collective-permute-start.5 = (bf16[512,768]{1,0:T(8,128)(2,1)}, bf16[512,768]{1,0:T(8,128)(2,1)}, u32[]{:S(2)}, u32[]{:S(2)}) collective-permute-start(bf16[512,768]{1,0:T(8,128)(2,1)} %pad_maximum_fusion), channel_id=1, source_target_pairs={{0,16},{24,8},{8,0},{16,24},{1,17},{25,9},{9,1},{17,25},{2,18},{26... | collective-permute-start | bytes 2359304 | tf_op jit(solution)/shard_map/ppermute | solution.py:417
  39.1 34.3 %copy-start.6 = (bf16[2048,8]{0,1:T(8,128)(2,1)S(1)}, bf16[2048,8]{0,1:T(8,128)(2,1)}, u32[]{:S(2)}) copy-start(bf16[2048,8]{0,1:T(8,128)(2,1)} %param.19) | copy-start | bytes 98308
  39.1 54.9 %all-to-all-start = ((bf16[8,48,2048]{2,1,0:T(8,128)(2,1)}), bf16[8,48,2048]{2,1,0:T(8,128)(2,1)S(1)}, u32[]{:S(2)}, u32[]{:S(2)}) async-start(bf16[8,48,2048]{2,1,0:T(8,128)(2,1)} %bitcast.30), calls=%async_computation | async-start | bytes 3145728 | tf_op jit(solution)/shard_map/all_to_all | solution.py:437
  43.2 2.2 %collective-permute-start.7 = (bf16[48,2176]{1,0:T(8,128)(2,1)S(1)}, bf16[48,2176]{1,0:T(8,128)(2,1)}, u32[]{:S(2)}, u32[]{:S(2)}) collective-permute-start(bf16[48,2176]{1,0:T(8,128)(2,1)S(1)} %copy-done.33), channel_id=1, source_target_pairs={{0,1},{1,0},{2,3},{3,2},{4,5},{5,4},{6,7},{7,6},{8,9},{9,8},{10,11... | collective-permute-start | bytes 626696 | tf_op jit(solution)/shard_map/ppermute | solution.py:404
  43.7 47.4 %collective-permute-start.6 = (bf16[512,768]{1,0:T(8,128)(2,1)}, bf16[512,768]{1,0:T(8,128)(2,1)}, u32[]{:S(2)}, u32[]{:S(2)}) collective-permute-start(bf16[512,768]{1,0:T(8,128)(2,1)} %pad_maximum_fusion), channel_id=1, source_target_pairs={{8,24},{16,0},{0,8},{24,16},{9,25},{17,1},{1,9},{25,17},{10,26},{1... | collective-permute-start | bytes 2359304 | tf_op jit(solution)/shard_map/ppermute | solution.py:418
  43.7 24.7 %collective-permute-start.8 = (bf16[48,2176]{1,0:T(8,128)(2,1)S(1)}, bf16[48,2176]{1,0:T(8,128)(2,1)}, u32[]{:S(2)}, u32[]{:S(2)}) collective-permute-start(bf16[48,2176]{1,0:T(8,128)(2,1)S(1)} %copy-done.32), channel_id=1, source_target_pairs={{0,2},{1,3},{2,0},{3,1},{4,6},{5,7},{6,4},{7,5},{8,10},{9,11},{10,... | collective-permute-start | bytes 626696 | tf_op jit(solution)/shard_map/ppermute | solution.py:404
  45.3 26.4 %collective-permute-start.9 = (bf16[48,2176]{1,0:T(8,128)(2,1)}, bf16[48,2176]{1,0:T(8,128)(2,1)}, u32[]{:S(2)}, u32[]{:S(2)}) collective-permute-start(bf16[48,2176]{1,0:T(8,128)(2,1)} %get-tuple-element.48), channel_id=1, source_target_pairs={{0,3},{1,2},{2,1},{3,0},{4,7},{5,6},{6,5},{7,4},{8,11},{9,10},{10,... | collective-permute-start | bytes 626696 | tf_op jit(solution)/shard_map/ppermute | solution.py:404
  45.4 51.9 %collective-permute-start.15 = (bf16[512,768]{1,0:T(8,128)(2,1)}, bf16[512,768]{1,0:T(8,128)(2,1)S(1)}, u32[]{:S(2)}, u32[]{:S(2)}) collective-permute-start(bf16[512,768]{1,0:T(8,128)(2,1)} %pad_maximum_fusion), channel_id=1, source_target_pairs={{8,16},{16,8},{9,17},{17,9},{10,18},{18,10},{11,19},{19,11},{12,20... | collective-permute-start | bytes 2359304 | tf_op jit(solution)/shard_map/ppermute | solution.py:420
  47.5 49.8 %collective-permute-start.14 = (bf16[512,768]{1,0:T(8,128)(2,1)}, bf16[512,768]{1,0:T(8,128)(2,1)S(1)}, u32[]{:S(2)}, u32[]{:S(2)}) collective-permute-start(bf16[512,768]{1,0:T(8,128)(2,1)} %collective-permute-done.5.refs_0_.refs_3_), channel_id=1, source_target_pairs={{8,0},{16,24},{9,1},{17,25},{10,2},{18,26},{11,3},{19,27},{12,4},{... | collective-permute-start | bytes 2359304 | tf_op jit(solution)/shard_map/ppermute | solution.py:419
  68.4 6.2 %collective-permute-start.10 = (bf16[48,2176]{1,0:T(8,128)(2,1)}, bf16[48,2176]{1,0:T(8,128)(2,1)S(1)}, u32[]{:S(2)}, u32[]{:S(2)}) collective-permute-start(bf16[48,2176]{1,0:T(8,128)(2,1)} %get-tuple-element.49), channel_id=1, source_target_pairs={{0,4},{1,5},{2,6},{3,7},{4,0},{5,1},{6,2},{7,3},{8,12},{9,13},{10,... | collective-permute-start | bytes 626696 | tf_op jit(solution)/shard_map/ppermute | solution.py:404
  71.7 11.5 %collective-permute-start.11 = (bf16[48,2176]{1,0:T(8,128)(2,1)}, bf16[48,2176]{1,0:T(8,128)(2,1)}, u32[]{:S(2)}, u32[]{:S(2)}) collective-permute-start(bf16[48,2176]{1,0:T(8,128)(2,1)} %get-tuple-element.50), channel_id=1, source_target_pairs={{0,5},{1,4},{2,7},{3,6},{4,1},{5,0},{6,3},{7,2},{8,13},{9,12},{10,... | collective-permute-start | bytes 626696 | tf_op jit(solution)/shard_map/ppermute | solution.py:404
  74.6 16.4 %copy-start.25 = (bf16[48,2176]{1,0:T(8,128)(2,1)}, bf16[48,2176]{1,0:T(8,128)(2,1)S(1)}, u32[]{:S(2)}) copy-start(bf16[48,2176]{1,0:T(8,128)(2,1)S(1)} %collective-permute-done.10.refs_6_.refs_9_) | copy-start | bytes 626692
  74.7 11.3 %collective-permute-start.12 = (bf16[48,2176]{1,0:T(8,128)(2,1)}, bf16[48,2176]{1,0:T(8,128)(2,1)S(1)}, u32[]{:S(2)}, u32[]{:S(2)}) collective-permute-start(bf16[48,2176]{1,0:T(8,128)(2,1)} %get-tuple-element.51), channel_id=1, source_target_pairs={{0,6},{1,7},{2,4},{3,5},{4,2},{5,3},{6,0},{7,1},{8,14},{9,15},{10,... | collective-permute-start | bytes 626696 | tf_op jit(solution)/shard_map/ppermute | solution.py:404
  83.2 7.8 %collective-permute-start.13 = (bf16[48,2176]{1,0:T(8,128)(2,1)}, bf16[48,2176]{1,0:T(8,128)(2,1)S(1)}, u32[]{:S(2)}, u32[]{:S(2)}) collective-permute-start(bf16[48,2176]{1,0:T(8,128)(2,1)} %get-tuple-element.52), channel_id=1, source_target_pairs={{0,7},{1,6},{2,5},{3,4},{4,3},{5,2},{6,1},{7,0},{8,15},{9,14},{10,... | collective-permute-start | bytes 626696 | tf_op jit(solution)/shard_map/ppermute | solution.py:404
  100.9 22.6 %collective-permute-start.18 = (bf16[512,512]{1,0:T(8,128)(2,1)}, bf16[512,512]{1,0:T(8,128)(2,1)}, u32[]{:S(2)}, u32[]{:S(2)}) collective-permute-start(bf16[512,512]{1,0:T(8,128)(2,1)} %get-tuple-element.62), channel_id=1, source_target_pairs={{0,8},{24,16},{1,9},{25,17},{2,10},{26,18},{3,11},{27,19},{4,12},{... | collective-permute-start | bytes 1572872 | tf_op jit(solution)/shard_map/ppermute | solution.py:428
  111.8 61.5 %all-to-all-start.1 = ((bf16[8,48,2048]{2,1,0:T(8,128)(2,1)}), bf16[8,48,2048]{2,1,0:T(8,128)(2,1)S(1)}, u32[]{:S(2)}, u32[]{:S(2)}) async-start(bf16[8,48,2048]{2,1,0:T(8,128)(2,1)} %bitcast.31), calls=%async_computation.1 | async-start | bytes 3145728 | tf_op jit(solution)/shard_map/all_to_all | solution.py:437
  115.5 59.6 %collective-permute-start.16 = (bf16[512,512]{1,0:T(8,128)(2,1)}, bf16[512,512]{1,0:T(8,128)(2,1)}, u32[]{:S(2)}, u32[]{:S(2)}) collective-permute-start(bf16[512,512]{1,0:T(8,128)(2,1)} %get-tuple-element.62), channel_id=1, source_target_pairs={{8,16},{16,8},{9,17},{17,9},{10,18},{18,10},{11,19},{19,11},{12,20... | collective-permute-start | bytes 1572872 | tf_op jit(solution)/shard_map/ppermute | solution.py:429
  116.9 14.8 %collective-permute-start.20 = (bf16[512,256]{1,0:T(8,128)(2,1)S(1)}, bf16[512,256]{1,0:T(8,128)(2,1)S(1)}, u32[]{:S(2)}, u32[]{:S(2)}) collective-permute-start(bf16[512,256]{1,0:T(8,128)(2,1)S(1)} %copy-done.17), channel_id=1, source_target_pairs={{8,16},{16,8},{9,17},{17,9},{10,18},{18,10},{11,19},{19,11},{12,20... | collective-permute-start | bytes 786440 | tf_op jit(solution)/shard_map/ppermute | solution.py:429
  117.6 11.6 %collective-permute-start.22 = (bf16[512,256]{1,0:T(8,128)(2,1)S(1)}, bf16[512,256]{1,0:T(8,128)(2,1)S(1)}, u32[]{:S(2)}, u32[]{:S(2)}) collective-permute-start(bf16[512,256]{1,0:T(8,128)(2,1)S(1)} %copy-done.17), channel_id=1, source_target_pairs={{0,8},{24,16},{1,9},{25,17},{2,10},{26,18},{3,11},{27,19},{4,12},{... | collective-permute-start | bytes 786440 | tf_op jit(solution)/shard_map/ppermute | solution.py:428
  122.6 52.5 %collective-permute-start.17 = (bf16[512,512]{1,0:T(8,128)(2,1)}, bf16[512,512]{1,0:T(8,128)(2,1)}, u32[]{:S(2)}, u32[]{:S(2)}) collective-permute-start(bf16[512,512]{1,0:T(8,128)(2,1)} %get-tuple-element.63), channel_id=1, source_target_pairs={{24,8},{0,16},{8,0},{16,24},{25,9},{1,17},{9,1},{17,25},{26,10},{2... | collective-permute-start | bytes 1572872 | tf_op jit(solution)/shard_map/ppermute | solution.py:430
  123.4 31.4 %collective-permute-start.21 = (bf16[512,256]{1,0:T(8,128)(2,1)S(1)}, bf16[512,256]{1,0:T(8,128)(2,1)S(1)}, u32[]{:S(2)}, u32[]{:S(2)}) collective-permute-start(bf16[512,256]{1,0:T(8,128)(2,1)S(1)} %copy-done.19), channel_id=1, source_target_pairs={{24,8},{0,16},{8,0},{16,24},{25,9},{1,17},{9,1},{17,25},{26,10},{2... | collective-permute-start | bytes 786440 | tf_op jit(solution)/shard_map/ppermute | solution.py:430
  129.2 45.9 %collective-permute-start.19 = (bf16[512,512]{1,0:T(8,128)(2,1)}, bf16[512,512]{1,0:T(8,128)(2,1)}, u32[]{:S(2)}, u32[]{:S(2)}) collective-permute-start(bf16[512,512]{1,0:T(8,128)(2,1)} %add_convert_fusion), channel_id=1, source_target_pairs={{16,0},{8,24},{0,8},{24,16},{17,1},{9,25},{1,9},{25,17},{18,2},{10... | collective-permute-start | bytes 1572872 | tf_op jit(solution)/shard_map/ppermute | solution.py:432
  131.8 38.5 %copy-start.29 = (bf16[512,256]{1,0:T(8,128)(2,1)}, bf16[512,256]{1,0:T(8,128)(2,1)S(1)}, u32[]{:S(2)}) copy-start(bf16[512,256]{1,0:T(8,128)(2,1)S(1)} %collective-permute-done.20.refs_1_) | copy-start | bytes 786436
  131.8 38.5 %collective-permute-start.23 = (bf16[512,256]{1,0:T(8,128)(2,1)S(1)}, bf16[512,256]{1,0:T(8,128)(2,1)S(1)}, u32[]{:S(2)}, u32[]{:S(2)}) collective-permute-start(bf16[512,256]{1,0:T(8,128)(2,1)S(1)} %add_convert_fusion.1), channel_id=1, source_target_pairs={{16,0},{8,24},{0,8},{24,16},{17,1},{9,25},{1,9},{25,17},{18,2},{10... | collective-permute-start | bytes 786440 | tf_op jit(solution)/shard_map/ppermute | solution.py:432
  (28 other events, 149.2 us)

commit v4 on v3

--- a/solution.py
+++ b/solution.py
@@ -167,19 +167,19 @@
         stream = residual_ref[0, :, at].astype(F32) + attended * attn_ref[:, at]
         stream_ref[:, at] = stream
         squares = squares + stream * stream
+    started.append(copies.start(stream_ref, stream_out))
     scale = lax.rsqrt(jnp.sum(squares, axis=-1, keepdims=True) / width + 1e-06)
     part = width // groups
     for h in range(heads):
         at = pl.ds(h * HD, HD)
         normed_ref[:, at] = (stream_ref[:, at] * scale * moe_ref[:, at]).astype(BF16)
     put = put_ref[...]
+    started.append(copies.start(normed_ref, normed_out))
     for d in range(groups):
         at = pl.ds(d * part, part)
         source = pl.multiple_of(block_at(i_ref[0], d, groups) * part, HD)
         send_ref[:, at] = dot(put, normed_ref[:, pl.ds(source, part)], ROWS).astype(BF16)
         started.append(copies.start(send_ref.at[:, at], send_out.at[:, at]))
-    started.append(copies.start(normed_ref, normed_out))
-    started.append(copies.start(stream_ref, stream_out))
     for copy in started:
         copy.wait()
 
@@ -388,11 +388,16 @@
     swap = [(j, j ^ 1) for j in range(n)]
     peer = lax.ppermute(other, axis, swap).astype(F32)
     mine = mine.astype(F32)
-    total = (mine + peer).astype(BF16)
+    total = mine + peer
     before = jnp.zeros_like(mine)
-    far = [lax.ppermute(total, axis, [(j, j + d) for j in range(n - d)]) for d in range(2, n, 2)]
-    for got in far:
-        before = before + got.astype(F32)
+    step = 2
+    while step < n:
+        last = 2 * step >= n
+        pairs = [(j, j ^ step) for j in range(n) if not (last and j & step)]
+        got = lax.ppermute(total.astype(BF16), axis, pairs).astype(F32)
+        before = before + jnp.where((i & step) != 0, got, 0.0)
+        total = total + got
+        step *= 2
     own = before + jnp.where(core == 1, peer, 0.0)
     theirs = before + jnp.where(core == 0, mine, 0.0)
     back = lax.ppermute(theirs.astype(BF16), axis, swap)
@@ -438,9 +443,11 @@
 
 
 def exchange_pieces(blocks):
-    return [blocks[0]] + [
-        send_xor(blocks[k], "seq", k) for k in range(len(blocks) - 1, 0, -1)
-    ][::-1]
+    n = len(blocks)
+    got = [blocks[0]]
+    for k in range(1, n):
+        got.append(send_xor(blocks[k], "seq", k))
+    return got
 
 
 def swap_blocks(x, axis, dim):

time: 178 us -> 179 us (level)
  starting transfers between devices: 70.6 us -> 67.3 us
  waiting for transfers between devices: 62 us -> 65.2 us
    ppermute x3 -> x2, starting transfers between devices: 10.9 us -> 7.29 us  [exclusive_prefix(): got = lax.ppermute(total.astype(BF16), axis, pairs).astype(F32)]
    ppermute x3 -> x2, waiting for transfers between devices: 8.3 us -> 10.9 us  [exclusive_prefix(): got = lax.ppermute(total.astype(BF16), axis, pairs).astype(F32)]
    unnamed x69 -> x67, local copies, waits for them, and re-layouts: 5.94 us -> 5.9 us
  transfers between devices with their start and end apart: 26 -> 25, of which waited for: 11 -> 11; matrix products, arithmetic and copies ran while one was open for 2% -> 3% of each run, Pallas kernels for 14% -> 13%
where the time goes in v4:
time: 179 us; the launch traced here: 178 us
  starting transfers between devices  67.3 us (38%)
  waiting for transfers between devices  65.2 us (36%)
  Pallas kernels  31.2 us (17%)
  other arithmetic  6.67 us (4%)
  local copies, waits for them, and re-layouts  5.93 us (3%)
    ppermute x7, waiting for transfers between devices, send_xor(): lax.ppermute(x, axis, [(j, j ^ d) for j in range(lax.axis_size(axis))])  35.7 us
    pallas_call x11, Pallas kernels, call(): pl.pallas_call(functools.partial(body, **static), in_specs=[pl.BlockSpec(...  31.2 us
    ppermute x2, starting transfers between devices, scatter_line(): first = lax.ppermute(merged, axis, [(b, a) for a, b in FIRST])  24.8 us
    ppermute x2, waiting for transfers between devices, scatter_line(): first = lax.ppermute(merged, axis, [(b, a) for a, b in FIRST])  15.5 us
    ppermute x2, waiting for transfers between devices, exclusive_prefix(): got = lax.ppermute(total.astype(BF16), axis, pairs).astype(F32)  10.9 us
    ppermute x7, starting transfers between devices, send_xor(): lax.ppermute(x, axis, [(j, j ^ d) for j in range(lax.axis_size(axis))])  8.72 us
    all_to_all x2, starting transfers between devices, exchange(): return lax.all_to_all(x, 'seq', split_axis=0, concat_axis=0, tiled=True)  8.64 us
    ppermute x2, starting transfers between devices, exclusive_prefix(): got = lax.ppermute(total.astype(BF16), axis, pairs).astype(F32)  7.29 us
  transfers between devices with their start and end apart: 25, of which 11 were waited for; matrix products, arithmetic and copies ran while one was open for 3% of the time, Pallas kernels for 13%

profile of v4, /device:TPU:0, one launch (start us, length us, event | category | flops | bytes accessed | tf_op | source)
XLA Modules:
  0.0 178.1 jit_solution(18353071960115378994)
XLA Ops:
  0.6 1.9 %shard_map.156 = bf16[16,128,128]{2,1,0:T(8,128)(2,1)S(1)} custom-call(bf16[1,128,2048]{2,1,0:T(8,128)(2,1)} %k_ref.1, bf16[1,128,2048]{2,1,0:T(8,128)(2,1)} %v_ref.1), custom_call_target="tpu_custom_call" | custom-call | flops 1000000000 | bytes 4000000 | tf_op jit(solution)/shard_map/pallas_call | solution.py:32
  4.4 2.9 %collective-permute-start.1 = (bf16[8,128,128]{2,1,0:T(8,128)(2,1)S(1)}, bf16[8,128,128]{2,1,0:T(8,128)(2,1)S(1)}, u32[]{:S(2)}, u32[]{:S(2)}) collective-permute-start(bf16[8,128,128]{2,1,0:T(8,128)(2,1)S(1)} %fusion.6), channel_id=1, source_target_pairs={{0,2},{1,3},{2,0},{3,1},{4,6},{5,7},{6,4},{7,5},{8,10},{9,11},{10,... | collective-permute-start | bytes 786440 | tf_op jit(solution)/shard_map/ppermute | solution.py:397
  7.3 6.6 %collective-permute-done.1 = bf16[8,128,128]{2,1,0:T(8,128)(2,1)S(1)} collective-permute-done((bf16[8,128,128]{2,1,0:T(8,128)(2,1)S(1)}, bf16[8,128,128]{2,1,0:T(8,128)(2,1)S(1)}, u32[]{:S(2)}, u32[]{:S(2)}) %collective-permute-start.1) | collective-permute-done | bytes 262176 | tf_op jit(solution)/shard_map/ppermute | solution.py:397
  14.0 4.4 %collective-permute-start.2 = (bf16[8,128,128]{2,1,0:T(8,128)(2,1)S(1)}, bf16[8,128,128]{2,1,0:T(8,128)(2,1)}, u32[]{:S(2)}, u32[]{:S(2)}) collective-permute-start(bf16[8,128,128]{2,1,0:T(8,128)(2,1)S(1)} %fusion.5), channel_id=1, source_target_pairs={{0,4},{1,5},{2,6},{3,7},{8,12},{9,13},{10,14},{11,15},{16,20},{17,... | collective-permute-start | bytes 786440 | tf_op jit(solution)/shard_map/ppermute | solution.py:397
  18.4 4.3 %collective-permute-done.2 = bf16[8,128,128]{2,1,0:T(8,128)(2,1)} collective-permute-done((bf16[8,128,128]{2,1,0:T(8,128)(2,1)S(1)}, bf16[8,128,128]{2,1,0:T(8,128)(2,1)}, u32[]{:S(2)}, u32[]{:S(2)}) %collective-permute-start.2) | collective-permute-done | bytes 262176 | tf_op jit(solution)/shard_map/ppermute | solution.py:397
  22.7 1.9 %fusion.3 = (bf16[8,128,128]{2,1,0:T(8,128)(2,1)S(1)}, bf16[8,128,128]{2,1,0:T(8,128)(2,1)}) fusion(bf16[8,128,128]{2,1,0:T(8,128)(2,1)S(1)} %collective-permute-done, bf16[8,128,128]{2,1,0:T(8,128)(2,1)} %collective-permute-done.2, bf16[8,128,128]{2,1,0:T(8,128)(2,1)S(1)} %collective-permute-done.1, pred[]{:T(512)S(6)} %eq.10, pred[]{:T(512)S(6)} %ne.14, ...), kind=kLoop, calls=%fused_computation.10 | loop fusion | flops 1703936 | bytes 1572872 | tf_op jit(solution)/shard_map/convert_element_type | solution.py:404
  24.6 1.9 %pad_maximum_fusion = bf16[512,768]{1,0:T(8,128)(2,1)} fusion(bf16[512,256]{1,0:T(8,128)(2,1)} %bitcast.34, bf16[512,256]{1,0:T(8,128)(2,1)S(1)} %bitcast.32, bf16[512,256]{1,0:T(8,128)(2,1)S(1)} %bitcast.33), kind=kLoop, calls=%fused_computation.1 | loop fusion | flops 2359296 | bytes 1572864 | tf_op jit(solution)/shard_map/concatenate | solution.py:511
  26.5 2.6 %collective-permute-start.4 = (bf16[512,768]{1,0:T(8,128)(2,1)}, bf16[512,768]{1,0:T(8,128)(2,1)}, u32[]{:S(2)}, u32[]{:S(2)}) collective-permute-start(bf16[512,768]{1,0:T(8,128)(2,1)} %pad_maximum_fusion), channel_id=1, source_target_pairs={{0,16},{24,8},{8,0},{16,24},{1,17},{25,9},{9,1},{17,25},{2,18},{26... | collective-permute-start | bytes 2359304 | tf_op jit(solution)/shard_map/ppermute | solution.py:422
  29.2 2.6 %shard_map.157.intra_ref = f32[128,2048]{1,0:T(8,128)S(1)} custom-call(bf16[1,128,2048]{2,1,0:T(8,128)(2,1)S(1)} %copy-done.12, bf16[1,128,2048]{2,1,0:T(8,128)(2,1)S(1)} %copy-done.10, bf16[1,128,2048]{2,1,0:T(8,128)(2,1)S(1)} %copy-done.11), custom_call_target="tpu_custom_call" | custom-call | flops 1000000000 | bytes 4000000 | tf_op jit(solution)/shard_map/pallas_call | solution.py:32
  31.9 3.6 %shard_map.158 = (bf16[128,384]{1,0:T(8,128)(2,1)S(1)}, s32[128,2]{1,0:T(8,128)S(1)}, bf16[48,2176]{1,0:T(8,128)(2,1)}, bf16[48,2176]{1,0:T(8,128)(2,1)}, bf16[4...) custom-call(s32[1]{0:T(128)} %bitcast.i_ref, ...), custom_call_target="tpu_custom_call" | custom-call | flops 1000000000 | bytes 4000000 | tf_op jit(solution)/shard_map/pallas_call | solution.py:32
  36.2 2.4 %shard_map.159 = (f32[128,2048]{1,0:T(8,128)}, bf16[128,2048]{1,0:T(8,128)(2,1)}, bf16[384,2048]{1,0:T(8,128)(2,1)}) custom-call(s32[1]{0:T(128)} %bitcast.i_ref, bf16[1,128,2048]{2,1,0:T(8,128)(2,1)S(1)} %copy-done.12, bf16[16,128,128]{2,1,0:T(8,128)(2,1)S(1)} %maximum_select_fusion.prefix_ref, f32[128,2048]{1,0:T(8,128)S(1)} %shard_map.157.intra_ref, ...), custom_call_target="tpu_custom_call" | custom-call | flops 1000000000 | bytes 4000000 | tf_op jit(solution)/shard_map/pallas_call | solution.py:32
  38.6 4.9 %all-to-all-start = ((bf16[8,48,2048]{2,1,0:T(8,128)(2,1)}), bf16[8,48,2048]{2,1,0:T(8,128)(2,1)S(1)}, u32[]{:S(2)}, u32[]{:S(2)}) async-start(bf16[8,48,2048]{2,1,0:T(8,128)(2,1)} %bitcast.30), calls=%async_computation | async-start | bytes 3145728 | tf_op jit(solution)/shard_map/all_to_all | solution.py:442
  48.6 20.2 %collective-permute-done.7.refs_4_.refs_7_ = bf16[48,2176]{1,0:T(8,128)(2,1)} collective-permute-done((bf16[48,2176]{1,0:T(8,128)(2,1)S(1)}, bf16[48,2176]{1,0:T(8,128)(2,1)}, u32[]{:S(2)}, u32[]{:S(2)}) %collective-permute-start.7) | collective-permute-done | bytes 208928 | tf_op jit(solution)/shard_map/ppermute | solution.py:409
  70.3 1.9 %collective-permute-done.8.refs_5_.refs_8_ = bf16[48,2176]{1,0:T(8,128)(2,1)} collective-permute-done((bf16[48,2176]{1,0:T(8,128)(2,1)}, bf16[48,2176]{1,0:T(8,128)(2,1)}, u32[]{:S(2)}, u32[]{:S(2)}) %collective-permute-start.8) | collective-permute-done | bytes 208928 | tf_op jit(solution)/shard_map/ppermute | solution.py:409
  76.6 7.1 %collective-permute-done.10.refs_7_.refs_10_ = bf16[48,2176]{1,0:T(8,128)(2,1)} collective-permute-done((bf16[48,2176]{1,0:T(8,128)(2,1)}, bf16[48,2176]{1,0:T(8,128)(2,1)}, u32[]{:S(2)}, u32[]{:S(2)}) %collective-permute-start.10) | collective-permute-done | bytes 208928 | tf_op jit(solution)/shard_map/ppermute | solution.py:409
  83.6 1.9 %collective-permute-start.12 = (bf16[48,2176]{1,0:T(8,128)(2,1)}, bf16[48,2176]{1,0:T(8,128)(2,1)S(1)}, u32[]{:S(2)}, u32[]{:S(2)}) collective-permute-start(bf16[48,2176]{1,0:T(8,128)(2,1)} %get-tuple-element.52), channel_id=1, source_target_pairs={{0,7},{1,6},{2,5},{3,4},{4,3},{5,2},{6,1},{7,0},{8,15},{9,14},{10,... | collective-permute-start | bytes 626696 | tf_op jit(solution)/shard_map/ppermute | solution.py:409
  86.1 5.3 %collective-permute-done.12.refs_9_.refs_12_ = bf16[48,2176]{1,0:T(8,128)(2,1)S(1)} collective-permute-done((bf16[48,2176]{1,0:T(8,128)(2,1)}, bf16[48,2176]{1,0:T(8,128)(2,1)S(1)}, u32[]{:S(2)}, u32[]{:S(2)}) %collective-permute-start.12) | collective-permute-done | bytes 208928 | tf_op jit(solution)/shard_map/ppermute | solution.py:409
  92.1 2.3 %shard_map.160 = (f32[384,256]{1,0:T(8,128)S(1)}, f32[384,128]{1,0:T(8,128)}) custom-call(s32[1]{0:T(128)} %bitcast.3.me_ref, bf16[1,512,256]{2,1,0:T(8,128)(2,1)} %refs_2_.1, bf16[512,768]{1,0:T(8,128)(2,1)} %collective-permute-done.4.refs_0_.refs_3_, bf16[512,768]{1,0:T(8,128)(2,1)} %collective-permute-done.5.refs_1_.refs_4_, ...), custom_call_target="tpu_custom_call" | custom-call | flops 1000000000 | bytes 4000000 | tf_op jit(solution)/shard_map/pallas_call | solution.py:32
  94.5 3.2 %shard_map.161 = (f32[384,512]{1,0:T(8,128)S(1)}, f32[384,128]{1,0:T(8,128)S(1)}) custom-call(s32[1]{0:T(128)} %bitcast.3.me_ref, bf16[384,2048]{1,0:T(8,128)(2,1)S(1)} %bitcast.23, bf16[8,2048]{1,0:T(8,128)(2,1)} %pad_maximum_fusion.1.router_hbm, f32[384,128]{1,0:T(8,128)} %get-tuple-element.53.tag_hbm, bf16[1,512,256]{2,1,0:T(8,128)(2,1)} %gate_hbm.1, ...), custom_call_target="tpu_custom_call" | custom-call | flops 1000000000 | bytes 4000000 | tf_op jit(solution)/shard_map/pallas_call | solution.py:32
  97.7 2.9 %shard_map.162 = (bf16[384,256]{1,0:T(8,128)(2,1)S(1)}, bf16[384,256]{1,0:T(8,128)(2,1)S(1)}, bf16[384,512]{1,0:T(8,128)(2,1)S(1)}, bf16[512,512]{1,0:T(8,128)(2,1)}, bf16[512,256]{1,0:T(8,128)(2,1)S(1)}) custom-call(s32[1]{0:T(128)} %bitcast.3.me_ref, f32[384,512]{1,0:T(8,128)S(1)} %get-tuple-element.54.pre_ref, f32[384,256]{1,0:T(8,128)S(1)} %get-tuple-element.55.back_ref, ...), custom_call_target="tpu_custom_call" | custom-call | flops 1000000000 | bytes 4000000 | tf_op jit(solution)/shard_map/pallas_call | solution.py:32
  101.3 2.1 %collective-permute-start.17 = (bf16[512,512]{1,0:T(8,128)(2,1)}, bf16[512,512]{1,0:T(8,128)(2,1)}, u32[]{:S(2)}, u32[]{:S(2)}) collective-permute-start(bf16[512,512]{1,0:T(8,128)(2,1)} %get-tuple-element.62), channel_id=1, source_target_pairs={{0,8},{24,16},{1,9},{25,17},{2,10},{26,18},{3,11},{27,19},{4,12},{... | collective-permute-start | bytes 1572872 | tf_op jit(solution)/shard_map/ppermute | solution.py:433
  103.4 5.7 %shard_map.163 = (bf16[384,2048]{1,0:T(8,128)(2,1)}, bf16[512,256]{1,0:T(8,128)(2,1)S(1)}, bf16[512,512]{1,0:T(8,128)(2,1)S(1)}, bf16[512,256]{1,0:T(8,128)(2,1)...) custom-call(s32[1]{0:T(128)} %bitcast.3.me_ref, ...), custom_call_target="tpu_custom_call" | custom-call | flops 1000000000 | bytes 4000000 | tf_op jit(solution)/shard_map/pallas_call | solution.py:32
  112.1 3.7 %all-to-all-start.1 = ((bf16[8,48,2048]{2,1,0:T(8,128)(2,1)}), bf16[8,48,2048]{2,1,0:T(8,128)(2,1)S(1)}, u32[]{:S(2)}, u32[]{:S(2)}) async-start(bf16[8,48,2048]{2,1,0:T(8,128)(2,1)} %bitcast.31), calls=%async_computation.1 | async-start | bytes 3145728 | tf_op jit(solution)/shard_map/all_to_all | solution.py:442
  118.0 4.9 %collective-permute-start.21 = (bf16[512,256]{1,0:T(8,128)(2,1)S(1)}, bf16[512,256]{1,0:T(8,128)(2,1)S(1)}, u32[]{:S(2)}, u32[]{:S(2)}) collective-permute-start(bf16[512,256]{1,0:T(8,128)(2,1)S(1)} %copy-done.17), channel_id=1, source_target_pairs={{0,8},{24,16},{1,9},{25,17},{2,10},{26,18},{3,11},{27,19},{4,12},{... | collective-permute-start | bytes 786440 | tf_op jit(solution)/shard_map/ppermute | solution.py:433
  123.8 2.7 %collective-permute-start.20 = (bf16[512,256]{1,0:T(8,128)(2,1)S(1)}, bf16[512,256]{1,0:T(8,128)(2,1)S(1)}, u32[]{:S(2)}, u32[]{:S(2)}) collective-permute-start(bf16[512,256]{1,0:T(8,128)(2,1)S(1)} %copy-done.19), channel_id=1, source_target_pairs={{24,8},{0,16},{8,0},{16,24},{25,9},{1,17},{9,1},{17,25},{26,10},{2... | collective-permute-start | bytes 786440 | tf_op jit(solution)/shard_map/ppermute | solution.py:435
  126.5 2.0 %add_convert_fusion = bf16[512,512]{1,0:T(8,128)(2,1)} fusion(bf16[512,512]{1,0:T(8,128)(2,1)} %collective-permute-done.17, bf16[512,512]{1,0:T(8,128)(2,1)S(1)} %copy-done.2), kind=kLoop, calls=%fused_computation | loop fusion | flops 1048576 | bytes 1572864 | tf_op jit(solution)/shard_map/convert_element_type | solution.py:436
  129.6 2.5 %collective-permute-start.18 = (bf16[512,512]{1,0:T(8,128)(2,1)}, bf16[512,512]{1,0:T(8,128)(2,1)}, u32[]{:S(2)}, u32[]{:S(2)}) collective-permute-start(bf16[512,512]{1,0:T(8,128)(2,1)} %add_convert_fusion), channel_id=1, source_target_pairs={{16,0},{8,24},{0,8},{24,16},{17,1},{9,25},{1,9},{25,17},{18,2},{10... | collective-permute-start | bytes 1572872 | tf_op jit(solution)/shard_map/ppermute | solution.py:437
  132.2 22.3 %collective-permute-start.22 = (bf16[512,256]{1,0:T(8,128)(2,1)S(1)}, bf16[512,256]{1,0:T(8,128)(2,1)S(1)}, u32[]{:S(2)}, u32[]{:S(2)}) collective-permute-start(bf16[512,256]{1,0:T(8,128)(2,1)S(1)} %add_convert_fusion.1), channel_id=1, source_target_pairs={{16,0},{8,24},{0,8},{24,16},{17,1},{9,25},{1,9},{25,17},{18,2},{10... | collective-permute-start | bytes 786440 | tf_op jit(solution)/shard_map/ppermute | solution.py:437
  155.2 15.5 %collective-permute-done.22.refs_3_ = bf16[512,256]{1,0:T(8,128)(2,1)S(1)} collective-permute-done((bf16[512,256]{1,0:T(8,128)(2,1)S(1)}, bf16[512,256]{1,0:T(8,128)(2,1)S(1)}, u32[]{:S(2)}, u32[]{:S(2)}) %collective-permute-start.22) | collective-permute-done | bytes 262176 | tf_op jit(solution)/shard_map/ppermute | solution.py:437
  171.4 2.2 %shard_map.166 = f32[512,256]{1,0:T(8,128)} custom-call(s32[1]{0:T(128)S(6)} %copy.19.scale_ref, bf16[512,256]{1,0:T(8,128)(2,1)} %copy-done.15, bf16[512,256]{1,0:T(8,128)(2,1)} %copy-done.28, bf16[512,256]{1,0:T(8,128)(2,1)} %copy-done.29, bf16[512,256]{1,0:T(8,128)(2,1)} %copy-done.30), custom_call_target="tpu_custom_call" | custom-call | flops 1000000000 | bytes 4000000 | tf_op jit(solution)/shard_map/pallas_call | solution.py:32
  173.7 1.8 %shard_map.164 = bf16[1,128,2048]{2,1,0:T(8,128)(2,1)} custom-call(s32[1]{0:T(128)} %bitcast.i_ref, f32[128,2048]{1,0:T(8,128)S(1)} %copy-done, bf16[128,2048]{1,0:T(8,128)(2,1)S(1)} %copy-done.3, bf16[8,2048]{1,0:T(8,128)(2,1)S(1)} %bitcast.27, s32[1,128,2]{2,1,0:T(8,128)S(1)} %copy-done.5, s32[128,2]{1,0:T(8,128)S(1)} %copy-done.9, ...), custom_call_target="tpu_custom_call" | custom-call | flops 1000000000 | bytes 4000000 | tf_op jit(solution)/shard_map/pallas_call | solution.py:32
  175.5 2.6 %shard_map.165 = (f32[512,256]{1,0:T(8,128)}, f32[512,256]{1,0:T(8,128)}) custom-call(s32[1]{0:T(128)S(6)} %copy.19.scale_ref, bf16[512,512]{1,0:T(8,128)(2,1)} %copy-done.14, bf16[512,512]{1,0:T(8,128)(2,1)} %collective-permute-done.15.refs_1_, bf16[512,512]{1,0:T(8,128)(2,1)} %collective-permute-done.16.refs_2_, ...), custom_call_target="tpu_custom_call" | custom-call | flops 1000000000 | bytes 4000000 | tf_op jit(solution)/shard_map/pallas_call | solution.py:32
  (106 shorter events, 23.7 us)
Async XLA Ops:
  2.6 1.7 collective-permute-start
  3.2 21.4 %copy-start.22 = (bf16[1,512,256]{2,1,0:T(8,128)(2,1)S(1)}, bf16[1,512,256]{2,1,0:T(8,128)(2,1)}, u32[]{:S(2)}) copy-start(bf16[1,512,256]{2,1,0:T(8,128)(2,1)} %up_hbm.1) | copy-start | bytes 786436
  3.2 21.4 %copy-start.23 = (bf16[1,512,256]{2,1,0:T(8,128)(2,1)S(1)}, bf16[1,512,256]{2,1,0:T(8,128)(2,1)}, u32[]{:S(2)}) copy-start(bf16[1,512,256]{2,1,0:T(8,128)(2,1)} %gate_hbm.1) | copy-start | bytes 786436
  4.4 9.5 %collective-permute-start.1 = (bf16[8,128,128]{2,1,0:T(8,128)(2,1)S(1)}, bf16[8,128,128]{2,1,0:T(8,128)(2,1)S(1)}, u32[]{:S(2)}, u32[]{:S(2)}) collective-permute-start(bf16[8,128,128]{2,1,0:T(8,128)(2,1)S(1)} %fusion.6), channel_id=1, source_target_pairs={{0,2},{1,3},{2,0},{3,1},{4,6},{5,7},{6,4},{7,5},{8,10},{9,11},{10,... | collective-permute-start | bytes 786440 | tf_op jit(solution)/shard_map/ppermute | solution.py:397
  14.0 8.7 %collective-permute-start.2 = (bf16[8,128,128]{2,1,0:T(8,128)(2,1)S(1)}, bf16[8,128,128]{2,1,0:T(8,128)(2,1)}, u32[]{:S(2)}, u32[]{:S(2)}) collective-permute-start(bf16[8,128,128]{2,1,0:T(8,128)(2,1)S(1)} %fusion.5), channel_id=1, source_target_pairs={{0,4},{1,5},{2,6},{3,7},{8,12},{9,13},{10,14},{11,15},{16,20},{17,... | collective-permute-start | bytes 786440 | tf_op jit(solution)/shard_map/ppermute | solution.py:397
  24.6 11.5 %collective-permute-start.3 = (bf16[8,128,128]{2,1,0:T(8,128)(2,1)}, bf16[8,128,128]{2,1,0:T(8,128)(2,1)S(1)}, u32[]{:S(2)}, u32[]{:S(2)}) collective-permute-start(bf16[8,128,128]{2,1,0:T(8,128)(2,1)} %get-tuple-element.77), channel_id=1, source_target_pairs={{0,1},{1,0},{2,3},{3,2},{4,5},{5,4},{6,7},{7,6},{8,9},{9,8},{10,11... | collective-permute-start | bytes 786440 | tf_op jit(solution)/shard_map/ppermute | solution.py:403
  26.5 20.8 %collective-permute-start.4 = (bf16[512,768]{1,0:T(8,128)(2,1)}, bf16[512,768]{1,0:T(8,128)(2,1)}, u32[]{:S(2)}, u32[]{:S(2)}) collective-permute-start(bf16[512,768]{1,0:T(8,128)(2,1)} %pad_maximum_fusion), channel_id=1, source_target_pairs={{0,16},{24,8},{8,0},{16,24},{1,17},{25,9},{9,1},{17,25},{2,18},{26... | collective-permute-start | bytes 2359304 | tf_op jit(solution)/shard_map/ppermute | solution.py:422
  38.6 35.2 %copy-start.6 = (bf16[2048,8]{0,1:T(8,128)(2,1)S(1)}, bf16[2048,8]{0,1:T(8,128)(2,1)}, u32[]{:S(2)}) copy-start(bf16[2048,8]{0,1:T(8,128)(2,1)} %param.19) | copy-start | bytes 98308
  38.6 55.8 %all-to-all-start = ((bf16[8,48,2048]{2,1,0:T(8,128)(2,1)}), bf16[8,48,2048]{2,1,0:T(8,128)(2,1)S(1)}, u32[]{:S(2)}, u32[]{:S(2)}) async-start(bf16[8,48,2048]{2,1,0:T(8,128)(2,1)} %bitcast.30), calls=%async_computation | async-start | bytes 3145728 | tf_op jit(solution)/shard_map/all_to_all | solution.py:442
  43.6 2.2 %collective-permute-start.6 = (bf16[48,2176]{1,0:T(8,128)(2,1)S(1)}, bf16[48,2176]{1,0:T(8,128)(2,1)}, u32[]{:S(2)}, u32[]{:S(2)}) collective-permute-start(bf16[48,2176]{1,0:T(8,128)(2,1)S(1)} %copy-done.32), channel_id=1, source_target_pairs={{0,1},{1,0},{2,3},{3,2},{4,5},{5,4},{6,7},{7,6},{8,9},{9,8},{10,11... | collective-permute-start | bytes 626696 | tf_op jit(solution)/shard_map/ppermute | solution.py:409
  44.1 47.4 %collective-permute-start.5 = (bf16[512,768]{1,0:T(8,128)(2,1)}, bf16[512,768]{1,0:T(8,128)(2,1)}, u32[]{:S(2)}, u32[]{:S(2)}) collective-permute-start(bf16[512,768]{1,0:T(8,128)(2,1)} %pad_maximum_fusion), channel_id=1, source_target_pairs={{8,24},{16,0},{0,8},{24,16},{9,25},{17,1},{1,9},{25,17},{10,26},{1... | collective-permute-start | bytes 2359304 | tf_op jit(solution)/shard_map/ppermute | solution.py:423
  44.1 24.7 %collective-permute-start.7 = (bf16[48,2176]{1,0:T(8,128)(2,1)S(1)}, bf16[48,2176]{1,0:T(8,128)(2,1)}, u32[]{:S(2)}, u32[]{:S(2)}) collective-permute-start(bf16[48,2176]{1,0:T(8,128)(2,1)S(1)} %copy-done.31), channel_id=1, source_target_pairs={{0,2},{1,3},{2,0},{3,1},{4,6},{5,7},{6,4},{7,5},{8,10},{9,11},{10,... | collective-permute-start | bytes 626696 | tf_op jit(solution)/shard_map/ppermute | solution.py:409
  45.7 26.4 %collective-permute-start.8 = (bf16[48,2176]{1,0:T(8,128)(2,1)}, bf16[48,2176]{1,0:T(8,128)(2,1)}, u32[]{:S(2)}, u32[]{:S(2)}) collective-permute-start(bf16[48,2176]{1,0:T(8,128)(2,1)} %get-tuple-element.48), channel_id=1, source_target_pairs={{0,3},{1,2},{2,1},{3,0},{4,7},{5,6},{6,5},{7,4},{8,11},{9,10},{10,... | collective-permute-start | bytes 626696 | tf_op jit(solution)/shard_map/ppermute | solution.py:409
  45.8 51.9 %collective-permute-start.14 = (bf16[512,768]{1,0:T(8,128)(2,1)}, bf16[512,768]{1,0:T(8,128)(2,1)S(1)}, u32[]{:S(2)}, u32[]{:S(2)}) collective-permute-start(bf16[512,768]{1,0:T(8,128)(2,1)} %pad_maximum_fusion), channel_id=1, source_target_pairs={{8,16},{16,8},{9,17},{17,9},{10,18},{18,10},{11,19},{19,11},{12,20... | collective-permute-start | bytes 2359304 | tf_op jit(solution)/shard_map/ppermute | solution.py:425
  47.3 50.3 %collective-permute-start.13 = (bf16[512,768]{1,0:T(8,128)(2,1)}, bf16[512,768]{1,0:T(8,128)(2,1)S(1)}, u32[]{:S(2)}, u32[]{:S(2)}) collective-permute-start(bf16[512,768]{1,0:T(8,128)(2,1)} %collective-permute-done.4.refs_0_.refs_3_), channel_id=1, source_target_pairs={{8,0},{16,24},{9,1},{17,25},{10,2},{18,26},{11,3},{19,27},{12,4},{... | collective-permute-start | bytes 2359304 | tf_op jit(solution)/shard_map/ppermute | solution.py:424
  68.8 6.2 %collective-permute-start.9 = (bf16[48,2176]{1,0:T(8,128)(2,1)}, bf16[48,2176]{1,0:T(8,128)(2,1)S(1)}, u32[]{:S(2)}, u32[]{:S(2)}) collective-permute-start(bf16[48,2176]{1,0:T(8,128)(2,1)} %get-tuple-element.49), channel_id=1, source_target_pairs={{0,4},{1,5},{2,6},{3,7},{4,0},{5,1},{6,2},{7,3},{8,12},{9,13},{10,... | collective-permute-start | bytes 626696 | tf_op jit(solution)/shard_map/ppermute | solution.py:409
  72.1 11.5 %collective-permute-start.10 = (bf16[48,2176]{1,0:T(8,128)(2,1)}, bf16[48,2176]{1,0:T(8,128)(2,1)}, u32[]{:S(2)}, u32[]{:S(2)}) collective-permute-start(bf16[48,2176]{1,0:T(8,128)(2,1)} %get-tuple-element.50), channel_id=1, source_target_pairs={{0,5},{1,4},{2,7},{3,6},{4,1},{5,0},{6,3},{7,2},{8,13},{9,12},{10,... | collective-permute-start | bytes 626696 | tf_op jit(solution)/shard_map/ppermute | solution.py:409
  75.1 16.4 %copy-start.24 = (bf16[48,2176]{1,0:T(8,128)(2,1)}, bf16[48,2176]{1,0:T(8,128)(2,1)S(1)}, u32[]{:S(2)}) copy-start(bf16[48,2176]{1,0:T(8,128)(2,1)S(1)} %collective-permute-done.9.refs_6_.refs_9_) | copy-start | bytes 626692
  75.1 11.1 %collective-permute-start.11 = (bf16[48,2176]{1,0:T(8,128)(2,1)}, bf16[48,2176]{1,0:T(8,128)(2,1)S(1)}, u32[]{:S(2)}, u32[]{:S(2)}) collective-permute-start(bf16[48,2176]{1,0:T(8,128)(2,1)} %get-tuple-element.51), channel_id=1, source_target_pairs={{0,6},{1,7},{2,4},{3,5},{4,2},{5,3},{6,0},{7,1},{8,14},{9,15},{10,... | collective-permute-start | bytes 626696 | tf_op jit(solution)/shard_map/ppermute | solution.py:409
  83.6 7.8 %collective-permute-start.12 = (bf16[48,2176]{1,0:T(8,128)(2,1)}, bf16[48,2176]{1,0:T(8,128)(2,1)S(1)}, u32[]{:S(2)}, u32[]{:S(2)}) collective-permute-start(bf16[48,2176]{1,0:T(8,128)(2,1)} %get-tuple-element.52), channel_id=1, source_target_pairs={{0,7},{1,6},{2,5},{3,4},{4,3},{5,2},{6,1},{7,0},{8,15},{9,14},{10,... | collective-permute-start | bytes 626696 | tf_op jit(solution)/shard_map/ppermute | solution.py:409
  101.3 22.6 %collective-permute-start.17 = (bf16[512,512]{1,0:T(8,128)(2,1)}, bf16[512,512]{1,0:T(8,128)(2,1)}, u32[]{:S(2)}, u32[]{:S(2)}) collective-permute-start(bf16[512,512]{1,0:T(8,128)(2,1)} %get-tuple-element.62), channel_id=1, source_target_pairs={{0,8},{24,16},{1,9},{25,17},{2,10},{26,18},{3,11},{27,19},{4,12},{... | collective-permute-start | bytes 1572872 | tf_op jit(solution)/shard_map/ppermute | solution.py:433
  112.1 14.3 %copy-start.2 = (bf16[512,512]{1,0:T(8,128)(2,1)S(1)}, bf16[512,512]{1,0:T(8,128)(2,1)}, u32[]{:S(2)}) copy-start(bf16[512,512]{1,0:T(8,128)(2,1)} %copy-done.1) | copy-start | bytes 1572868
  112.1 61.5 %all-to-all-start.1 = ((bf16[8,48,2048]{2,1,0:T(8,128)(2,1)}), bf16[8,48,2048]{2,1,0:T(8,128)(2,1)S(1)}, u32[]{:S(2)}, u32[]{:S(2)}) async-start(bf16[8,48,2048]{2,1,0:T(8,128)(2,1)} %bitcast.31), calls=%async_computation.1 | async-start | bytes 3145728 | tf_op jit(solution)/shard_map/all_to_all | solution.py:442
  115.9 59.6 %collective-permute-start.15 = (bf16[512,512]{1,0:T(8,128)(2,1)}, bf16[512,512]{1,0:T(8,128)(2,1)}, u32[]{:S(2)}, u32[]{:S(2)}) collective-permute-start(bf16[512,512]{1,0:T(8,128)(2,1)} %get-tuple-element.62), channel_id=1, source_target_pairs={{8,16},{16,8},{9,17},{17,9},{10,18},{18,10},{11,19},{19,11},{12,20... | collective-permute-start | bytes 1572872 | tf_op jit(solution)/shard_map/ppermute | solution.py:434
  117.3 14.8 %collective-permute-start.19 = (bf16[512,256]{1,0:T(8,128)(2,1)S(1)}, bf16[512,256]{1,0:T(8,128)(2,1)S(1)}, u32[]{:S(2)}, u32[]{:S(2)}) collective-permute-start(bf16[512,256]{1,0:T(8,128)(2,1)S(1)} %copy-done.17), channel_id=1, source_target_pairs={{8,16},{16,8},{9,17},{17,9},{10,18},{18,10},{11,19},{19,11},{12,20... | collective-permute-start | bytes 786440 | tf_op jit(solution)/shard_map/ppermute | solution.py:434
  118.0 11.6 %collective-permute-start.21 = (bf16[512,256]{1,0:T(8,128)(2,1)S(1)}, bf16[512,256]{1,0:T(8,128)(2,1)S(1)}, u32[]{:S(2)}, u32[]{:S(2)}) collective-permute-start(bf16[512,256]{1,0:T(8,128)(2,1)S(1)} %copy-done.17), channel_id=1, source_target_pairs={{0,8},{24,16},{1,9},{25,17},{2,10},{26,18},{3,11},{27,19},{4,12},{... | collective-permute-start | bytes 786440 | tf_op jit(solution)/shard_map/ppermute | solution.py:433
  123.0 52.5 %collective-permute-start.16 = (bf16[512,512]{1,0:T(8,128)(2,1)}, bf16[512,512]{1,0:T(8,128)(2,1)}, u32[]{:S(2)}, u32[]{:S(2)}) collective-permute-start(bf16[512,512]{1,0:T(8,128)(2,1)} %get-tuple-element.63), channel_id=1, source_target_pairs={{24,8},{0,16},{8,0},{16,24},{25,9},{1,17},{9,1},{17,25},{26,10},{2... | collective-permute-start | bytes 1572872 | tf_op jit(solution)/shard_map/ppermute | solution.py:435
  123.8 31.4 %collective-permute-start.20 = (bf16[512,256]{1,0:T(8,128)(2,1)S(1)}, bf16[512,256]{1,0:T(8,128)(2,1)S(1)}, u32[]{:S(2)}, u32[]{:S(2)}) collective-permute-start(bf16[512,256]{1,0:T(8,128)(2,1)S(1)} %copy-done.19), channel_id=1, source_target_pairs={{24,8},{0,16},{8,0},{16,24},{25,9},{1,17},{9,1},{17,25},{26,10},{2... | collective-permute-start | bytes 786440 | tf_op jit(solution)/shard_map/ppermute | solution.py:435
  129.6 45.9 %collective-permute-start.18 = (bf16[512,512]{1,0:T(8,128)(2,1)}, bf16[512,512]{1,0:T(8,128)(2,1)}, u32[]{:S(2)}, u32[]{:S(2)}) collective-permute-start(bf16[512,512]{1,0:T(8,128)(2,1)} %add_convert_fusion), channel_id=1, source_target_pairs={{16,0},{8,24},{0,8},{24,16},{17,1},{9,25},{1,9},{25,17},{18,2},{10... | collective-permute-start | bytes 1572872 | tf_op jit(solution)/shard_map/ppermute | solution.py:437
  132.2 38.5 %copy-start.28 = (bf16[512,256]{1,0:T(8,128)(2,1)}, bf16[512,256]{1,0:T(8,128)(2,1)S(1)}, u32[]{:S(2)}) copy-start(bf16[512,256]{1,0:T(8,128)(2,1)S(1)} %collective-permute-done.19.refs_1_) | copy-start | bytes 786436
  132.2 38.5 %collective-permute-start.22 = (bf16[512,256]{1,0:T(8,128)(2,1)S(1)}, bf16[512,256]{1,0:T(8,128)(2,1)S(1)}, u32[]{:S(2)}, u32[]{:S(2)}) collective-permute-start(bf16[512,256]{1,0:T(8,128)(2,1)S(1)} %add_convert_fusion.1), channel_id=1, source_target_pairs={{16,0},{8,24},{0,8},{24,16},{17,1},{9,25},{1,9},{25,17},{18,2},{10... | collective-permute-start | bytes 786440 | tf_op jit(solution)/shard_map/ppermute | solution.py:437
  155.2 15.5 %copy-start.29 = (bf16[512,256]{1,0:T(8,128)(2,1)}, bf16[512,256]{1,0:T(8,128)(2,1)S(1)}, u32[]{:S(2)}) copy-start(bf16[512,256]{1,0:T(8,128)(2,1)S(1)} %collective-permute-done.20.refs_2_) | copy-start | bytes 786436
  (26 other events, 108.5 us)
